TPU v7x, 32 devices: a whole 2x2x4 slice. The times are simulated.
32 devices in a mesh: seq: 4 (over x, core), wide: 8 (over z, y).
Axes of the slice: x: 2, y: 2, z: 4, core: 2. Of those that a mesh axis runs over, the one named last changes fastest.
Arguments:
- images: bfloat16 [8, 1028, 768], P('wide', 'seq'), may hold values from -6 to 6
- cotangent: bfloat16 [8, 1028, 768], P('wide', 'seq'), may hold values from -6 to 6
- key_mask: int32 [8, 1028], P('wide'), may hold values from 0 to 1, as said below
- routes: int32 [8, 1028, 2], P('wide', 'seq'), may hold values from 0 to 3, all different within a row
- fill_order: int32 [8, 1028], P('wide', 'seq'), may hold values from 0 to 256, as said below
- norm_gain1: bfloat16 [768], P('wide'), may hold values from 0.099609375 to 1.8984375
- qkv_weight1: bfloat16 [768, 2304], P('wide'), may hold values from -0.21875 to 0.21875
- proj_weight1: bfloat16 [768, 768], P('wide'), may hold values from -6 to 6
- norm_gain2: bfloat16 [768], P('wide'), may hold values from 0.099609375 to 1.8984375
- fc_in: bfloat16 [768, 3072], P('wide'), may hold values from -0.21875 to 0.21875
- fc_out: bfloat16 [3072, 768], P('wide'), may hold values from -0.109375 to 0.109375
- norm_gain3: bfloat16 [768], P('wide'), may hold values from 0.099609375 to 1.8984375
- qkv_weight2: bfloat16 [768, 2304], P('wide'), may hold values from -0.21875 to 0.21875
- proj_weight2: bfloat16 [768, 768], P('wide'), may hold values from -6 to 6
- norm_gain4: bfloat16 [768], P('wide'), may hold values from 0.099609375 to 1.8984375
- router: bfloat16 [768, 4], P('wide'), may hold values from -0.21875 to 0.21875
- expert_in: bfloat16 [8, 768, 1536], P('wide'), may hold values from -0.21875 to 0.21875
- expert_out: bfloat16 [8, 1536, 768], P('wide'), may hold values from -3.5 to 3.5
Outputs:
- output: float32 [8, 1028, 768], P('wide', 'seq')
- image_grad: float32 [8, 1028, 768], P('wide', 'seq')
- norm_gain1_grad: float32 [768], P('wide')
- qkv_weight1_grad: float32 [768, 2304], P('wide')
- proj_weight1_grad: float32 [768, 768], P('wide')
- norm_gain2_grad: float32 [768], P('wide')
- fc_in_grad: float32 [768, 3072], P('wide')
- fc_out_grad: float32 [3072, 768], P('wide')
- norm_gain3_grad: float32 [768], P('wide')
- qkv_weight2_grad: float32 [768, 2304], P('wide')
- proj_weight2_grad: float32 [768, 768], P('wide')
- norm_gain4_grad: float32 [768], P('wide')
- router_grad: float32 [768, 4], P('wide')
- expert_in_grad: float32 [8, 768, 1536], P('wide')
- expert_out_grad: float32 [8, 1536, 768], P('wide')
Inputs may be any that keep to these rules, and one draw needn't show every extreme that they name: `key_mask`: position 0 of every image is 1. The two routes of a token differ. `fill_order`: in each image, each aligned block of 257 positions holds every number from 0 to 256 once.
All inputs are finite; a program needn't handle non-finite values.
Results may differ from a plain program's by a relative error of at most 0.02.
Values may be sent and summed in bfloat16 or wider, within the bound.
A program may use at most 256 MiB of HBM per device.

v0:
```python
import jax
import jax.numpy as jnp
from jax import lax
from jax.sharding import PartitionSpec as P

HEAD_DIM = 64


def shortened(x):
    return jax.tree.map(lambda a: a.astype(jnp.bfloat16) if a.dtype == jnp.float32 else a, x)


def in_blocks(x, dim, peers):
    shape = x.shape
    blocks = x.reshape(*shape[:dim], peers, shape[dim] // peers, *shape[dim + 1 :])
    return jnp.moveaxis(blocks, dim, 0)


def sent_and_summed(x, axis, dim):
    blocks = in_blocks(x, dim, lax.axis_size(axis))
    arrived = lax.all_to_all(blocks, axis, split_axis=0, concat_axis=0, tiled=True)
    return arrived.astype(jnp.float32).sum(axis=0)


def layer_norm(values, gain):
    centred = values - jnp.mean(values, axis=-1, keepdims=True)
    variance = jnp.mean(centred * centred, axis=-1, keepdims=True)
    return centred * lax.rsqrt(variance + 1e-06) * gain


def gelu_exact(values):
    return jax.nn.gelu(values, approximate=False)


def gather_block(weights):
    return jax.tree.map(
        lambda part, own: part.astype(own.dtype),
        lax.all_gather(shortened(weights), "wide", axis=0, tiled=True),
        weights,
    )


def scatter_grads(grads):
    return jax.tree.map(lambda part: sent_and_summed(part, "wide", 0), shortened(grads))


def gather_rows(first_rows, middle_rows, last_rows):
    return (
        lax.all_gather(first_rows, "seq", axis=0, tiled=True),
        lax.all_gather(middle_rows, "seq", axis=0, tiled=True),
        lax.all_gather(last_rows, "seq", axis=0, tiled=True),
    )


def spread_columns(piece, place, groups):
    pick = (jnp.arange(groups, dtype=jnp.int32) == place).astype(jnp.float32)
    spread = piece[..., None, :] * pick[:, None]
    return spread.reshape(piece.shape[:-1] + (groups * piece.shape[-1],))


def masked_scores(query, keys, valid):
    scores = jnp.einsum(
        "qhd,khd->hqk", query, keys, preferred_element_type=jnp.float32
    ) * query.shape[-1] ** (-0.5)
    return jnp.where(valid[None, None, :], scores, -1e30)


def attend_forward(residual, gain, wqkv, wproj, valid):
    groups = lax.axis_size("seq")
    tokens, width = residual.shape
    per_group = width // groups
    normed_low = layer_norm(residual, gain.astype(jnp.float32)).astype(jnp.bfloat16)
    packed = jnp.dot(normed_low, wqkv, preferred_element_type=jnp.float32).astype(jnp.bfloat16)
    packed = packed.reshape(tokens, 3, groups, per_group)
    heads = lax.all_to_all(packed, "seq", split_axis=2, concat_axis=0, tiled=True)
    length = heads.shape[0]
    heads = heads.reshape(length, 3, per_group // HEAD_DIM, HEAD_DIM)
    scores = masked_scores(heads[:, 0], heads[:, 1], valid)
    peak_score = jnp.max(scores, axis=-1, keepdims=True)
    exp_scores = jnp.exp(scores - peak_score)
    row_total = jnp.sum(exp_scores, axis=-1, keepdims=True)
    probs_low = (exp_scores / row_total).astype(jnp.bfloat16)
    log_total = peak_score + jnp.log(row_total)
    mixed = jnp.einsum(
        "hqk,khd->qhd", probs_low, heads[:, 2], preferred_element_type=jnp.float32
    ).astype(jnp.bfloat16)
    returned = lax.all_to_all(
        mixed.reshape(length, 1, per_group), "seq", split_axis=0, concat_axis=1, tiled=True
    )
    mixed_tok = returned.reshape(tokens, width)
    branch = jnp.dot(mixed_tok, wproj, preferred_element_type=jnp.float32)
    return (residual + branch, (residual, normed_low, heads, log_total, mixed_tok))


def attend_backward(grad_res, saved, gain, wqkv, wproj, valid):
    residual, normed_low, heads, log_total, mixed_tok = saved
    groups = lax.axis_size("seq")
    place = lax.axis_index("seq")
    tokens, width = residual.shape
    per_group = width // groups
    length = heads.shape[0]
    grad_branch = grad_res.astype(jnp.bfloat16)
    normed_all, mixed_all, branch_all = gather_rows(normed_low, mixed_tok, grad_branch)
    branch_cols = lax.dynamic_slice_in_dim(branch_all, place * per_group, per_group, 1)
    grad_proj = jnp.einsum("td,te->de", mixed_all, branch_cols, preferred_element_type=jnp.float32)
    grad_mixed = jnp.einsum(
        "te,de->td", grad_branch, wproj, preferred_element_type=jnp.float32
    ).astype(jnp.bfloat16)
    grad_heads = lax.all_to_all(
        grad_mixed.reshape(tokens, groups, per_group),
        "seq",
        split_axis=1,
        concat_axis=0,
        tiled=True,
    )
    grad_heads = grad_heads.reshape(length, per_group // HEAD_DIM, HEAD_DIM)
    query = heads[:, 0]
    keys = heads[:, 1]
    values = heads[:, 2]
    attn_probs = jnp.exp(masked_scores(query, keys, valid) - log_total)
    grad_probs = jnp.einsum("qhd,khd->hqk", grad_heads, values, preferred_element_type=jnp.float32)
    row_delta = jnp.sum(attn_probs * grad_probs, axis=-1, keepdims=True)
    grad_scores = (attn_probs * (grad_probs - row_delta) * HEAD_DIM ** (-0.5)).astype(jnp.bfloat16)
    grad_query = jnp.einsum("hqk,khd->qhd", grad_scores, keys, preferred_element_type=jnp.float32)
    grad_keys = jnp.einsum("hqk,qhd->khd", grad_scores, query, preferred_element_type=jnp.float32)
    grad_values = jnp.einsum(
        "hqk,qhd->khd",
        attn_probs.astype(jnp.bfloat16),
        grad_heads,
        preferred_element_type=jnp.float32,
    )
    grad_packed = jnp.stack([grad_query, grad_keys, grad_values], axis=1).astype(jnp.bfloat16)
    grad_packed = grad_packed.reshape(length, 3 * per_group)
    grad_qkv = jnp.einsum("td,te->de", normed_all, grad_packed, preferred_element_type=jnp.float32)
    grad_tok = lax.all_to_all(
        grad_packed.reshape(length, 3, 1, per_group), "seq", split_axis=0, concat_axis=2, tiled=True
    )
    grad_tok = grad_tok.reshape(tokens, 3 * width)
    grad_normed = jnp.einsum("te,de->td", grad_tok, wqkv, preferred_element_type=jnp.float32)
    pullback = jax.vjp(layer_norm, residual, gain.astype(jnp.float32))[1]
    grad_input, grad_gain = pullback(grad_normed)
    return (grad_res + grad_input, (grad_gain, grad_qkv.reshape(width, 3, per_group), grad_proj))


def ffn_forward(residual, gain, weight_in, weight_out):
    normed_low = layer_norm(residual, gain.astype(jnp.float32)).astype(jnp.bfloat16)
    pre_act = jnp.dot(normed_low, weight_in, preferred_element_type=jnp.float32)
    hidden = gelu_exact(pre_act).astype(jnp.bfloat16)
    branch = jnp.dot(hidden, weight_out, preferred_element_type=jnp.float32)
    return (residual + branch, (residual, normed_low, pre_act, hidden))


def ffn_backward(grad_res, saved, gain, weight_in, weight_out):
    residual, normed_low, pre_act, hidden = saved
    groups = lax.axis_size("seq")
    place = lax.axis_index("seq")
    tokens, width = residual.shape
    per_group = width // groups
    units = hidden.shape[1]
    grad_branch = grad_res.astype(jnp.bfloat16)
    normed_all, hidden_all, branch_all = gather_rows(normed_low, hidden, grad_branch)
    branch_cols = lax.dynamic_slice_in_dim(branch_all, place * per_group, per_group, 1)
    grad_out = jnp.einsum("tf,td->fd", hidden_all, branch_cols, preferred_element_type=jnp.float32)
    grad_hidden = jnp.einsum(
        "td,fd->tf", grad_branch, weight_out, preferred_element_type=jnp.float32
    )
    grad_pre = jax.vjp(gelu_exact, pre_act)[1](grad_hidden)[0].astype(jnp.bfloat16)
    pre_cols = lax.all_to_all(
        grad_pre.reshape(tokens, groups, units // groups),
        "seq",
        split_axis=1,
        concat_axis=0,
        tiled=True,
    )
    pre_cols = pre_cols.reshape(tokens * groups, units // groups)
    grad_in = jnp.einsum("td,tf->df", normed_all, pre_cols, preferred_element_type=jnp.float32)
    grad_normed = jnp.einsum("tf,df->td", grad_pre, weight_in, preferred_element_type=jnp.float32)
    pullback = jax.vjp(layer_norm, residual, gain.astype(jnp.float32))[1]
    grad_input, grad_gain = pullback(grad_normed)
    return (grad_res + grad_input, (grad_gain, grad_in, grad_out))


def route_slots(routes, fill_order, experts, capacity):
    tokens = routes.shape[0]
    pair_expert = routes.reshape(-1)
    pair_key = (jnp.arange(2, dtype=jnp.int32)[None, :] * tokens + fill_order[:, None]).reshape(-1)
    same_expert = pair_expert[:, None] == pair_expert[None, :]
    earlier = pair_key[None, :] < pair_key[:, None]
    slot_rank = jnp.sum((same_expert & earlier).astype(jnp.int32), axis=1)
    target = jnp.where(slot_rank < capacity, pair_expert * capacity + slot_rank, experts * capacity)
    slot_pair = jnp.full((experts * capacity + 1,), 2 * tokens, jnp.int32)
    slot_pair = slot_pair.at[target].set(jnp.arange(2 * tokens, dtype=jnp.int32))
    return (target, slot_pair[:-1])


def to_slots(pair_rows, slot_pair, experts, capacity):
    width = pair_rows.shape[-1]
    padded = jnp.concatenate([pair_rows, jnp.zeros((1, width), pair_rows.dtype)], axis=0)
    filled = padded[slot_pair].reshape(experts, 1, capacity, width)
    return jnp.broadcast_to(filled, (experts, 2, capacity, width)).reshape(
        2 * experts * capacity, width
    )


def from_slots(returned, target, experts, capacity):
    width = returned.shape[-1]
    halves = returned.astype(jnp.float32).reshape(experts, 2, capacity, width)
    summed = jnp.sum(halves, axis=1).reshape(experts * capacity, width)
    padded = jnp.concatenate([summed, jnp.zeros((1, width), jnp.float32)], axis=0)
    return padded[target].reshape(-1, 2, width)


def expert_forward(residual, gain, w_router, w_in, w_out, routes, fill_order):
    tokens, width = residual.shape
    experts = w_router.shape[1]
    capacity = (5 * tokens + 2 * experts - 1) // (2 * experts)
    normed_low = layer_norm(residual, gain.astype(jnp.float32)).astype(jnp.bfloat16)
    logits = jnp.dot(normed_low, w_router, preferred_element_type=jnp.float32)
    router_probs = jax.nn.softmax(logits, axis=-1)
    chosen = (routes[:, :, None] == jnp.arange(experts, dtype=jnp.int32)[None, None, :]).astype(
        jnp.float32
    )
    gates = jnp.sum(chosen * router_probs[:, None, :], axis=-1)
    target, slot_pair = route_slots(routes, fill_order, experts, capacity)
    send_rows = to_slots(jnp.repeat(normed_low, 2, axis=0), slot_pair, experts, capacity)
    received = lax.all_to_all(send_rows, "wide", split_axis=0, concat_axis=0, tiled=True)
    pre_act = jnp.dot(received, w_in, preferred_element_type=jnp.float32)
    hidden = gelu_exact(pre_act).astype(jnp.bfloat16)
    part_out = jnp.dot(hidden, w_out, preferred_element_type=jnp.float32).astype(jnp.bfloat16)
    returned = lax.all_to_all(part_out, "wide", split_axis=0, concat_axis=0, tiled=True)
    picked = from_slots(returned, target, experts, capacity)
    mixed = jnp.sum(gates[:, :, None] * picked, axis=1)
    saved = (
        residual,
        normed_low,
        router_probs,
        chosen,
        gates,
        target,
        slot_pair,
        received,
        pre_act,
        hidden,
        picked,
    )
    return (residual + mixed, saved)


def expert_backward(grad_res, saved, gain, w_router, w_in, w_out):
    (
        residual,
        normed_low,
        router_probs,
        chosen,
        gates,
        target,
        slot_pair,
        received,
        pre_act,
        hidden,
        picked,
    ) = saved
    tokens, width = residual.shape
    experts = w_router.shape[1]
    capacity = (5 * tokens + 2 * experts - 1) // (2 * experts)
    grad_gates = jnp.sum(grad_res[:, None, :] * picked, axis=-1)
    grad_probs = jnp.sum(chosen * grad_gates[:, :, None], axis=1)
    row_delta = jnp.sum(router_probs * grad_probs, axis=-1, keepdims=True)
    grad_logits = (router_probs * (grad_probs - row_delta)).astype(jnp.bfloat16)
    grad_router = jnp.einsum(
        "td,te->de", normed_low, grad_logits, preferred_element_type=jnp.float32
    )
    grad_normed = jnp.einsum("te,de->td", grad_logits, w_router, preferred_element_type=jnp.float32)
    pair_grads = (
        (gates[:, :, None] * grad_res[:, None, :]).astype(jnp.bfloat16).reshape(2 * tokens, width)
    )
    send_grads = to_slots(pair_grads, slot_pair, experts, capacity)
    grad_part = lax.all_to_all(send_grads, "wide", split_axis=0, concat_axis=0, tiled=True)
    grad_w_out = jnp.einsum("rf,rd->fd", hidden, grad_part, preferred_element_type=jnp.float32)
    grad_hidden = jnp.einsum("rd,fd->rf", grad_part, w_out, preferred_element_type=jnp.float32)
    grad_pre = jax.vjp(gelu_exact, pre_act)[1](grad_hidden)[0].astype(jnp.bfloat16)
    grad_w_in = jnp.einsum("rd,rf->df", received, grad_pre, preferred_element_type=jnp.float32)
    grad_rows = jnp.einsum("rf,df->rd", grad_pre, w_in, preferred_element_type=jnp.float32).astype(
        jnp.bfloat16
    )
    grad_back = lax.all_to_all(grad_rows, "wide", split_axis=0, concat_axis=0, tiled=True)
    grad_normed = grad_normed + jnp.sum(from_slots(grad_back, target, experts, capacity), axis=1)
    pullback = jax.vjp(layer_norm, residual, gain.astype(jnp.float32))[1]
    grad_input, grad_gain = pullback(grad_normed)
    return (grad_res + grad_input, (grad_gain, grad_router), (grad_w_in[None], grad_w_out[None]))


def on_device(
    images,
    cotangent,
    key_mask,
    routes,
    fill_order,
    norm_gain1,
    qkv_weight1,
    proj_weight1,
    norm_gain2,
    fc_in,
    fc_out,
    norm_gain3,
    qkv_weight2,
    proj_weight2,
    norm_gain4,
    router,
    expert_in,
    expert_out,
):
    groups = lax.axis_size("seq")
    place = lax.axis_index("seq")
    valid = key_mask[0] > 0
    start = images[0].astype(jnp.float32)
    gain_one, wqkv_one, wproj_one, gain_two, weight_in, weight_out = gather_block(
        (norm_gain1, qkv_weight1, proj_weight1, norm_gain2, fc_in, fc_out)
    )
    first, saved_one = attend_forward(start, gain_one, wqkv_one, wproj_one, valid)
    second, saved_two = ffn_forward(first, gain_two, weight_in, weight_out)
    gain_three, wqkv_two, wproj_two, gain_four, w_router = gather_block(
        (norm_gain3, qkv_weight2, proj_weight2, norm_gain4, router)
    )
    third, saved_three = attend_forward(second, gain_three, wqkv_two, wproj_two, valid)
    output, saved_four = expert_forward(
        third, gain_four, w_router, expert_in[0], expert_out[0], routes[0], fill_order[0]
    )
    grad_res = cotangent[0].astype(jnp.float32)
    grad_res, router_terms, expert_terms = expert_backward(
        grad_res, saved_four, gain_four, w_router, expert_in[0], expert_out[0]
    )
    grad_res, attn_two = attend_backward(
        grad_res, saved_three, gain_three, wqkv_two, wproj_two, valid
    )
    gain3_part, qkv2_part, proj2_part, gain4_part, router_part = scatter_grads(
        (attn_two[0], attn_two[1], attn_two[2], router_terms[0], router_terms[1])
    )
    grad_res, ffn_terms = ffn_backward(grad_res, saved_two, gain_two, weight_in, weight_out)
    grad_res, attn_one = attend_backward(grad_res, saved_one, gain_one, wqkv_one, wproj_one, valid)
    gain1_part, qkv1_part, proj1_part, gain2_part, fcin_part, fcout_part = scatter_grads(
        (attn_one[0], attn_one[1], attn_one[2], ffn_terms[0], ffn_terms[1], ffn_terms[2])
    )
    qkv1_full = spread_columns(qkv1_part, place, groups).reshape(qkv1_part.shape[0], -1)
    qkv2_full = spread_columns(qkv2_part, place, groups).reshape(qkv2_part.shape[0], -1)
    proj1_full = spread_columns(proj1_part, place, groups)
    proj2_full = spread_columns(proj2_part, place, groups)
    fcin_full = spread_columns(fcin_part, place, groups)
    fcout_full = spread_columns(fcout_part, place, groups)
    summed = (
        lax.psum(gain1_part.astype(jnp.bfloat16), "seq").astype(jnp.float32),
        lax.psum(qkv1_full.astype(jnp.bfloat16), "seq").astype(jnp.float32),
        lax.psum(proj1_full.astype(jnp.bfloat16), "seq").astype(jnp.float32),
        lax.psum(gain2_part.astype(jnp.bfloat16), "seq").astype(jnp.float32),
        lax.psum(fcin_full.astype(jnp.bfloat16), "seq").astype(jnp.float32),
        lax.psum(fcout_full.astype(jnp.bfloat16), "seq").astype(jnp.float32),
        lax.psum(gain3_part.astype(jnp.bfloat16), "seq").astype(jnp.float32),
        lax.psum(qkv2_full.astype(jnp.bfloat16), "seq").astype(jnp.float32),
        lax.psum(proj2_full.astype(jnp.bfloat16), "seq").astype(jnp.float32),
        lax.psum(gain4_part.astype(jnp.bfloat16), "seq").astype(jnp.float32),
        lax.psum(router_part.astype(jnp.bfloat16), "seq").astype(jnp.float32),
        lax.psum(expert_terms[0].astype(jnp.bfloat16), "seq").astype(jnp.float32),
        lax.psum(expert_terms[1].astype(jnp.bfloat16), "seq").astype(jnp.float32),
    )
    return (
        output[None],
        grad_res[None],
        summed[0],
        summed[1],
        summed[2],
        summed[3],
        summed[4],
        summed[5],
        summed[6],
        summed[7],
        summed[8],
        summed[9],
        summed[10],
        summed[11],
        summed[12],
    )


def solution(mesh):
    placed = (
        P("wide", "seq", None),
        P("wide", "seq", None),
        P("wide", None),
        P("wide", "seq", None),
        P("wide", "seq"),
        P("wide"),
        P("wide", None),
        P("wide", None),
        P("wide"),
        P("wide", None),
        P("wide", None),
        P("wide"),
        P("wide", None),
        P("wide", None),
        P("wide"),
        P("wide", None),
        P("wide", None, None),
        P("wide", None, None),
    )
    return jax.shard_map(
        on_device,
        mesh=mesh,
        in_specs=placed,
        out_specs=(
            P("wide", "seq", None),
            P("wide", "seq", None),
            P("wide"),
            P("wide", None),
            P("wide", None),
            P("wide"),
            P("wide", None),
            P("wide", None),
            P("wide"),
            P("wide", None),
            P("wide", None),
            P("wide"),
            P("wide", None),
            P("wide", None, None),
            P("wide", None, None),
        ),
        check_vma=False,
    )
```

profile of v0, /device:TPU:0, one launch (start us, length us, event | category | flops | bytes accessed | tf_op | source)
XLA Modules:
  0.0 1362.9 jit_solution(10859970604001512667)
XLA Ops:
  15.3 24.7 %all-reduce.8 = (bf16[768]{0:T(1024)(128)(2,1)S(1)}, bf16[768]{0:T(1024)(128)(2,1)S(1)}, bf16[768]{0:T(1024)(128)(2,1)S(1)}, bf16[768]{0:T(1024)(128)(2,1)S(1)}) all-reduce(bf16[768]{0:T(1024)(128)(2,1)S(1)} %dynamic-update-slice, bf16[768]{0:T(1024)(128)(2,1)S(1)} %dynamic-update-slice.1, ...), channel_id=1, replica_groups=mesh['seq'=4,'wide'=8] {'wide'}, use_global_device_ids=true, to_apply=%add.4 | all-reduce | flops 3072 | bytes 12288
  43.0 35.1 %all-gather.26.cloned.1.call-done = bf16[768,2304]{1,0:T(8,128)(2,1)} async-done(((bf16[96,2304]{1,0:T(8,128)(2,1)}), bf16[768,2304]{1,0:T(8,128)(2,1)}) %all-gather.26.cloned.1.call-update) | async-done | bytes 3538960 | tf_op jit(solution)/shard_map/all_gather | solution.py:38
  94.7 20.0 %all-to-all-done = bf16[257,3,4,192]{3,0,1,2:T(8,128)(2,1)} async-done(((bf16[257,3,4,192]{3,0,1,2:T(8,128)(2,1)}), bf16[257,3,4,192]{3,0,1,2:T(8,128)(2,1)}, u32[]{:S(2)}, u32[]{:S(2)}) %all-to-all-start) | async-done | bytes 1184288 | tf_op jit(solution)/shard_map/all_to_all | solution.py:75
  114.7 5.1 copy.205
  123.8 9.0 fusion.136
  132.8 7.0 fusion.14
  139.9 7.8 fusion.73
  154.9 7.3 all-to-all-done.1
  165.7 7.4 reduce.15
  181.9 18.5 %all-gather.30.cloned.1.call-done = bf16[768,3072]{1,0:T(8,128)(2,1)} async-done(((bf16[96,3072]{1,0:T(8,128)(2,1)}), bf16[768,3072]{1,0:T(8,128)(2,1)}) %all-gather.30.cloned.1.call-update) | async-done | bytes 4718608 | tf_op jit(solution)/shard_map/all_gather | solution.py:38
  200.4 11.9 multiply_convert_fusion.1
  212.3 67.8 %all-gather.32.cloned.1.call-done = bf16[3072,768]{1,0:T(8,128)(2,1)} async-done(((bf16[384,768]{1,0:T(8,128)(2,1)}), bf16[3072,768]{1,0:T(8,128)(2,1)}) %all-gather.32.cloned.1.call-update) | async-done | bytes 4718608 | tf_op jit(solution)/shard_map/all_gather | solution.py:38
  286.3 58.9 %all-gather.34.cloned.1.call-done = bf16[768,2304]{1,0:T(8,128)(2,1)} async-done(((bf16[96,2304]{1,0:T(8,128)(2,1)}), bf16[768,2304]{1,0:T(8,128)(2,1)}) %all-gather.34.cloned.1.call-update) | async-done | bytes 3538960 | tf_op jit(solution)/shard_map/all_gather | solution.py:38
  367.4 14.6 %all-to-all-done.2 = bf16[257,3,4,192]{3,0,1,2:T(8,128)(2,1)} async-done(((bf16[257,3,4,192]{3,0,1,2:T(8,128)(2,1)}), bf16[257,3,4,192]{3,0,1,2:T(8,128)(2,1)}, u32[]{:S(2)}, u32[]{:S(2)}) %all-to-all-start.2) | async-done | bytes 1184288 | tf_op jit(solution)/shard_map/all_to_all | solution.py:75
  382.0 5.1 copy.211
  391.1 8.8 fusion.139
  400.0 7.0 fusion.15
  407.0 7.8 fusion.72
  421.3 7.3 all-to-all-done.3
  432.1 7.4 reduce.16
  466.7 49.0 %all-gather = bf16[8,96,4]{1,2,0:T(4,128)(2,1)S(1)} all-gather(bf16[1,96,4]{1,2,0:T(4,128)(2,1)S(1)} %bitcast.314), channel_id=1, replica_groups=mesh['seq'=4,'wide'=8] {'wide'}, dimensions={0}, use_global_device_ids=true | all-gather | bytes 6912 | tf_op jit(solution)/shard_map/all_gather | solution.py:38
  530.3 10.4 all-to-all-start.6
  544.2 21.8 %multiply_convert_fusion = (bf16[1288,1536]{1,0:T(8,128)(2,1)S(1)}, f32[1288,1536]{1,0:T(8,128)}, f32[1288,1536]{1,0:T(8,128)}) fusion(bf16[1288,768]{1,0:T(8,128)(2,1)} %all_to_all.178, bf16[1,768,1536]{2,1,0:T(8,128)(2,1)S(1)} %copy-done), kind=kOutput, calls=%fused_computation.36 | convolution fusion | flops 3167367168 | bytes 24121344 | tf_op jit(solution)/shard_map/dot_general | solution.py:227
  575.8 10.0 all-to-all-done.6
  593.6 12.0 add_convert_fusion
  615.6 21.5 %all-to-all-done.5 = bf16[8,161,768]{2,1,0:T(8,128)(2,1)} async-done(((bf16[8,161,768]{2,1,0:T(8,128)(2,1)}), bf16[8,161,768]{2,1,0:T(8,128)(2,1)}, u32[]{:S(2)}, u32[]{:S(2)}) %all-to-all-start.5) | async-done | bytes 1978400 | tf_op jit(solution)/shard_map/all_to_all | solution.py:230
  655.0 5.9 multiply_reduce_fusion.2
  661.0 27.5 %all-to-all-done.7 = bf16[8,161,768]{2,1,0:T(8,128)(2,1)} async-done(((bf16[8,161,768]{2,1,0:T(8,128)(2,1)}), bf16[8,161,768]{2,1,0:T(8,128)(2,1)}, u32[]{:S(2)}, u32[]{:S(2)}) %all-to-all-start.7) | async-done | bytes 1978400 | tf_op jit(solution)/shard_map/all_to_all | solution.py:286
  716.3 8.2 all-to-all-done.8
  727.4 7.3 fusion.98
  734.7 22.4 %fusion.60 = bf16[3,64,1028]{2,1,0:T(8,128)(2,1)S(1)} fusion(f32[3,1028,1028]{1,2,0:T(8,128)} %fusion.98, f32[3,1028,1028]{1,2,0:T(8,128)} %get-tuple-element.148, f32[3,1028]{1,0:T(4,128)S(1)} %log_add_fusion.1, bf16[1028,3,3,64]{0,3,2,1:T(8,128)(2,1)S(1)} %copy-done.15), kind=kOutput, calls=%fused_computation.92 | convolution fusion | flops 428199008 | bytes 57939456 | tf_op jit(solution)/shard_map/hqk,khd->qhd/dot_general | solution.py:124
  759.9 20.6 %fusion.63 = bf16[3,64,1028]{2,1,0:T(8,128)(2,1)} fusion(f32[3,1028,1028]{1,2,0:T(8,128)} %fusion.98, f32[3,1028,1028]{1,2,0:T(8,128)} %get-tuple-element.148, f32[3,1028]{1,0:T(4,128)S(1)} %log_add_fusion.1, bf16[1028,3,3,64]{0,3,2,1:T(8,128)(2,1)S(1)} %copy-done.15), kind=kOutput, calls=%fused_computation.93 | convolution fusion | flops 428199008 | bytes 57939456 | tf_op jit(solution)/shard_map/hqk,qhd->khd/dot_general | solution.py:125
  784.1 8.2 fusion.66
  795.5 6.0 pad_maximum_fusion
  807.9 31.7 %all-to-all-done.9 = bf16[1028,3,1,192]{3,1,2,0:T(4,128)(2,1)S(1)} async-done(((bf16[1028,3,1,192]{3,1,2,0:T(4,128)(2,1)}), bf16[1028,3,1,192]{3,1,2,0:T(4,128)(2,1)S(1)}, u32[]{:S(2)}, u32[]{:S(2)}) %all-to-all-start.9) | async-done | bytes 1184288 | tf_op jit(solution)/shard_map/all_to_all | solution.py:135
  843.9 5.7 copy.231
  860.2 4.8 add_convert_fusion.1
  877.3 14.5 %all-to-all-done.10 = bf16[257,4,192]{2,0,1:T(8,128)(2,1)S(1)} async-done(((bf16[257,4,192]{2,0,1:T(8,128)(2,1)}), bf16[257,4,192]{2,0,1:T(8,128)(2,1)S(1)}, u32[]{:S(2)}, u32[]{:S(2)}) %all-to-all-start.10) | async-done | bytes 394784 | tf_op jit(solution)/shard_map/all_to_all | solution.py:109
  894.5 7.3 fusion.97
  901.8 22.3 %fusion.54 = bf16[3,64,1028]{2,1,0:T(8,128)(2,1)S(1)} fusion(f32[3,1028,1028]{1,2,0:T(8,128)} %fusion.97, f32[3,1028,1028]{1,2,0:T(8,128)} %get-tuple-element.141, f32[3,1028]{1,0:T(4,128)S(1)} %log_add_fusion, bf16[1028,3,3,64]{0,3,2,1:T(8,128)(2,1)S(1)} %copy-done.14), kind=kOutput, calls=%fused_computation.90 | convolution fusion | flops 428199008 | bytes 57939456 | tf_op jit(solution)/shard_map/hqk,khd->qhd/dot_general | solution.py:124
  927.0 20.9 %fusion.57 = bf16[3,64,1028]{2,1,0:T(8,128)(2,1)} fusion(f32[3,1028,1028]{1,2,0:T(8,128)} %fusion.97, f32[3,1028,1028]{1,2,0:T(8,128)} %get-tuple-element.141, f32[3,1028]{1,0:T(4,128)S(1)} %log_add_fusion, bf16[1028,3,3,64]{0,3,2,1:T(8,128)(2,1)S(1)} %copy-done.14), kind=kOutput, calls=%fused_computation.91 | convolution fusion | flops 428199008 | bytes 57939456 | tf_op jit(solution)/shard_map/hqk,qhd->khd/dot_general | solution.py:125
  951.6 8.2 fusion.69
  963.1 6.1 pad_maximum_fusion.1
  980.1 26.7 %all-to-all-done.11 = bf16[1028,3,1,192]{3,1,2,0:T(4,128)(2,1)S(1)} async-done(((bf16[1028,3,1,192]{3,1,2,0:T(4,128)(2,1)}), bf16[1028,3,1,192]{3,1,2,0:T(4,128)(2,1)S(1)}, u32[]{:S(2)}, u32[]{:S(2)}) %all-to-all-start.11) | async-done | bytes 1184288 | tf_op jit(solution)/shard_map/all_to_all | solution.py:135
  1022.6 9.1 all-to-all-done.16
  1031.7 5.5 all-to-all-start.21
  1048.8 5.9 all-to-all-start.14
  1070.0 6.0 all-to-all-start.20
  1082.6 4.7 convolution_convert_fusion.7
  1087.3 16.2 %all-to-all-done.20 = bf16[8,96,3,192]{1,3,2,0:T(8,128)(2,1)} async-done(((bf16[8,96,3,192]{1,3,2,0:T(8,128)(2,1)}), bf16[8,96,3,192]{1,3,2,0:T(8,128)(2,1)}, u32[]{:S(2)}, u32[]{:S(2)}) %all-to-all-start.20) | async-done | bytes 884768 | tf_op jit(solution)/shard_map/all_to_all | solution.py:21
  1108.8 7.2 reshape.682
  1120.3 4.6 copy.241
  1141.6 6.3 all-to-all-start.18
  1147.9 8.2 fusion.53
  1156.2 5.2 fusion.52
  1175.5 5.3 all-to-all-start.13
  1192.6 15.3 %all-to-all-done.13 = bf16[8,96,3,192]{1,3,2,0:T(8,128)(2,1)S(1)} async-done(((bf16[8,96,3,192]{1,3,2,0:T(8,128)(2,1)}), bf16[8,96,3,192]{1,3,2,0:T(8,128)(2,1)S(1)}, u32[]{:S(2)}, u32[]{:S(2)}) %all-to-all-start.13) | async-done | bytes 884768 | tf_op jit(solution)/shard_map/all_to_all | solution.py:21
  1216.1 5.5 all-to-all-done.22
  1225.6 5.8 all-to-all-done.23
  1235.4 5.7 all-to-all-done.15
  1245.1 5.7 all-to-all-done.19
  1260.5 6.5 all-reduce.9
  1269.7 71.6 %all-reduce.13.cloned.1.call-done = (bf16[384,768]{0,1:T(8,128)(2,1)}, bf16[96,2304]{1,0:T(8,128)(2,1)}, bf16[96,768]{1,0:T(8,128)(2,1)}, bf16[96,3072]{1,0:T(8,...) async-done(((bf16[384,768]{0,1:T(8,128)(2,1)}, bf16[96,2304]{1,0:T(8,128)(2,1)}, ...) | async-done | bytes 7077904 | tf_op jit(solution)/shard_map/psum | solution.py:356
  1341.3 4.6 convert_element_type.437
  (539 shorter events, 423.8 us)
Async XLA Ops:
  7.2 537.0 %copy-start = (bf16[1,768,1536]{2,1,0:T(8,128)(2,1)S(1)}, bf16[1,768,1536]{2,1,0:T(8,128)(2,1)}, u32[]{:S(2)}) copy-start(bf16[1,768,1536]{2,1,0:T(8,128)(2,1)} %param.34) | copy-start | bytes 7077892
  7.2 70.9 %all-gather.26.cloned.1.call-start = ((), (), s32[]{:S(2)}) async-start(), calls=%async_computation.24 | async-start | bytes 3981312 | tf_op jit(solution)/shard_map/all_gather | solution.py:38
  7.9 170.7 %all-gather.28.cloned.1.call-start = ((), (), s32[]{:S(2)}) async-start(), calls=%async_computation.25 | async-start | bytes 1327104 | tf_op jit(solution)/shard_map/all_gather | solution.py:38
  8.7 191.7 %all-gather.30.cloned.1.call-start = ((), (), s32[]{:S(2)}) async-start(), calls=%async_computation.26 | async-start | bytes 5308416 | tf_op jit(solution)/shard_map/all_gather | solution.py:38
  9.4 270.7 %all-gather.32.cloned.1.call-start = ((), (), s32[]{:S(2)}) async-start(), calls=%async_computation.27 | async-start | bytes 5308416 | tf_op jit(solution)/shard_map/all_gather | solution.py:38
  40.0 42.5 %copy-start.63 = (f32[768]{0:T(1024)}, f32[768]{0:T(1024)S(1)}, u32[]{:S(2)}) copy-start(f32[768]{0:T(1024)S(1)} %convert_element_type.354) | copy-start | bytes 9220
  41.1 41.3 %copy-start.67 = (f32[257]{0:T(512)}, f32[257]{0:T(512)S(1)}, u32[]{:S(2)}) copy-start(f32[257]{0:T(512)S(1)} %broadcast_multiply_fusion.4) | copy-start | bytes 3088
  43.0 43.8 %copy-start.75 = (f32[257]{0:T(512)}, f32[257]{0:T(512)S(1)}, u32[]{:S(2)}) copy-start(f32[257]{0:T(512)S(1)} %fusion.110) | copy-start | bytes 3088
  89.7 25.0 %all-to-all-start = ((bf16[257,3,4,192]{3,0,1,2:T(8,128)(2,1)}), bf16[257,3,4,192]{3,0,1,2:T(8,128)(2,1)}, u32[]{:S(2)}, u32[]{:S(2)}) async-start(bf16[257,3,4,192]{3,0,1,2:T(8,128)(2,1)} %copy.204), calls=%async_computation | async-start | bytes 3244032 | tf_op jit(solution)/shard_map/all_to_all | solution.py:75
  94.1 251.1 %all-gather.34.cloned.1.call-start = ((), (), s32[]{:S(2)}) async-start(), calls=%async_computation.28 | async-start | bytes 3981312 | tf_op jit(solution)/shard_map/all_gather | solution.py:38
  150.9 11.4 all-to-all-start.1
  154.9 45.5 %copy-start.89 = (f32[768]{0:T(1024)}, f32[768]{0:T(1024)S(1)}, u32[]{:S(2)}) copy-start(f32[768]{0:T(1024)S(1)} %convert_element_type.360) | copy-start | bytes 9220
  154.9 190.2 %copy-start.91 = (f32[768]{0:T(1024)}, f32[768]{0:T(1024)S(1)}, u32[]{:S(2)}) copy-start(f32[768]{0:T(1024)S(1)} %convert_element_type.363) | copy-start | bytes 9220
  180.7 31.5 %copy-start.85 = (f32[257]{0:T(512)}, f32[257]{0:T(512)S(1)}, u32[]{:S(2)}) copy-start(f32[257]{0:T(512)S(1)} %broadcast_multiply_fusion.3) | copy-start | bytes 3088
  181.9 30.4 %copy-start.79 = (f32[257]{0:T(512)}, f32[257]{0:T(512)S(1)}, u32[]{:S(2)}) copy-start(f32[257]{0:T(512)S(1)} %multiply_reduce_fusion.12) | copy-start | bytes 3088
  181.9 30.4 %copy-start.97 = (f32[257]{0:T(512)}, f32[257]{0:T(512)S(1)}, u32[]{:S(2)}) copy-start(f32[257]{0:T(512)S(1)} %fusion.111) | copy-start | bytes 3088
  181.9 98.2 %copy-start.7 = (f32[257,768]{1,0:T(8,128)S(1)}, f32[257,768]{1,0:T(8,128)}, u32[]{:S(2)}) copy-start(f32[257,768]{1,0:T(8,128)} %copy-done.6) | copy-start | bytes 2368516
  284.5 65.1 %copy-start.87 = (f32[257]{0:T(512)}, f32[257]{0:T(512)S(1)}, u32[]{:S(2)}) copy-start(f32[257]{0:T(512)S(1)} %broadcast_multiply_fusion.2) | copy-start | bytes 3088
  286.3 63.4 %copy-start.99 = (f32[257]{0:T(512)}, f32[257]{0:T(512)S(1)}, u32[]{:S(2)}) copy-start(f32[257]{0:T(512)S(1)} %fusion.112) | copy-start | bytes 3088
  357.0 25.0 %all-to-all-start.2 = ((bf16[257,3,4,192]{3,0,1,2:T(8,128)(2,1)}), bf16[257,3,4,192]{3,0,1,2:T(8,128)(2,1)}, u32[]{:S(2)}, u32[]{:S(2)}) async-start(bf16[257,3,4,192]{3,0,1,2:T(8,128)(2,1)} %copy.210), calls=%async_computation.2 | async-start | bytes 3244032 | tf_op jit(solution)/shard_map/all_to_all | solution.py:75
  361.4 87.0 %all-gather.36.cloned.1.call-start = ((), (), s32[]{:S(2)}) async-start(), calls=%async_computation.29 | async-start | bytes 1327104 | tf_op jit(solution)/shard_map/all_gather | solution.py:38
  362.0 88.7 %copy-start.52 = (f32[768]{0:T(1024)}, f32[768]{0:T(1024)S(1)}, u32[]{:S(2)}) copy-start(f32[768]{0:T(1024)S(1)} %convert_element_type.369) | copy-start | bytes 9220
  363.3 27.8 %copy-start.93 = (s32[514]{0:T(1024)}, s32[514]{0:T(1024)S(1)}, u32[]{:S(2)}) copy-start(s32[514]{0:T(1024)S(1)} %fusion.107) | copy-start | bytes 6172
  417.4 11.3 all-to-all-start.3
  421.3 34.5 %copy-start.65 = (s32[1024]{0:T(1024)}, s32[1024]{0:T(1024)S(1)}, u32[]{:S(2)}) copy-start(s32[1024]{0:T(1024)S(1)} %pad_clamp_fusion.1) | copy-start | bytes 12292
  462.2 53.6 %copy-start.26 = (bf16[1,257,768]{2,1,0:T(8,128)(2,1)S(1)}, bf16[1,257,768]{2,1,0:T(8,128)(2,1)}, u32[]{:S(2)}) copy-start(bf16[1,257,768]{2,1,0:T(8,128)(2,1)} %param.19) | copy-start | bytes 1184260
  462.2 66.6 %all-to-all-start.4 = ((bf16[8,161,768]{2,1,0:T(8,128)(2,1)}), bf16[8,161,768]{2,1,0:T(8,128)(2,1)}, u32[]{:S(2)}, u32[]{:S(2)}) async-start(bf16[8,161,768]{2,1,0:T(8,128)(2,1)} %bitcast.282), calls=%async_computation.4 | async-start | bytes 4128768 | tf_op jit(solution)/shard_map/all_to_all | solution.py:226
  530.3 55.5 %all-to-all-start.6 = ((bf16[8,161,768]{2,1,0:T(8,128)(2,1)}), bf16[8,161,768]{2,1,0:T(8,128)(2,1)}, u32[]{:S(2)}, u32[]{:S(2)}) async-start(bf16[8,161,768]{2,1,0:T(8,128)(2,1)} %bitcast.283), calls=%async_computation.6 | async-start | bytes 4128768 | tf_op jit(solution)/shard_map/all_to_all | solution.py:278
  544.2 23.7 %copy-start.106 = (bf16[1,1536,768]{2,1,0:T(8,128)(2,1)S(1)}, bf16[1,1536,768]{2,1,0:T(8,128)(2,1)}, u32[]{:S(2)}) copy-start(bf16[1,1536,768]{2,1,0:T(8,128)(2,1)} %param.35) | copy-start | bytes 7077892
  585.8 51.2 %all-to-all-start.5 = ((bf16[8,161,768]{2,1,0:T(8,128)(2,1)}), bf16[8,161,768]{2,1,0:T(8,128)(2,1)}, u32[]{:S(2)}, u32[]{:S(2)}) async-start(bf16[8,161,768]{2,1,0:T(8,128)(2,1)} %all_to_all.179), calls=%async_computation.5 | async-start | bytes 4128768 | tf_op jit(solution)/shard_map/all_to_all | solution.py:230
  612.0 29.4 %copy-start.94 = (s32[514]{0:T(1024)S(1)}, s32[514]{0:T(1024)}, u32[]{:S(2)}) copy-start(s32[514]{0:T(1024)} %copy-done.93) | copy-start | bytes 6172
  612.0 29.4 %copy-start.20 = (bf16[257,4,1,192]{3,1,0,2:T(4,128)(2,1)S(1)}, bf16[257,4,1,192]{3,1,0,2:T(4,128)(2,1)}, u32[]{:S(2)}) copy-start(bf16[257,4,1,192]{3,1,0,2:T(4,128)(2,1)} %copy.215) | copy-start | bytes 1184260
  637.0 51.5 %all-to-all-start.7 = ((bf16[8,161,768]{2,1,0:T(8,128)(2,1)}), bf16[8,161,768]{2,1,0:T(8,128)(2,1)}, u32[]{:S(2)}, u32[]{:S(2)}) async-start(bf16[8,161,768]{2,1,0:T(8,128)(2,1)} %all_to_all.184), calls=%async_computation.7 | async-start | bytes 4128768 | tf_op jit(solution)/shard_map/all_to_all | solution.py:286
  641.4 369.7 %all-gather.52.cloned.1.call-start = ((), (), s32[]{:S(2)}) async-start(), calls=%async_computation.37 | async-start | bytes 2027520 | tf_op jit(solution)/shard_map/all_gather | solution.py:50
  712.1 12.4 all-to-all-start.8
  715.6 298.6 %all-gather.54.cloned.1.call-start = ((), (), s32[]{:S(2)}) async-start(), calls=%async_computation.38 | async-start | bytes 2027520 | tf_op jit(solution)/shard_map/all_gather | solution.py:51
  801.5 38.0 %all-to-all-start.9 = ((bf16[1028,3,1,192]{3,1,2,0:T(4,128)(2,1)}), bf16[1028,3,1,192]{3,1,2,0:T(4,128)(2,1)S(1)}, u32[]{:S(2)}, u32[]{:S(2)}) async-start(bf16[1028,3,1,192]{3,1,2,0:T(4,128)(2,1)} %pad_maximum_fusion), calls=%async_computation.9 | async-start | bytes 4210688 | tf_op jit(solution)/shard_map/all_to_all | solution.py:135
  805.2 232.1 %all-gather.40.cloned.1.call-start = ((), (), s32[]{:S(2)}) async-start(), calls=%async_computation.31 | async-start | bytes 2027520 | tf_op jit(solution)/shard_map/all_gather | solution.py:50
  807.8 232.5 %all-gather.42.cloned.1.call-start = ((), (), s32[]{:S(2)}) async-start(), calls=%async_computation.32 | async-start | bytes 2027520 | tf_op jit(solution)/shard_map/all_gather | solution.py:51
  869.4 187.9 %all-gather.50.cloned.1.call-start = ((), (), s32[]{:S(2)}) async-start(), calls=%async_computation.36 | async-start | bytes 2027520 | tf_op jit(solution)/shard_map/all_gather | solution.py:49
  870.1 209.4 %all-gather.44.cloned.1.call-start = ((), (), s32[]{:S(2)}) async-start(), calls=%async_computation.33 | async-start | bytes 2027520 | tf_op jit(solution)/shard_map/all_gather | solution.py:49
  870.7 238.1 %all-gather.46.cloned.1.call-start = ((), (), s32[]{:S(2)}) async-start(), calls=%async_computation.34 | async-start | bytes 8110080 | tf_op jit(solution)/shard_map/all_gather | solution.py:50
  873.4 18.5 %all-to-all-start.10 = ((bf16[257,4,192]{2,0,1:T(8,128)(2,1)}), bf16[257,4,192]{2,0,1:T(8,128)(2,1)S(1)}, u32[]{:S(2)}, u32[]{:S(2)}) async-start(bf16[257,4,192]{2,0,1:T(8,128)(2,1)} %copy.232), calls=%async_computation.10 | async-start | bytes 1081344 | tf_op jit(solution)/shard_map/all_to_all | solution.py:109
  924.2 23.8 %copy-start.38 = (bf16[3,64,1028]{2,1,0:T(8,128)(2,1)}, bf16[3,64,1028]{2,1,0:T(8,128)(2,1)S(1)}, u32[]{:S(2)}) copy-start(bf16[3,64,1028]{2,1,0:T(8,128)(2,1)S(1)} %fusion.54) | copy-start | bytes 1184260
  969.2 37.5 %all-to-all-start.11 = ((bf16[1028,3,1,192]{3,1,2,0:T(4,128)(2,1)}), bf16[1028,3,1,192]{3,1,2,0:T(4,128)(2,1)S(1)}, u32[]{:S(2)}, u32[]{:S(2)}) async-start(bf16[1028,3,1,192]{3,1,2,0:T(4,128)(2,1)} %pad_maximum_fusion.1), calls=%async_computation.11 | async-start | bytes 4210688 | tf_op jit(solution)/shard_map/all_to_all | solution.py:135
  1006.7 25.0 %all-to-all-start.16 = ((bf16[257,4,768]{2,0,1:T(8,128)(2,1)}), bf16[257,4,768]{2,0,1:T(8,128)(2,1)}, u32[]{:S(2)}, u32[]{:S(2)}) async-start(bf16[257,4,768]{2,0,1:T(8,128)(2,1)} %copy.251), calls=%async_computation.16 | async-start | bytes 3244032 | tf_op jit(solution)/shard_map/all_to_all | solution.py:168
  1031.7 17.0 %all-to-all-start.21 = ((bf16[8,96,192]{1,2,0:T(8,128)(2,1)}), bf16[8,96,192]{1,2,0:T(8,128)(2,1)}, u32[]{:S(2)}, u32[]{:S(2)}) async-start(bf16[8,96,192]{1,2,0:T(8,128)(2,1)} %copy.258), calls=%async_computation.21 | async-start | bytes 786432 | tf_op jit(solution)/shard_map/all_to_all | solution.py:21
  1048.8 21.2 %all-to-all-start.14 = ((bf16[8,96,192]{1,2,0:T(8,128)(2,1)}), bf16[8,96,192]{1,2,0:T(8,128)(2,1)}, u32[]{:S(2)}, u32[]{:S(2)}) async-start(bf16[8,96,192]{1,2,0:T(8,128)(2,1)} %copy.247), calls=%async_computation.14 | async-start | bytes 786432 | tf_op jit(solution)/shard_map/all_to_all | solution.py:21
  1070.0 33.5 %all-to-all-start.20 = ((bf16[8,96,3,192]{1,3,2,0:T(8,128)(2,1)}), bf16[8,96,3,192]{1,3,2,0:T(8,128)(2,1)}, u32[]{:S(2)}, u32[]{:S(2)}) async-start(bf16[8,96,3,192]{1,3,2,0:T(8,128)(2,1)} %copy.254), calls=%async_computation.20 | async-start | bytes 2359296 | tf_op jit(solution)/shard_map/all_to_all | solution.py:21
  1076.0 57.9 %all-gather.48.cloned.1.call-start = ((), (), s32[]{:S(2)}) async-start(), calls=%async_computation.35 | async-start | bytes 2027520 | tf_op jit(solution)/shard_map/all_gather | solution.py:51
  1103.5 38.1 %all-to-all-start.17 = ((bf16[8,96,768]{2,1,0:T(8,128)(2,1)}), bf16[8,96,768]{2,1,0:T(8,128)(2,1)}, u32[]{:S(2)}, u32[]{:S(2)}) async-start(bf16[8,96,768]{2,1,0:T(8,128)(2,1)} %bitcast.308), calls=%async_computation.17 | async-start | bytes 2359296 | tf_op jit(solution)/shard_map/all_to_all | solution.py:21
  1107.8 56.4 %all-gather.38.cloned.1.call-start = ((), (), s32[]{:S(2)}) async-start(), calls=%async_computation.30 | async-start | bytes 2027520 | tf_op jit(solution)/shard_map/all_gather | solution.py:49
  1141.6 33.9 %all-to-all-start.18 = ((bf16[8,384,192]{1,2,0:T(8,128)(2,1)}), bf16[8,384,192]{1,2,0:T(8,128)(2,1)S(1)}, u32[]{:S(2)}, u32[]{:S(2)}) async-start(bf16[8,384,192]{1,2,0:T(8,128)(2,1)} %bitcast.279), calls=%async_computation.18 | async-start | bytes 2359296 | tf_op jit(solution)/shard_map/all_to_all | solution.py:21
  1175.5 32.5 %all-to-all-start.13 = ((bf16[8,96,3,192]{1,3,2,0:T(8,128)(2,1)}), bf16[8,96,3,192]{1,3,2,0:T(8,128)(2,1)S(1)}, u32[]{:S(2)}, u32[]{:S(2)}) async-start(bf16[8,96,3,192]{1,3,2,0:T(8,128)(2,1)} %copy.243), calls=%async_computation.13 | async-start | bytes 2359296 | tf_op jit(solution)/shard_map/all_to_all | solution.py:21
  1180.8 160.4 %all-reduce.13.cloned.1.call-start = ((), (), s32[]{:S(2)}) async-start(), calls=%async_computation.39 | async-start | bytes 14155776 | tf_op jit(solution)/shard_map/psum | solution.py:356
  1210.4 24.3 %copy-start.102 = (bf16[768]{0:T(1024)(128)(2,1)S(1)}, bf16[768]{0:T(1024)(128)(2,1)}, u32[]{:S(2)}) copy-start(bf16[768]{0:T(1024)(128)(2,1)} %get-tuple-element.92) | copy-start | bytes 4612
  1210.4 34.0 %copy-start.95 = (bf16[768]{0:T(1024)(128)(2,1)S(1)}, bf16[768]{0:T(1024)(128)(2,1)}, u32[]{:S(2)}) copy-start(bf16[768]{0:T(1024)(128)(2,1)} %get-tuple-element.98) | copy-start | bytes 4612
  1210.4 43.6 %copy-start.31 = (f32[1,257,768]{2,1,0:T(8,128)S(1)}, f32[1,257,768]{2,1,0:T(8,128)}, u32[]{:S(2)}) copy-start(f32[1,257,768]{2,1,0:T(8,128)} %get-tuple-element.133) | copy-start | bytes 2368516
  1210.4 45.4 %copy-start.32 = (f32[1,257,768]{2,1,0:T(8,128)S(1)}, f32[1,257,768]{2,1,0:T(8,128)}, u32[]{:S(2)}) copy-start(f32[1,257,768]{2,1,0:T(8,128)} %get-tuple-element.135) | copy-start | bytes 2368516
  1211.8 9.8 all-to-all-start.22
  1221.6 9.8 all-to-all-start.23
  1231.4 9.7 all-to-all-start.15
  1241.1 9.7 all-to-all-start.19
  1250.7 9.7 all-to-all-start.12
  (90 other events, 549.9 us)
Sparse Core Ops, SparseCore 0:
  10.2 67.8 all-gather.25
  80.3 39.8 all-gather.27
  122.3 78.0 all-gather.29
  202.4 77.6 all-gather.31
  282.2 62.9 all-gather.33
  364.1 40.1 all-gather.35
  643.8 20.4 all-gather.51
  717.9 19.4 all-gather.53
  807.9 28.1 all-gather.39
  869.5 23.6 all-gather.41
  895.4 20.0 all-gather.49
  916.9 19.9 all-gather.43
  938.4 55.5 all-gather.45
  1078.1 20.3 all-gather.47
  1134.0 20.3 all-gather.37
  1210.6 130.6 all-reduce.12
where the time goes:
time: 1370 us; the launch traced here: 1360 us
  waiting for transfers between devices  514 us (38%)
  matrix products  277 us (20%)
  local copies, waits for them, and re-layouts  264 us (19%)
  starting transfers between devices  111 us (8%)
  other arithmetic  101 us (7%)
  blocking collectives  80.2 us (6%)
  between operations  16.6 us (1%)
    all_gather x6, waiting for transfers between devices, gather_block(): lax.all_gather(shortened(weights), 'wide', axis=0, tiled=True)  180 us
    psum x1, waiting for transfers between devices, on_device(): lax.psum(fcout_full.astype(jnp.bfloat16), 'seq').astype(jnp.float32)  71.6 us
    unnamed x260, local copies, waits for them, and re-layouts  66.3 us
    all_to_all x2, waiting for transfers between devices, attend_backward(): lax.all_to_all(grad_packed.reshape(length, 3, 1, per_group), 'seq', split...  58.4 us
    all_to_all x11, waiting for transfers between devices, sent_and_summed(): lax.all_to_all(blocks, axis, split_axis=0, concat_axis=0, tiled=True)  57.8 us
    all_to_all x11, starting transfers between devices, sent_and_summed(): lax.all_to_all(blocks, axis, split_axis=0, concat_axis=0, tiled=True)  50 us
    all_gather x1, blocking collectives, gather_block(): lax.all_gather(shortened(weights), 'wide', axis=0, tiled=True)  49 us
    dot_general x2, matrix products, attend_backward(): jnp.einsum('hqk,khd->qhd', grad_scores, keys, preferred_element_type=jnp....  44.8 us
  transfers between devices with their start and end apart: 40, of which 26 were waited for; matrix products, arithmetic and copies ran while one was open for 42% of the time, Pallas kernels for 0%

commit v1 on v0

v1 whole, which is shorter than its diff:
```python
import functools

import jax
import jax.numpy as jnp
from jax import lax
from jax.experimental import pallas as pl
from jax.experimental.pallas import tpu as pltpu
from jax.sharding import PartitionSpec as P

HEAD_DIM = 64
LANES = 128
ROW_TILE = 16
F32 = jnp.float32
BF16 = jnp.bfloat16
VMEM = pl.BlockSpec(memory_space=pltpu.VMEM)
NT = (((1,), (1,)), ((), ()))


def round_up(n, m):
    return -(-n // m) * m


def seq_places():
    me = lax.axis_index("seq")
    near = me + 1 - 2 * lax.rem(me, 2)
    across = lax.rem(me + 2, 4)
    far = lax.rem(near + 2, 4)
    return me, near, across, far


def cuts_of(rows, parts):
    tiles = rows // ROW_TILE
    edges = [(tiles * i // parts) * ROW_TILE for i in range(parts + 1)]
    return [(a, b - a) for a, b in zip(edges[:-1], edges[1:])]


def remote(src, dst, sems, n, axis, place):
    return pltpu.make_async_remote_copy(
        src_ref=src,
        dst_ref=dst,
        send_sem=sems.at[0, n],
        recv_sem=sems.at[1, n],
        device_id={axis: place},
        device_id_type=pl.DeviceIdType.MESH,
    )


def greet(seq_peers, wide_peers=()):
    barrier = pltpu.get_barrier_semaphore()
    for place in seq_peers:
        pl.semaphore_signal(
            barrier, inc=1, device_id={"seq": place}, device_id_type=pl.DeviceIdType.MESH
        )
    for place in wide_peers:
        pl.semaphore_signal(
            barrier, inc=1, device_id={"wide": place}, device_id_type=pl.DeviceIdType.MESH
        )
    pl.semaphore_wait(barrier, len(seq_peers) + len(wide_peers))


class RowScatter:
    def __init__(self, partial, got, sent, crossed, sems, cuts):
        self.partial, self.got, self.sent, self.crossed = partial, got, sent, crossed
        me, near, across, far = seq_places()
        self.me, self.across = me, across
        self.cuts = cuts
        self.far_part, self.near_part, self.cross = [], [], []
        for i, (at, size) in enumerate(cuts):
            rows = pl.ds(at, size)
            self.far_part.append(
                remote(partial.at[far, rows], got.at[1, rows], sems, 3 * i, "seq", near)
            )
            self.near_part.append(
                remote(partial.at[near, rows], got.at[0, rows], sems, 3 * i + 1, "seq", near)
            )
            self.cross.append(
                remote(sent.at[rows], crossed.at[rows], sems, 3 * i + 2, "seq", across)
            )

    def start(self):
        for copy in self.far_part:
            copy.start()
        for copy in self.near_part:
            copy.start()
        for i, (at, size) in enumerate(self.cuts):
            rows = pl.ds(at, size)
            self.far_part[i].wait_recv()
            self.sent[rows, :] = (
                self.partial[self.across, rows].astype(F32) + self.got[1, rows].astype(F32)
            ).astype(BF16)
            self.cross[i].start()

    def total(self, i):
        at, size = self.cuts[i]
        rows = pl.ds(at, size)
        self.near_part[i].wait_recv()
        chip = self.partial[self.me, rows].astype(F32) + self.got[0, rows].astype(F32)
        self.cross[i].wait_recv()
        return chip + self.crossed[rows, :].astype(F32)

    def finish(self):
        for copy in self.far_part + self.near_part + self.cross:
            copy.wait_send()


class RowGather:
    def __init__(self, whole, sems, cuts):
        self.whole = whole
        me, near, across, far = seq_places()
        self.me = me
        self.cuts = cuts
        self.near_copy, self.cross, self.onward = [], [], []
        for i, (at, size) in enumerate(cuts):
            mine = whole.at[me, pl.ds(at, size)]
            theirs = whole.at[across, pl.ds(at, size)]
            self.near_copy.append(remote(mine, mine, sems, 3 * i, "seq", near))
            self.cross.append(remote(mine, mine, sems, 3 * i + 1, "seq", across))
            self.onward.append(remote(theirs, theirs, sems, 3 * i + 2, "seq", near))

    def send(self, i, rows):
        at, size = self.cuts[i]
        self.whole[self.me, pl.ds(at, size)] = rows
        self.cross[i].start()
        self.near_copy[i].start()

    def finish(self):
        for i in range(len(self.cuts)):
            self.cross[i].wait_recv()
            self.onward[i].start()
        for copy in self.near_copy + self.onward:
            copy.wait_recv()
        for copy in self.near_copy + self.cross + self.onward:
            copy.wait_send()


def real_rows(at, size, tokens):
    return at + lax.broadcasted_iota(jnp.int32, (size, 1), 0) < tokens


def centre(values):
    centred = values - jnp.mean(values, axis=-1, keepdims=True)
    variance = jnp.mean(centred * centred, axis=-1, keepdims=True)
    scale = lax.rsqrt(variance + 1e-06)
    return centred * scale, scale


def norm_forward(values, gain):
    return centre(values)[0] * gain


def norm_backward(values, gain, grad):
    unit, scale = centre(values)
    grad_unit = grad * gain
    grad_in = scale * (
        grad_unit
        - jnp.mean(grad_unit, axis=-1, keepdims=True)
        - unit * jnp.mean(grad_unit * unit, axis=-1, keepdims=True)
    )
    return grad_in, jnp.sum(grad * unit, axis=0, keepdims=True)


def sems(n):
    return pltpu.SemaphoreType.DMA((2, n))


def scatter_scratch(rows, width, parts):
    return [
        pltpu.VMEM((2, rows, width), BF16),
        pltpu.VMEM((rows, width), BF16),
        pltpu.VMEM((rows, width), BF16),
        sems(3 * parts),
    ]


def comm_params(collective_id):
    return pltpu.CompilerParams(collective_id=collective_id, has_side_effects=True)


PARTS = 2


def spread_norm(residual, gain, tokens, collective_id):
    rows, width = residual.shape
    cuts = cuts_of(rows, PARTS)

    def kernel(residual_ref, gain_ref, whole_ref, gather_sems):
        _, near, across, _ = seq_places()
        gather = RowGather(whole_ref, gather_sems, cuts)
        greet((near, across))
        for i, (at, size) in enumerate(cuts):
            normed = norm_forward(residual_ref[pl.ds(at, size), :], gain_ref[...])
            normed = jnp.where(real_rows(at, size, tokens), normed, 0.0)
            gather.send(i, normed.astype(BF16))
        gather.finish()

    return pl.pallas_call(
        kernel,
        out_shape=jax.ShapeDtypeStruct((4, rows, width), BF16),
        in_specs=[VMEM] * 2,
        out_specs=VMEM,
        scratch_shapes=[sems(3 * PARTS)],
        compiler_params=comm_params(collective_id),
    )(residual, gain)


def join_forward(partial, residual, gain, tokens, collective_id):
    rows, width = residual.shape
    cuts = cuts_of(rows, PARTS)

    def kernel(
        partial_ref, residual_ref, gain_ref, out_ref, whole_ref, got, sent, crossed, s_sems, g_sems
    ):
        _, near, across, _ = seq_places()
        scatter = RowScatter(partial_ref, got, sent, crossed, s_sems, cuts)
        gather = RowGather(whole_ref, g_sems, cuts)
        greet((near, across))
        scatter.start()
        for i, (at, size) in enumerate(cuts):
            total = residual_ref[pl.ds(at, size), :] + scatter.total(i)
            out_ref[pl.ds(at, size), :] = total
            normed = norm_forward(total, gain_ref[...])
            normed = jnp.where(real_rows(at, size, tokens), normed, 0.0)
            gather.send(i, normed.astype(BF16))
        gather.finish()
        scatter.finish()

    return pl.pallas_call(
        kernel,
        out_shape=(
            jax.ShapeDtypeStruct((rows, width), F32),
            jax.ShapeDtypeStruct((4, rows, width), BF16),
        ),
        in_specs=[VMEM] * 3,
        out_specs=(VMEM, VMEM),
        scratch_shapes=scatter_scratch(rows, width, PARTS) + [sems(3 * PARTS)],
        compiler_params=comm_params(collective_id),
    )(partial, residual, gain)


def join_backward(partial, residual, gain, grad, tokens, collective_id, last):
    rows, width = residual.shape
    cuts = cuts_of(rows, PARTS)

    def kernel(partial_ref, residual_ref, gain_ref, grad_ref, out_ref, gain_grad_ref, *rest):
        if last:
            got, sent, crossed, s_sems = rest
        else:
            whole_ref, got, sent, crossed, s_sems, g_sems = rest
            gather = RowGather(whole_ref, g_sems, cuts)
        _, near, across, _ = seq_places()
        scatter = RowScatter(partial_ref, got, sent, crossed, s_sems, cuts)
        greet((near, across))
        scatter.start()
        gain_grad = jnp.zeros((1, width), F32)
        for i, (at, size) in enumerate(cuts):
            rows_here = pl.ds(at, size)
            grad_in, term = norm_backward(
                residual_ref[rows_here, :], gain_ref[...], scatter.total(i)
            )
            gain_grad = gain_grad + term
            grad_out = grad_ref[rows_here, :] + grad_in
            if last:
                keep = min(size, tokens - at)
                out_ref[pl.ds(at, keep), :] = grad_out[:keep]
            else:
                out_ref[rows_here, :] = grad_out
                gather.send(i, grad_out.astype(BF16))
        gain_grad_ref[...] = gain_grad
        if not last:
            gather.finish()
        scatter.finish()

    out_shape = [
        jax.ShapeDtypeStruct((tokens if last else rows, width), F32),
        jax.ShapeDtypeStruct((1, width), F32),
    ]
    scratch = scatter_scratch(rows, width, PARTS)
    if not last:
        out_shape.append(jax.ShapeDtypeStruct((4, rows, width), BF16))
        scratch.append(sems(3 * PARTS))
    return pl.pallas_call(
        kernel,
        out_shape=tuple(out_shape),
        in_specs=[VMEM] * 4,
        out_specs=(VMEM,) * len(out_shape),
        scratch_shapes=scratch,
        compiler_params=comm_params(collective_id),
    )(partial, residual, gain, grad)


def head_lanes(rows, head):
    lane = lax.broadcasted_iota(jnp.int32, (rows, LANES), 1)
    low = (head % 2) * HEAD_DIM
    return (lane >= low) & (lane < low + HEAD_DIM)


def attend_forward(normed_all, wqkv, wproj, bias_row, heads):
    blocks, rows, width = normed_all.shape
    group = wproj.shape[0]
    total = blocks * rows

    def kernel(normed_ref, wqkv_ref, wproj_ref, bias_ref, qkv_ref, lse_ref, mixed_ref, part_ref):
        step = pl.program_id(0)

        @pl.when(step == 0)
        def _():
            @pl.loop(0, blocks)
            def _(b):
                qkv_ref[b] = jnp.dot(
                    normed_ref[b], wqkv_ref[...], preferred_element_type=F32
                ).astype(BF16)

        lane = lax.broadcasted_iota(jnp.int32, (rows, LANES), 1)
        lse = jnp.zeros((rows, LANES), F32)
        for pair in range(group // LANES):
            lo = pair * LANES
            query = qkv_ref[step, :, lo : lo + LANES].astype(F32) * HEAD_DIM ** (-0.5)
            keys = qkv_ref[:, :, group + lo : group + lo + LANES].reshape(total, LANES)
            values = qkv_ref[:, :, 2 * group + lo : 2 * group + lo + LANES].reshape(total, LANES)
            mixed = jnp.zeros((rows, LANES), F32)
            for head in range(2 * pair, min(2 * pair + 2, heads)):
                mine = head_lanes(rows, head)
                scores = lax.dot_general(
                    jnp.where(mine, query, 0.0).astype(BF16), keys, NT, preferred_element_type=F32
                )
                scores = scores + bias_ref[...]
                peak = jnp.max(scores, axis=-1, keepdims=True)
                exps = jnp.exp(scores - peak)
                row_total = jnp.sum(exps, axis=-1, keepdims=True)
                out = jnp.dot(exps.astype(BF16), values, preferred_element_type=F32)
                mixed = jnp.where(mine, out / row_total, mixed)
                lse = jnp.where(lane == head, peak + jnp.log(row_total), lse)
            mixed_ref[step, :, lo : lo + LANES] = mixed.astype(BF16)
        lse_ref[step] = lse
        part_ref[step] = jnp.dot(
            mixed_ref[step], wproj_ref[...], preferred_element_type=F32
        ).astype(BF16)

    def whole(*shape):
        return pl.BlockSpec(shape, lambda i: (0,) * len(shape))

    return pl.pallas_call(
        kernel,
        grid=(blocks,),
        out_shape=(
            jax.ShapeDtypeStruct((blocks, rows, 3 * group), BF16),
            jax.ShapeDtypeStruct((blocks, rows, LANES), F32),
            jax.ShapeDtypeStruct((blocks, rows, group), BF16),
            jax.ShapeDtypeStruct((blocks, rows, width), BF16),
        ),
        in_specs=[
            whole(blocks, rows, width),
            whole(width, 3 * group),
            whole(group, width),
            whole(1, total),
        ],
        out_specs=(
            whole(blocks, rows, 3 * group),
            whole(blocks, rows, LANES),
            whole(blocks, rows, group),
            whole(blocks, rows, width),
        ),
        compiler_params=pltpu.CompilerParams(dimension_semantics=("arbitrary",)),
    )(normed_all, wqkv, wproj, bias_row)


def attend_backward(branch_all, qkv, lse, mixed, wqkv, wproj, bias_col, heads):
    blocks, rows, width = branch_all.shape
    group = wproj.shape[0]
    pairs = group // LANES
    total = blocks * rows

    def kernel(
        branch_ref,
        qkv_ref,
        lse_ref,
        mixed_ref,
        wqkv_ref,
        wproj_ref,
        bias_ref,
        grad_ref,
        part_ref,
        gm_ref,
        query_ref,
        grads_ref,
        stats_ref,
        dq_ref,
    ):
        step = pl.program_id(0)

        @pl.when(step == 0)
        def _():
            @pl.loop(0, blocks)
            def _(b):
                gm_ref[b] = lax.dot_general(
                    branch_ref[b], wproj_ref[...], NT, preferred_element_type=F32
                ).astype(BF16)

            lse_rows = lse_ref[...].reshape(total, LANES).T
            for head in range(heads):
                lo = (head // 2) * LANES
                mine = head_lanes(total, head)
                query = qkv_ref[:, :, lo : lo + LANES].reshape(total, LANES).astype(F32)
                query_ref[head] = jnp.where(mine, query * HEAD_DIM ** (-0.5), 0.0).astype(BF16)
                grads = gm_ref[:, :, lo : lo + LANES].reshape(total, LANES).astype(F32)
                grads = jnp.where(mine, grads, 0.0)
                grads_ref[head] = grads.astype(BF16)
                out = mixed_ref[:, :, lo : lo + LANES].reshape(total, LANES).astype(F32)
                stats_ref[head] = jnp.concatenate(
                    [
                        lse_rows[head : head + 1],
                        jnp.sum((grads * out).T, axis=0, keepdims=True),
                        jnp.zeros((6, total), F32),
                    ],
                    axis=0,
                )
            dq_ref[...] = jnp.zeros_like(dq_ref)

        for pair in range(pairs):
            lo = pair * LANES
            keys = qkv_ref[step, :, group + lo : group + lo + LANES]
            values = qkv_ref[step, :, 2 * group + lo : 2 * group + lo + LANES]
            grad_keys = jnp.zeros((rows, LANES), F32)
            grad_values = jnp.zeros((rows, LANES), F32)
            for head in range(2 * pair, min(2 * pair + 2, heads)):
                scores = lax.dot_general(keys, query_ref[head], NT, preferred_element_type=F32)
                probs = jnp.exp(scores + bias_ref[step] - stats_ref[head, 0:1])
                grad_probs = lax.dot_general(
                    values, grads_ref[head], NT, preferred_element_type=F32
                )
                grad_scores = (probs * (grad_probs - stats_ref[head, 1:2])).astype(BF16)
                grad_values += jnp.dot(
                    probs.astype(BF16), grads_ref[head], preferred_element_type=F32
                )
                grad_keys += jnp.dot(grad_scores, query_ref[head], preferred_element_type=F32)
                mine = head_lanes(rows, head)
                own_keys = jnp.where(mine, keys.astype(F32), 0.0).T.astype(BF16)
                dq_ref[pl.ds(lo, LANES), :] += jnp.dot(
                    own_keys, grad_scores, preferred_element_type=F32
                )
            grad_ref[step, :, group + lo : group + lo + LANES] = grad_keys.astype(BF16)
            grad_ref[step, :, 2 * group + lo : 2 * group + lo + LANES] = grad_values.astype(BF16)

        @pl.when(step == blocks - 1)
        def _():
            for pair in range(pairs):
                lo = pair * LANES
                grad_query = dq_ref[pl.ds(lo, LANES), :].T * HEAD_DIM ** (-0.5)
                grad_ref[:, :, lo : lo + LANES] = grad_query.astype(BF16).reshape(
                    blocks, rows, LANES
                )

            @pl.loop(0, blocks)
            def _(b):
                part_ref[b] = lax.dot_general(
                    grad_ref[b], wqkv_ref[...], NT, preferred_element_type=F32
                ).astype(BF16)

    def whole(*shape):
        return pl.BlockSpec(shape, lambda i: (0,) * len(shape))

    return pl.pallas_call(
        kernel,
        grid=(blocks,),
        out_shape=(
            jax.ShapeDtypeStruct((blocks, rows, 3 * group), BF16),
            jax.ShapeDtypeStruct((blocks, rows, width), BF16),
        ),
        in_specs=[
            whole(blocks, rows, width),
            whole(blocks, rows, 3 * group),
            whole(blocks, rows, LANES),
            whole(blocks, rows, group),
            whole(width, 3 * group),
            whole(group, width),
            whole(blocks, rows, 1),
        ],
        out_specs=(whole(blocks, rows, 3 * group), whole(blocks, rows, width)),
        scratch_shapes=[
            pltpu.VMEM((blocks, rows, group), BF16),
            pltpu.VMEM((heads, total, LANES), BF16),
            pltpu.VMEM((heads, total, LANES), BF16),
            pltpu.VMEM((heads, 8, total), F32),
            pltpu.VMEM((group, total), F32),
        ],
        compiler_params=pltpu.CompilerParams(dimension_semantics=("arbitrary",)),
    )(branch_all, qkv, lse, mixed, wqkv, wproj, bias_col)


def wide_places():
    me = lax.axis_index("wide")
    half = lax.rem(me, 2)
    return me, half, me // 2, me + 1 - 2 * half


def dispatch(partial, residual, gain, router, routes, cotangent, target, tokens, slots, cid):
    rows, width = residual.shape
    wide = lax.axis_size("wide")
    experts = wide // 2
    cuts = cuts_of(rows, PARTS)

    def kernel(
        partial_ref,
        residual_ref,
        gain_ref,
        router_ref,
        routes_ref,
        cot_ref,
        target_ref,
        third_ref,
        routed_ref,
        probs_ref,
        gates_ref,
        rows_ref,
        grads_ref,
        got,
        sent,
        crossed,
        s_sems,
        send_rows,
        send_grads,
        gated_ref,
        e_sems,
        p_sems,
    ):
        _, near, across, _ = seq_places()
        me, half, expert, partner = wide_places()
        scatter = RowScatter(partial_ref, got, sent, crossed, s_sems, cuts)
        others = [lax.rem(expert + d, experts) for d in range(1, experts)]
        greet((near, across), [2 * e + half for e in others] + [partner])
        scatter.start()
        for i, (at, size) in enumerate(cuts):
            here = pl.ds(at, size)
            total = residual_ref[here, :] + scatter.total(i)
            third_ref[here, :] = total
            normed = norm_forward(total, gain_ref[...])
            normed = jnp.where(real_rows(at, size, tokens), normed, 0.0)
            routed_ref[here, :] = normed.astype(BF16)
        scatter.finish()

        slot = lax.broadcasted_iota(jnp.int32, (slots, rows), 0)

        def chosen(e, k):
            return (slot + e * slots == target_ref[k : k + 1, :]).astype(F32)

        def exchange(block_of, send, out, base):
            first = []
            for d, e in enumerate(others):
                send[d] = block_of(e)
                first.append(
                    remote(send.at[d], out.at[me], e_sems, base + d, "wide", 2 * e + half)
                )
                first[-1].start()
            out[me] = block_of(expert)
            return first

        def pass_on(first, out, base):
            second = [remote(out.at[me], out.at[me], p_sems, base, "wide", partner)]
            second[0].start()
            for d in range(1, experts):
                first[d - 1].wait_recv()
                source = 2 * lax.rem(expert + experts - d, experts) + half
                second.append(
                    remote(out.at[source], out.at[source], p_sems, base + d, "wide", partner)
                )
                second[-1].start()
            return second

        def row_block(e):
            pick = (chosen(e, 0) + chosen(e, 1)).astype(BF16)
            return jnp.dot(pick, routed_ref[...], preferred_element_type=F32).astype(BF16)

        first_rows = exchange(row_block, send_rows, rows_ref, 0)

        lane = lax.broadcasted_iota(jnp.int32, (rows, LANES), 1)
        logits = jnp.dot(routed_ref[...], router_ref[...], preferred_element_type=F32)
        logits = jnp.where(lane < experts, logits, -1e30)
        exps = jnp.exp(logits - jnp.max(logits, axis=-1, keepdims=True))
        probs = exps / jnp.sum(exps, axis=-1, keepdims=True)
        probs_ref[...] = probs
        gates = jnp.zeros((rows, LANES), F32)
        for k in range(2):
            gate = jnp.sum(
                jnp.where(lane == routes_ref[:, k : k + 1], probs, 0.0), axis=-1, keepdims=True
            )
            gates = jnp.where(lane == k, gate, gates)
            gated_ref[k] = (gate * cot_ref[...].astype(F32)).astype(BF16)
        gates_ref[...] = gates

        def grad_block(e):
            both = jnp.dot(chosen(e, 0).astype(BF16), gated_ref[0], preferred_element_type=F32)
            both += jnp.dot(chosen(e, 1).astype(BF16), gated_ref[1], preferred_element_type=F32)
            return both.astype(BF16)

        first_grads = exchange(grad_block, send_grads, grads_ref, experts)
        second = pass_on(first_rows, rows_ref, 0)
        second += pass_on(first_grads, grads_ref, experts)
        for copy in second:
            copy.wait_recv()
        for copy in first_rows + first_grads + second:
            copy.wait_send()

    return pl.pallas_call(
        kernel,
        out_shape=(
            jax.ShapeDtypeStruct((rows, width), F32),
            jax.ShapeDtypeStruct((rows, width), BF16),
            jax.ShapeDtypeStruct((rows, LANES), F32),
            jax.ShapeDtypeStruct((rows, LANES), F32),
            jax.ShapeDtypeStruct((wide, slots, width), BF16),
            jax.ShapeDtypeStruct((wide, slots, width), BF16),
        ),
        in_specs=[VMEM] * 7,
        out_specs=(VMEM,) * 6,
        scratch_shapes=scatter_scratch(rows, width, PARTS)
        + [
            pltpu.VMEM((experts - 1, slots, width), BF16),
            pltpu.VMEM((experts - 1, slots, width), BF16),
            pltpu.VMEM((2, rows, width), BF16),
            sems(2 * experts),
            sems(2 * experts),
        ],
        compiler_params=comm_params(cid),
    )(partial, residual, gain, router, routes, cotangent, target)


def combine(
    part, row_grads, third, routed, probs, gates, gain, router, routes, cotangent, target, tokens, cid
):
    wide, slots, width = part.shape
    experts = wide // 2
    rows = third.shape[0]
    cuts = cuts_of(rows, PARTS)

    def kernel(
        part_ref,
        row_grads_ref,
        third_ref,
        routed_ref,
        probs_ref,
        gates_ref,
        gain_ref,
        router_ref,
        routes_ref,
        cot_ref,
        target_ref,
        output_ref,
        grad_ref,
        gain_grad_ref,
        router_grad_ref,
        whole_ref,
        from_part,
        from_grads,
        send_part,
        send_grads,
        back_part,
        back_grads,
        e_sems,
        p_sems,
        g_sems,
    ):
        _, near, across, _ = seq_places()
        me, half, expert, partner = wide_places()
        gather = RowGather(whole_ref, g_sems, cuts)
        homes = [lax.rem(expert + d, experts) for d in range(1, experts)] + [expert]
        greet((near, across), [2 * h + half for h in homes[:-1]] + [partner])

        def halves(src, into, base):
            copies = []
            for d, home in enumerate(homes):
                copies.append(
                    remote(
                        src.at[2 * home + 1 - half], into.at[d], p_sems, base + d, "wide", partner
                    )
                )
                copies[-1].start()
            return copies

        def homeward(copies, src, arrived, send, back, base):
            sent = []
            for d, home in enumerate(homes):
                copies[d].wait_recv()
                both = (src[2 * home + half].astype(F32) + arrived[d].astype(F32)).astype(BF16)
                if d == experts - 1:
                    back[expert] = both
                else:
                    send[d] = both
                    sent.append(
                        remote(
                            send.at[d], back.at[expert], e_sems, base + d, "wide", 2 * home + half
                        )
                    )
                    sent[-1].start()
            return sent

        part_halves = halves(part_ref, from_part, 0)
        grad_halves = halves(row_grads_ref, from_grads, experts)
        part_sent = homeward(part_halves, part_ref, from_part, send_part, back_part, 0)
        grad_sent = homeward(
            grad_halves, row_grads_ref, from_grads, send_grads, back_grads, experts
        )

        spot = lax.broadcasted_iota(jnp.int32, (rows, experts * slots), 1)
        picks = [(spot == target_ref[:, k : k + 1]).astype(F32) for k in range(2)]
        cot = cot_ref[...].astype(F32)
        lane = lax.broadcasted_iota(jnp.int32, (rows, LANES), 1)
        for copy in part_sent:
            copy.wait_recv()
        returned = back_part[...].reshape(experts * slots, width)
        output = third_ref[...]
        grad_probs = jnp.zeros((rows, LANES), F32)
        for k in range(2):
            picked = jnp.dot(picks[k].astype(BF16), returned, preferred_element_type=F32)
            output += gates_ref[:, k : k + 1] * picked
            grad_gate = jnp.sum(cot * picked, axis=-1, keepdims=True)
            grad_probs += jnp.where(lane == routes_ref[:, k : k + 1], grad_gate, 0.0)
        output_ref[...] = output[:tokens]
        probs = probs_ref[...]
        delta = jnp.sum(probs * grad_probs, axis=-1, keepdims=True)
        logit_grad = probs * (grad_probs - delta)
        logit_low = logit_grad.astype(BF16)
        router_grad_ref[...] = jnp.dot(
            logit_low.astype(F32).T.astype(BF16), routed_ref[...], preferred_element_type=F32
        )
        routed_grad = lax.dot_general(
            logit_low, router_ref[...], NT, preferred_element_type=F32
        )
        for copy in grad_sent:
            copy.wait_recv()
        routed_grad += jnp.dot(
            (picks[0] + picks[1]).astype(BF16),
            back_grads[...].reshape(experts * slots, width),
            preferred_element_type=F32,
        )
        grad_in, gain_grad = norm_backward(third_ref[...], gain_ref[...], routed_grad)
        gain_grad_ref[...] = gain_grad
        grad_ref[...] = cot + grad_in
        for i, (at, size) in enumerate(cuts):
            gather.send(i, grad_ref[pl.ds(at, size), :].astype(BF16))
        gather.finish()
        for copy in part_halves + grad_halves + part_sent + grad_sent:
            copy.wait_send()

    blocks = pltpu.VMEM((experts, slots, width), BF16)
    sends = pltpu.VMEM((experts - 1, slots, width), BF16)
    return pl.pallas_call(
        kernel,
        out_shape=(
            jax.ShapeDtypeStruct((tokens, width), F32),
            jax.ShapeDtypeStruct((rows, width), F32),
            jax.ShapeDtypeStruct((1, width), F32),
            jax.ShapeDtypeStruct((LANES, width), F32),
            jax.ShapeDtypeStruct((4, rows, width), BF16),
        ),
        in_specs=[VMEM] * 11,
        out_specs=(VMEM,) * 5,
        scratch_shapes=[
            blocks,
            blocks,
            sends,
            sends,
            blocks,
            blocks,
            sems(2 * experts),
            sems(2 * experts),
            sems(3 * PARTS),
        ],
        compiler_params=comm_params(cid),
    )(part, row_grads, third, routed, probs, gates, gain, router, routes, cotangent, target)


def gelu_parts(values):
    cdf = 0.5 * (1.0 + lax.erf(values * 0.5**0.5))
    density = jnp.exp(-0.5 * values * values) * 0.3989422804014327
    return values * cdf, cdf + values * density


def slot_targets(routes, fill_order, experts, capacity, slots):
    tokens = routes.shape[0]
    pair_expert = routes.reshape(-1)
    pair_key = (jnp.arange(2, dtype=jnp.int32)[None, :] * tokens + fill_order[:, None]).reshape(-1)
    same_expert = pair_expert[:, None] == pair_expert[None, :]
    earlier = pair_key[None, :] < pair_key[:, None]
    slot_rank = jnp.sum((same_expert & earlier).astype(jnp.int32), axis=1)
    target = jnp.where(slot_rank < capacity, pair_expert * slots + slot_rank, -1)
    return target.reshape(tokens, 2)


def dense(a, b, dims, dtype=BF16):
    return lax.dot_general(a, b, (dims, ((), ())), preferred_element_type=F32).astype(dtype)


def on_device(
    images,
    cotangent,
    key_mask,
    routes,
    fill_order,
    norm_gain1,
    qkv_weight1,
    proj_weight1,
    norm_gain2,
    fc_in,
    fc_out,
    norm_gain3,
    qkv_weight2,
    proj_weight2,
    norm_gain4,
    router,
    expert_in,
    expert_out,
):
    seq = lax.axis_size("seq")
    wide = lax.axis_size("wide")
    place = lax.axis_index("seq")
    tokens, width = images.shape[1:]
    rows = round_up(tokens, ROW_TILE)
    pad = rows - tokens
    total = seq * rows
    experts = wide // 2
    capacity = (5 * tokens + 2 * experts - 1) // (2 * experts)
    slots = round_up(capacity, ROW_TILE)
    span = width // seq
    heads = span // HEAD_DIM
    group = round_up(span, LANES)
    shard = width // wide
    units = fc_in.shape[1]
    unit_cut = units // (seq * wide)

    def gathered(x):
        return lax.all_gather(x, "wide", axis=0, tiled=True)

    def own_qkv(w):
        own = lax.dynamic_index_in_dim(w.reshape(shard, 3, seq, span), place, 2, keepdims=False)
        own = jnp.pad(own, ((0, 0), (0, 0), (0, group - span)))
        return gathered(own.reshape(shard, 3 * group))

    def own_proj(w):
        own = lax.dynamic_slice_in_dim(gathered(w), place * span, span, 0)
        return jnp.pad(own, ((0, group - span), (0, 0)))

    small = jnp.concatenate(
        [jnp.stack([norm_gain1, norm_gain2, norm_gain3, norm_gain4]), router.T], axis=0
    )
    small = lax.all_gather(small, "wide", axis=0)
    small = small.transpose(1, 0, 2).reshape(4 + experts, width)
    gains = [small[i : i + 1].astype(F32) for i in range(4)]
    router_all = jnp.pad(small[4:].T, ((0, 0), (0, LANES - experts)))

    wqkv_one = own_qkv(qkv_weight1)
    wproj_one = own_proj(proj_weight1)
    w_in = gathered(
        lax.dynamic_index_in_dim(
            fc_in.reshape(shard, wide, seq, unit_cut), place, 2, keepdims=False
        ).reshape(shard, wide * unit_cut)
    )
    w_out = gathered(lax.dynamic_slice_in_dim(fc_out, place * unit_cut, unit_cut, 0))
    wqkv_two = own_qkv(qkv_weight2)
    wproj_two = own_proj(proj_weight2)

    valid = jnp.pad(key_mask[0].reshape(seq, tokens) > 0, ((0, 0), (0, pad)))
    bias = jnp.where(valid, 0.0, -1e30).astype(F32)
    bias_row = bias.reshape(1, total)
    bias_col = bias.reshape(seq, rows, 1)
    target = jnp.pad(
        slot_targets(routes[0], fill_order[0], experts, capacity, slots),
        ((0, pad), (0, 0)),
        constant_values=-1,
    )
    routes_rows = jnp.pad(routes[0], ((0, pad), (0, 0)))
    cot = jnp.pad(cotangent[0], ((0, pad), (0, 0)))
    start = jnp.pad(images[0].astype(F32), ((0, pad), (0, 0)))

    normed_one = spread_norm(start, gains[0], tokens, 1)
    qkv_one, lse_one, mixed_one, part = attend_forward(
        normed_one, wqkv_one, wproj_one, bias_row, heads
    )
    first, normed_two = join_forward(part, start, gains[1], tokens, 2)
    flat_two = normed_two.reshape(total, width)
    pre = dense(flat_two, w_in, ((1,), (0,)), F32)
    hidden, slope = gelu_parts(pre)
    hidden, slope = hidden.astype(BF16), slope.astype(BF16)
    part = dense(hidden, w_out, ((1,), (0,))).reshape(seq, rows, width)
    second, normed_three = join_forward(part, first, gains[2], tokens, 3)
    qkv_two, lse_two, mixed_two, part = attend_forward(
        normed_three, wqkv_two, wproj_two, bias_row, heads
    )
    third, routed, probs, gates, got_rows, got_grads = dispatch(
        part, second, gains[3], router_all, routes_rows, cot, target.T, tokens, slots, 4
    )
    got_rows = got_rows.reshape(wide * slots, width)
    got_grads = got_grads.reshape(wide * slots, width)
    pre = dense(got_rows, expert_in[0], ((1,), (0,)), F32)
    e_hidden, e_slope = gelu_parts(pre)
    e_hidden = e_hidden.astype(BF16)
    e_part = dense(e_hidden, expert_out[0], ((1,), (0,)))
    e_pre = (dense(got_grads, expert_out[0], ((1,), (1,)), F32) * e_slope).astype(BF16)
    e_rows = dense(e_pre, expert_in[0], ((1,), (1,)))
    output, grad, gain4_grad, router_grad, branch = combine(
        e_part.reshape(wide, slots, width),
        e_rows.reshape(wide, slots, width),
        third,
        routed,
        probs,
        gates,
        gains[3],
        router_all,
        routes_rows,
        cot,
        target,
        tokens,
        5,
    )
    e_out_grad = dense(e_hidden, got_grads, ((0,), (0,)))
    e_in_grad = dense(got_rows, e_pre, ((0,), (0,)))

    def attention_terms(normed, mixed, branch, grad_qkv):
        gq = dense(normed.reshape(total, width), grad_qkv.reshape(total, 3 * group), ((0,), (0,)))
        gq = gq.reshape(width, 3, group)[:, :, :span].reshape(width, 3 * span)
        gp = dense(mixed.reshape(total, group)[:, :span], branch.reshape(total, width), ((0,), (0,)))
        gp = lax.all_to_all(gp, "seq", split_axis=1, concat_axis=0, tiled=True)
        return jnp.concatenate([gq, gp], axis=1)

    def reduced(terms):
        own = lax.psum_scatter(terms, "wide", scatter_dimension=0, tiled=True)
        return lax.all_gather(own, "seq", axis=0).astype(F32)

    def attention_grads(whole):
        gq = whole[:, :, : 3 * span].reshape(seq, shard, 3, span).transpose(1, 2, 0, 3)
        gp = whole[:, :, 3 * span :].transpose(1, 0, 2)
        return gq.reshape(shard, 3 * width), gp.reshape(shard, width)

    grad_qkv, part = attend_backward(
        branch, qkv_two, lse_two, mixed_two, wqkv_two, wproj_two, bias_col, heads
    )
    qkv2_grad, proj2_grad = attention_grads(
        reduced(attention_terms(normed_three, mixed_two, branch, grad_qkv))
    )
    grad, gain3_grad, branch = join_backward(part, second, gains[2], grad, tokens, 6, False)
    branch_flat = branch.reshape(total, width)
    pre_grad = (dense(branch_flat, w_out, ((1,), (1,)), F32) * slope).astype(BF16)
    part = dense(pre_grad, w_in, ((1,), (1,))).reshape(seq, rows, width)
    fc_terms = jnp.concatenate(
        [
            dense(flat_two, pre_grad, ((0,), (0,))),
            dense(hidden, branch_flat, ((0,), (0,))),
        ],
        axis=1,
    )
    fc_whole = reduced(fc_terms)
    fc_in_grad = fc_whole[:, :, : wide * unit_cut].reshape(seq, shard, wide, unit_cut)
    fc_in_grad = fc_in_grad.transpose(1, 2, 0, 3).reshape(shard, units)
    fc_out_grad = fc_whole[:, :, wide * unit_cut :].reshape(seq * unit_cut, width)
    grad, gain2_grad, branch = join_backward(part, first, gains[1], grad, tokens, 7, False)
    grad_qkv, part = attend_backward(
        branch, qkv_one, lse_one, mixed_one, wqkv_one, wproj_one, bias_col, heads
    )
    qkv1_grad, proj1_grad = attention_grads(
        reduced(attention_terms(normed_one, mixed_one, branch, grad_qkv))
    )
    image_grad, gain1_grad = join_backward(part, start, gains[0], grad, tokens, 8, True)

    small_grads = jnp.concatenate(
        [gain1_grad, gain2_grad, gain3_grad, gain4_grad, router_grad[:experts]], axis=0
    )
    small_grads = lax.psum(small_grads, ("seq", "wide"))
    small_own = lax.dynamic_slice_in_dim(
        small_grads, lax.axis_index("wide") * shard, shard, 1
    )
    e_in_all = lax.psum(e_in_grad, "seq").astype(F32)
    e_out_all = lax.psum(e_out_grad, "seq").astype(F32)
    return (
        output[None],
        image_grad[None],
        small_own[0],
        qkv1_grad,
        proj1_grad,
        small_own[1],
        fc_in_grad,
        fc_out_grad,
        small_own[2],
        qkv2_grad,
        proj2_grad,
        small_own[3],
        small_own[4:].T,
        e_in_all[None],
        e_out_all[None],
    )


def solution(mesh):
    placed = (
        P("wide", "seq", None),
        P("wide", "seq", None),
        P("wide", None),
        P("wide", "seq", None),
        P("wide", "seq"),
        P("wide"),
        P("wide", None),
        P("wide", None),
        P("wide"),
        P("wide", None),
        P("wide", None),
        P("wide"),
        P("wide", None),
        P("wide", None),
        P("wide"),
        P("wide", None),
        P("wide", None, None),
        P("wide", None, None),
    )
    return jax.shard_map(
        on_device,
        mesh=mesh,
        in_specs=placed,
        out_specs=(
            P("wide", "seq", None),
            P("wide", "seq", None),
            P("wide"),
            P("wide", None),
            P("wide", None),
            P("wide"),
            P("wide", None),
            P("wide", None),
            P("wide"),
            P("wide", None),
            P("wide", None),
            P("wide"),
            P("wide", None),
            P("wide", None, None),
            P("wide", None, None),
        ),
        check_vma=False,
    )
```

time: 1370 us -> 875 us (0.64)
  Pallas kernels: 0 us -> 379 us
  waiting for transfers between devices: 514 us -> 238 us
  matrix products: 277 us -> 68 us
  local copies, waits for them, and re-layouts: 264 us -> 65.6 us
  starting transfers between devices: 111 us -> 7.76 us
  other arithmetic: 101 us -> 11.3 us
    pallas_call x0 -> x12, Pallas kernels: none -> 379 us  [the longest x1 82.2 us: combine(): pl.pallas_call(kernel, out_shape=(jax.ShapeDtypeStruct((tokens, width), F...]
    all_to_all x24 -> x2, waiting for transfers between devices: 256 us -> 3.5 us  [attention_terms(): gp = lax.all_to_all(gp, 'seq', split_axis=1, concat_axis=0, tiled=True)]
    dot_general x39 -> x16, matrix products: 277 us -> 68 us  [dense(): lax.dot_general(a, b, (dims, ((), ())), preferred_element_type=F32)]
    reduce_scatter x0 -> x3, waiting for transfers between devices: none -> 121 us  [reduced(): own = lax.psum_scatter(terms, 'wide', scatter_dimension=0, tiled=True)]
    all_to_all x24 -> x2, starting transfers between devices: 109 us -> 6.93 us  [attention_terms(): gp = lax.all_to_all(gp, 'seq', split_axis=1, concat_axis=0, tiled=True)]
    all_gather x15 -> x7, waiting for transfers between devices: 180 us -> 107 us  [the longest x6 107 us: gathered(): return lax.all_gather(x, 'wide', axis=0, tiled=True)]
    psum x1, waiting for transfers between devices: 71.6 us -> 3.95 us  [on_device(): e_in_all = lax.psum(e_in_grad, 'seq').astype(F32)]
    reshape x36 -> x12, local copies, waits for them, and re-layouts: 77.1 us -> 19.8 us  [the longest x4 5.27 us: attention_grads(): return (gq.reshape(shard, 3 * width), gp.reshape(shard, width))]
  transfers between devices with their start and end apart: 40 -> 13, of which waited for: 26 -> 9; matrix products, arithmetic and copies ran while one was open for 42% -> 11% of each run, Pallas kernels for 0% -> 18%
where the time goes in v1:
time: 875 us; the launch traced here: 870 us
  Pallas kernels  379 us (43%)
  waiting for transfers between devices  238 us (27%)
  blocking collectives  85.9 us (10%)
  matrix products  68 us (8%)
  local copies, waits for them, and re-layouts  65.6 us (7%)
  between operations  15.2 us (2%)
  other arithmetic  11.3 us (1%)
    reduce_scatter x3, waiting for transfers between devices, reduced(): own = lax.psum_scatter(terms, 'wide', scatter_dimension=0, tiled=True)  121 us
    all_gather x6, waiting for transfers between devices, gathered(): return lax.all_gather(x, 'wide', axis=0, tiled=True)  107 us
    pallas_call x1, Pallas kernels, combine(): pl.pallas_call(kernel, out_shape=(jax.ShapeDtypeStruct((tokens, width), F...  82.2 us
    pallas_call x3, Pallas kernels, join_backward(): pl.pallas_call(kernel, out_shape=tuple(out_shape), in_specs=[VMEM] * 4, o...  81.6 us
    pallas_call x1, Pallas kernels, dispatch(): pl.pallas_call(kernel, out_shape=(jax.ShapeDtypeStruct((rows, width), F32...  75 us
    dot_general x16, matrix products, dense(): lax.dot_general(a, b, (dims, ((), ())), preferred_element_type=F32)  68 us
    pallas_call x2, Pallas kernels, join_forward(): pl.pallas_call(kernel, out_shape=(jax.ShapeDtypeStruct((rows, width), F32...  53.6 us
    pallas_call x2, Pallas kernels, attend_backward(): pl.pallas_call(kernel, grid=(blocks,), out_shape=(jax.ShapeDtypeStruct((b...  43.3 us
  transfers between devices with their start and end apart: 13, of which 9 were waited for; matrix products, arithmetic and copies ran while one was open for 11% of the time, Pallas kernels for 18%

profile of v1, /device:TPU:0, one launch (start us, length us, event | category | flops | bytes accessed | tf_op | source)
XLA Modules:
  0.0 869.8 jit_solution(6177243276434637142)
XLA Ops:
  8.7 1.6 reshape.244
  10.3 1.6 reshape.251
  12.0 1.3 constant_dynamic-slice_fusion.2
  14.4 2.3 reshape.248
  16.7 1.9 dynamic-slice_reduce_fusion
  18.6 1.8 reshape.249
  20.5 1.6 constant_dynamic-slice_fusion.3
  23.3 28.3 %all-gather = bf16[64,96]{1,0:T(8,128)(2,1)S(1)} all-gather(bf16[8,96]{1,0:T(8,128)(2,1)S(1)} %concatenate.15), channel_id=2, replica_groups=mesh['seq'=4,'wide'=8] {'wide'}, dimensions={0}, use_global_device_ids=true | all-gather | bytes 13824 | tf_op jit(solution)/shard_map/all_gather | solution.py:845
  62.0 15.6 %shard_map.289.normed_ref = bf16[4,272,768]{2,1,0:T(8,128)(2,1)} custom-call(f32[272,768]{1,0:T(8,128)} %pad_convert_fusion.residual_ref, f32[1,768]{1,0:T(1,128)} %reshape.277.gain_ref), custom_call_target="tpu_custom_call" | custom-call | tf_op jit(solution)/shard_map/pallas_call | solution.py:196
  79.4 16.6 %all-gather.22.cloned.1.call-done = bf16[768,768]{1,0:T(8,128)(2,1)} async-done(((bf16[96,768]{1,0:T(8,128)(2,1)}), bf16[768,768]{1,0:T(8,128)(2,1)}) %all-gather.22.cloned.1.call-update) | async-done | bytes 1179664 | tf_op jit(solution)/shard_map/all_gather | solution.py:831
  97.7 40.9 %all-gather.12.cloned.1.call-done.wqkv_ref = bf16[768,768]{1,0:T(8,128)(2,1)} async-done(((bf16[96,768]{1,0:T(8,128)(2,1)}), bf16[768,768]{1,0:T(8,128)(2,1)}) %all-gather.12.cloned.1.call-update) | async-done | bytes 1179664 | tf_op jit(solution)/shard_map/all_gather | solution.py:831
  138.6 13.6 %shard_map.290 = (bf16[4,272,768]{2,1,0:T(8,128)(2,1)}, f32[4,272,128]{2,1,0:T(8,128)}, bf16[4,272,256]{2,1,0:T(8,128)(2,1)}, bf16[4,272,768]{2,1,0:T(8,128)(2,1)}) custom-call(bf16[4,272,768]{2,1,0:T(8,128)(2,1)} %shard_map.289.normed_ref, bf16[768,768]{1,0:T(8,128)(2,1)} %all-gather.12.cloned.1.call-done.wqkv_ref, bf16[256,768]{1,0:T(8,128)(2,1)} %pad.42.wproj_ref, ...), custom_call_target="tpu_custom_call" | custom-call | tf_op jit(solution)/shard_map/pallas_call | solution.py:342
  152.2 26.8 %shard_map.291 = (f32[272,768]{1,0:T(8,128)}, bf16[4,272,768]{2,1,0:T(8,128)(2,1)}) custom-call(bf16[4,272,768]{2,1,0:T(8,128)(2,1)} %get-tuple-element.50.partial_ref, f32[272,768]{1,0:T(8,128)} %pad_convert_fusion.residual_ref, f32[1,768]{1,0:T(1,128)} %reshape.278.gain_ref), custom_call_target="tpu_custom_call" | custom-call | tf_op jit(solution)/shard_map/pallas_call | solution.py:227
  179.0 2.0 all-gather.16.cloned.1.call-done
  181.0 5.6 multiply_convert_fusion.1
  186.7 36.8 %all-gather.18.cloned.1.call-done = bf16[768,768]{1,0:T(8,128)(2,1)} async-done(((bf16[96,768]{1,0:T(8,128)(2,1)}), bf16[768,768]{1,0:T(8,128)(2,1)}) %all-gather.18.cloned.1.call-update) | async-done | bytes 1179664 | tf_op jit(solution)/shard_map/all_gather | solution.py:831
  223.5 4.4 convolution_convert_fusion.5
  227.9 26.8 %shard_map.292 = (f32[272,768]{1,0:T(8,128)}, bf16[4,272,768]{2,1,0:T(8,128)(2,1)}) custom-call(bf16[4,272,768]{2,1,0:T(8,128)(2,1)} %bitcast.151, f32[272,768]{1,0:T(8,128)} %get-tuple-element.52.residual_ref, f32[1,768]{1,0:T(1,128)} %reshape.279.gain_ref), custom_call_target="tpu_custom_call" | custom-call | tf_op jit(solution)/shard_map/pallas_call | solution.py:227
  254.7 11.2 %all-gather.20.cloned.1.call-done.wqkv_ref = bf16[768,768]{1,0:T(8,128)(2,1)} async-done(((bf16[96,768]{1,0:T(8,128)(2,1)}), bf16[768,768]{1,0:T(8,128)(2,1)}) %all-gather.20.cloned.1.call-update) | async-done | bytes 1179664 | tf_op jit(solution)/shard_map/all_gather | solution.py:831
  265.8 13.8 %shard_map.293 = (bf16[4,272,768]{2,1,0:T(8,128)(2,1)}, f32[4,272,128]{2,1,0:T(8,128)}, bf16[4,272,256]{2,1,0:T(8,128)(2,1)}, bf16[4,272,768]{2,1,0:T(8,128)(2,1)}) custom-call(bf16[4,272,768]{2,1,0:T(8,128)(2,1)} %get-tuple-element.53.normed_ref, bf16[768,768]{1,0:T(8,128)(2,1)} %all-gather.20.cloned.1.call-done.wqkv_ref, bf16[256,768]{1,0:T(8,128)(2,1)} %pad.45.wproj_ref, ...), custom_call_target="tpu_custom_call" | custom-call | tf_op jit(solution)/shard_map/pallas_call | solution.py:342
  279.6 75.0 %shard_map.294 = (f32[272,768]{1,0:T(8,128)}, bf16[272,768]{1,0:T(8,128)(2,1)}, f32[272,128]{1,0:T(8,128)}, f32[272,128]{1,0:T(8,128)}, bf16[8,176,768]{2,1,0:T(8,128)(2,1)}, /*index=5*/bf16[8,176,768]{2,1,0:T(8,128)(2,1)}) custom-call(bf16[4,272,768]{2,1,0:T(8,128)(2,1)} %get-tuple-element.54.partial_ref, f32[272,768]{1,0:T(8,128)} %get-tuple-element.55.residual_ref, ...), custom_call_target="tpu_custom_call" | custom-call | tf_op jit(solution)/shard_map/pallas_call | solution.py:603
  354.7 5.6 multiply_convert_fusion
  360.4 6.1 fusion.4
  366.5 4.8 convolution_convert_fusion.2
  371.3 4.7 convolution_convert_fusion.3
  376.0 82.2 %shard_map.295 = (f32[257,768]{1,0:T(8,128)}, f32[272,768]{1,0:T(8,128)}, f32[1,768]{1,0:T(1,128)}, f32[128,768]{1,0:T(8,128)}, bf16[4,272,768]{2,1,0:T(8,128)(2,1)}) custom-call(bf16[8,176,768]{2,1,0:T(8,128)(2,1)} %bitcast.149, bf16[8,176,768]{2,1,0:T(8,128)(2,1)} %bitcast.148, f32[272,768]{1,0:T(8,128)} %get-tuple-element.58.third_ref, ...), custom_call_target="tpu_custom_call" | custom-call | tf_op jit(solution)/shard_map/pallas_call | solution.py:746
  458.2 21.8 %shard_map.296 = (bf16[4,272,768]{2,1,0:T(8,128)(2,1)}, bf16[4,272,768]{2,1,0:T(8,128)(2,1)}) custom-call(bf16[4,272,768]{2,1,0:T(8,128)(2,1)} %get-tuple-element.63.branch_ref, bf16[4,272,768]{2,1,0:T(8,128)(2,1)} %get-tuple-element.64.qkv_ref, f32[4,272,128]{2,1,0:T(8,128)} %get-tuple-element.65.lse_ref, bf16[4,272,256]{2,1,0:T(8,128)(2,1)} %get-tuple-element.66.mixed_ref, ...), custom_call_target="tpu_custom_call" | custom-call | tf_op jit(solution)/shard_map/pallas_call | solution.py:462
  480.0 28.6 %shard_map.297 = (f32[272,768]{1,0:T(8,128)}, f32[1,768]{1,0:T(1,128)}, bf16[4,272,768]{2,1,0:T(8,128)(2,1)}) custom-call(bf16[4,272,768]{2,1,0:T(8,128)(2,1)} %get-tuple-element.67.partial_ref, f32[272,768]{1,0:T(8,128)} %get-tuple-element.55.residual_ref, f32[1,768]{1,0:T(1,128)} %reshape.279.gain_ref, f32[272,768]{1,0:T(8,128)} %get-tuple-element.68.grad_ref), custom_call_target="tpu_custom_call" | custom-call | tf_op jit(solution)/shard_map/pallas_call | solution.py:281
  508.6 3.3 convolution_convert_fusion.6
  512.0 2.3 fusion.5
  514.3 1.7 convolution_convert_fusion.7
  516.2 2.5 copy.151
  519.0 8.3 fusion.11
  527.3 7.4 fusion.12
  534.7 1.4 copy-done.2
  537.8 3.5 all-to-all-start.1
  541.3 3.8 bitcast_convert_fusion
  545.1 3.5 all-to-all-done.1
  549.4 1.5 copy.153
  550.9 4.2 convolution_convert_fusion.4
  555.0 26.8 %shard_map.298 = (f32[272,768]{1,0:T(8,128)}, f32[1,768]{1,0:T(1,128)}, bf16[4,272,768]{2,1,0:T(8,128)(2,1)}) custom-call(bf16[4,272,768]{2,1,0:T(8,128)(2,1)} %bitcast.150, f32[272,768]{1,0:T(8,128)} %get-tuple-element.52.residual_ref, f32[1,768]{1,0:T(1,128)} %reshape.278.gain_ref, f32[272,768]{1,0:T(8,128)} %get-tuple-element.70.grad_ref), custom_call_target="tpu_custom_call" | custom-call | tf_op jit(solution)/shard_map/pallas_call | solution.py:281
  581.8 2.0 convolution_convert_fusion.9
  584.8 3.5 all-to-all-start
  588.5 21.5 %shard_map.299 = (bf16[4,272,768]{2,1,0:T(8,128)(2,1)}, bf16[4,272,768]{2,1,0:T(8,128)(2,1)}) custom-call(bf16[4,272,768]{2,1,0:T(8,128)(2,1)} %get-tuple-element.71.branch_ref, bf16[4,272,768]{2,1,0:T(8,128)(2,1)} %get-tuple-element.72.qkv_ref, f32[4,272,128]{2,1,0:T(8,128)} %get-tuple-element.73.lse_ref, bf16[4,272,256]{2,1,0:T(8,128)(2,1)} %get-tuple-element.74.mixed_ref, ...), custom_call_target="tpu_custom_call" | custom-call | tf_op jit(solution)/shard_map/pallas_call | solution.py:462
  610.0 3.2 bitcast_convert_fusion.1
  614.0 1.5 copy.149
  617.0 26.2 %shard_map.300 = (f32[257,768]{1,0:T(8,128)}, f32[1,768]{1,0:T(1,128)}) custom-call(bf16[4,272,768]{2,1,0:T(8,128)(2,1)} %get-tuple-element.75.partial_ref, f32[272,768]{1,0:T(8,128)} %pad_convert_fusion.residual_ref, f32[1,768]{1,0:T(1,128)} %reshape.277.gain_ref, f32[272,768]{1,0:T(8,128)} %get-tuple-element.76.grad_ref), custom_call_target="tpu_custom_call" | custom-call | tf_op jit(solution)/shard_map/pallas_call | solution.py:281
  643.2 2.9 copy.146
  646.1 1.7 copy.145
  647.8 42.1 %psum.21 = f32[8,768]{1,0:T(8,128)S(1)} all-reduce(f32[8,768]{1,0:T(8,128)S(1)} %concatenate.16), channel_id=1, replica_groups=mesh['seq'=4,'wide'=8] {'seq','wide'}, use_global_device_ids=true, to_apply=%region_1.2 | all-reduce | flops 6144 | bytes 49152 | tf_op jit(solution)/shard_map/psum | solution.py:966
  691.1 4.0 all-reduce.13.cloned.1.call-done
  695.1 4.6 broadcast_in_dim.37
  699.7 2.5 broadcast_in_dim.39
  702.3 61.7 %reduce-scatter.14.cloned.1.call-done = bf16[96,768]{1,0:T(8,128)(2,1)} async-done(((bf16[768,768]{1,0:T(8,128)(2,1)}), bf16[96,768]{1,0:T(8,128)(2,1)}) %reduce-scatter.14.cloned.1.call-update) | async-done | bytes 147472 | tf_op jit(solution)/shard_map/reduce_scatter | solution.py:925
  764.0 7.7 all-gather.3
  772.9 58.8 %reduce-scatter.10.cloned.1.call-done = bf16[96,768]{1,0:T(8,128)(2,1)} async-done(((bf16[768,768]{1,0:T(8,128)(2,1)}), bf16[96,768]{1,0:T(8,128)(2,1)}) %reduce-scatter.10.cloned.1.call-update) | async-done | bytes 147472 | tf_op jit(solution)/shard_map/reduce_scatter | solution.py:925
  831.7 7.7 all-gather.1
  841.8 1.7 reshape.275
  843.5 1.2 slice_bitcast_fusion
  847.1 1.7 reshape.265
  851.2 2.5 fusion.21
  853.6 1.9 reshape.267
  855.5 3.7 copy.138
  859.2 3.6 reshape.268
  (166 shorter events, 33.6 us)
Async XLA Ops:
  7.2 347.5 %copy-start = (bf16[1,768,1536]{2,1,0:T(8,128)(2,1)S(1)}, bf16[1,768,1536]{2,1,0:T(8,128)(2,1)}, u32[]{:S(2)}) copy-start(bf16[1,768,1536]{2,1,0:T(8,128)(2,1)} %param.34) | copy-start | bytes 7077892
  7.2 70.4 %all-gather.14.cloned.1.call-start = ((), (), s32[]{:S(2)}) async-start(), calls=%async_computation.6 | async-start | bytes 1327104 | tf_op jit(solution)/shard_map/all_gather | solution.py:831
  7.9 88.0 %all-gather.22.cloned.1.call-start = ((), (), s32[]{:S(2)}) async-start(), calls=%async_computation.10 | async-start | bytes 1327104 | tf_op jit(solution)/shard_map/all_gather | solution.py:831
  8.7 129.9 %all-gather.12.cloned.1.call-start = ((), (), s32[]{:S(2)}) async-start(), calls=%async_computation.5 | async-start | bytes 1327104 | tf_op jit(solution)/shard_map/all_gather | solution.py:831
  13.3 8.9 %copy-start.7 = (bf16[96,3,1,192]{3,2,1,0:T(2,128)(2,1)S(1)}, bf16[96,3,1,192]{3,2,1,0:T(2,128)(2,1)}, u32[]{:S(2)}) copy-start(bf16[96,3,1,192]{3,2,1,0:T(2,128)(2,1)} %get-tuple-element.180) | copy-start | bytes 331780
  14.3 8.9 %copy-start.18 = (bf16[96,4]{0,1:T(4,128)(2,1)S(1)}, bf16[96,4]{0,1:T(4,128)(2,1)}, u32[]{:S(2)}) copy-start(bf16[96,4]{0,1:T(4,128)(2,1)} %param.33) | copy-start | bytes 2308
  14.3 8.9 %copy-start.19 = (bf16[96]{0:T(256)(128)(2,1)S(1)}, bf16[96]{0:T(256)(128)(2,1)}, u32[]{:S(2)}) copy-start(bf16[96]{0:T(256)(128)(2,1)} %param.23) | copy-start | bytes 580
  14.3 8.9 %copy-start.20 = (bf16[96]{0:T(256)(128)(2,1)S(1)}, bf16[96]{0:T(256)(128)(2,1)}, u32[]{:S(2)}) copy-start(bf16[96]{0:T(256)(128)(2,1)} %param.26) | copy-start | bytes 580
  14.3 8.9 %copy-start.21 = (bf16[96]{0:T(256)(128)(2,1)S(1)}, bf16[96]{0:T(256)(128)(2,1)}, u32[]{:S(2)}) copy-start(bf16[96]{0:T(256)(128)(2,1)} %param.29) | copy-start | bytes 580
  14.3 8.9 %copy-start.22 = (bf16[96]{0:T(256)(128)(2,1)S(1)}, bf16[96]{0:T(256)(128)(2,1)}, u32[]{:S(2)}) copy-start(bf16[96]{0:T(256)(128)(2,1)} %param.32) | copy-start | bytes 580
  14.3 37.3 %copy-start.11 = (s32[1,1028]{1,0:T(1,128)S(1)}, s32[1,1028]{1,0:T(1,128)}, u32[]{:S(2)}) copy-start(s32[1,1028]{1,0:T(1,128)} %param.20) | copy-start | bytes 12340
  14.3 40.1 %copy-start.16 = (s32[1,257,2]{1,2,0:T(2,128)S(1)}, s32[1,257,2]{1,2,0:T(2,128)}, u32[]{:S(2)}) copy-start(s32[1,257,2]{1,2,0:T(2,128)} %param.21) | copy-start | bytes 6172
  14.3 166.7 %all-gather.16.cloned.1.call-start = ((), (), s32[]{:S(2)}) async-start(), calls=%async_computation.7 | async-start | bytes 1327104 | tf_op jit(solution)/shard_map/all_gather | solution.py:831
  16.7 38.0 %copy-start.17 = (s32[1,257]{1,0:T(1,128)S(1)}, s32[1,257]{1,0:T(1,128)}, u32[]{:S(2)}) copy-start(s32[1,257]{1,0:T(1,128)} %param.22) | copy-start | bytes 3088
  20.4 203.0 %all-gather.18.cloned.1.call-start = ((), (), s32[]{:S(2)}) async-start(), calls=%async_computation.8 | async-start | bytes 1327104 | tf_op jit(solution)/shard_map/all_gather | solution.py:831
  22.1 243.7 %all-gather.20.cloned.1.call-start = ((), (), s32[]{:S(2)}) async-start(), calls=%async_computation.9 | async-start | bytes 1327104 | tf_op jit(solution)/shard_map/all_gather | solution.py:831
  22.2 37.1 %copy-start.9 = (bf16[1,257,768]{2,1,0:T(8,128)(2,1)S(1)}, bf16[1,257,768]{2,1,0:T(8,128)(2,1)}, u32[]{:S(2)}) copy-start(bf16[1,257,768]{2,1,0:T(8,128)(2,1)} %param.19) | copy-start | bytes 1184260
  23.1 38.0 %copy-start.10 = (bf16[1,257,768]{2,1,0:T(8,128)(2,1)S(1)}, bf16[1,257,768]{2,1,0:T(8,128)(2,1)}, u32[]{:S(2)}) copy-start(bf16[1,257,768]{2,1,0:T(8,128)(2,1)} %param.18) | copy-start | bytes 1184260
  23.1 592.4 %reduce-scatter.12.cloned.1.call-start = ((), (), s32[]{:S(2)}) async-start(), calls=%async_computation.13 | async-start | bytes 2654208 | tf_op jit(solution)/shard_map/reduce_scatter | solution.py:925
  354.7 5.7 copy-start.23
  354.7 5.7 copy-start.24
  360.4 10.9 %copy-start.34 = (bf16[1408,1536]{1,0:T(8,128)(2,1)}, bf16[1408,1536]{1,0:T(8,128)(2,1)S(1)}, u32[]{:S(2)}) copy-start(bf16[1408,1536]{1,0:T(8,128)(2,1)S(1)} %get-tuple-element.178) | copy-start | bytes 12976132
  366.5 4.8 copy-start.33
  480.0 28.7 %copy-start.31 = (bf16[1088,768]{1,0:T(8,128)(2,1)S(1)}, bf16[1088,768]{1,0:T(8,128)(2,1)}, u32[]{:S(2)}) copy-start(bf16[1088,768]{1,0:T(8,128)(2,1)} %get-tuple-element.176) | copy-start | bytes 5013508
  508.6 3.4 copy-start.27
  508.6 3.4 copy-start.29
  508.6 3.4 copy-start.30
  512.0 2.3 copy-start.26
  514.3 1.8 copy-start.32
  518.8 8.5 copy-start.25
  518.8 176.3 %all-reduce.13.cloned.1.call-start = ((), (), s32[]{:S(2)}) async-start(), calls=%async_computation.15 | async-start | bytes 9437184 | tf_op jit(solution)/shard_map/psum | solution.py:970
  534.7 1.5 copy-start.2
  534.7 1.6 copy-start.6
  537.8 10.9 %all-to-all-start.1 = ((bf16[192,4,192]{0,2,1:T(8,128)(2,1)}), bf16[192,4,192]{0,2,1:T(8,128)(2,1)S(1)}, u32[]{:S(2)}, u32[]{:S(2)}) async-start(bf16[192,4,192]{0,2,1:T(8,128)(2,1)} %bitcast.52), calls=%async_computation.1 | async-start | bytes 786432 | tf_op jit(solution)/shard_map/all_to_all | solution.py:921
  541.3 222.8 %reduce-scatter.14.cloned.1.call-start = ((), (), s32[]{:S(2)}) async-start(), calls=%async_computation.14 | async-start | bytes 1327104 | tf_op jit(solution)/shard_map/reduce_scatter | solution.py:925
  549.4 1.5 copy-start.28
  555.0 26.8 %copy-start.5 = (bf16[4,272,256]{2,1,0:T(8,128)(2,1)S(1)}, bf16[4,272,256]{2,1,0:T(8,128)(2,1)}, u32[]{:S(2)}) copy-start(bf16[4,272,256]{2,1,0:T(8,128)(2,1)} %get-tuple-element.74.mixed_ref) | copy-start | bytes 1671172
  584.8 28.5 %all-to-all-start = ((bf16[192,4,192]{0,2,1:T(8,128)(2,1)}), bf16[192,4,192]{0,2,1:T(8,128)(2,1)S(1)}, u32[]{:S(2)}, u32[]{:S(2)}) async-start(bf16[192,4,192]{0,2,1:T(8,128)(2,1)} %bitcast.34), calls=%async_computation | async-start | bytes 786432 | tf_op jit(solution)/shard_map/all_to_all | solution.py:921
  588.2 243.5 %reduce-scatter.10.cloned.1.call-start = ((), (), s32[]{:S(2)}) async-start(), calls=%async_computation.12 | async-start | bytes 1327104 | tf_op jit(solution)/shard_map/reduce_scatter | solution.py:925
  588.5 21.5 %copy-start.3 = (bf16[4,272,768]{2,1,0:T(8,128)(2,1)S(1)}, bf16[4,272,768]{2,1,0:T(8,128)(2,1)}, u32[]{:S(2)}) copy-start(bf16[4,272,768]{2,1,0:T(8,128)(2,1)} %shard_map.289.normed_ref) | copy-start | bytes 5013508
  615.5 235.7 %all-gather.24.cloned.1.call-start = ((), (), s32[]{:S(2)}) async-start(), calls=%async_computation.11 | async-start | bytes 1474560 | tf_op jit(solution)/shard_map/all_gather | solution.py:926
  617.0 29.1 %copy-start.8 = (f32[257,768]{1,0:T(8,128)S(1)}, f32[257,768]{1,0:T(8,128)}, u32[]{:S(2)}) copy-start(f32[257,768]{1,0:T(8,128)} %get-tuple-element.62) | copy-start | bytes 2368516
  643.2 4.6 copy-start.12
  643.2 4.6 copy-start.13
  643.2 4.6 copy-start.14
  643.2 4.6 copy-start.15
  695.1 4.7 copy-start.4
  855.5 7.3 copy-start.1
Sparse Core Ops, SparseCore 0:
  10.2 43.8 all-gather.13
  56.3 39.6 all-gather.21
  98.7 39.7 all-gather.11
  141.2 39.7 all-gather.15
  183.6 39.7 all-gather.17
  226.1 39.7 all-gather.19
  518.9 69.5 reduce-scatter.11
  591.5 103.5 all-reduce.12
  699.1 64.9 reduce-scatter.13
  767.8 63.8 reduce-scatter.9
  833.3 16.3 all-gather.23

commit v2 on v1

v2 whole, which is shorter than its diff:
```python
import functools

import jax
import jax.numpy as jnp
from jax import lax
from jax.experimental import pallas as pl
from jax.experimental.pallas import tpu as pltpu
from jax.sharding import PartitionSpec as P

HEAD_DIM = 64
LANES = 128
ROW_TILE = 16
F32 = jnp.float32
BF16 = jnp.bfloat16
VMEM = pl.BlockSpec(memory_space=pltpu.VMEM)
ANY = pl.BlockSpec(memory_space=pl.ANY)
NT = (((1,), (1,)), ((), ()))


def round_up(n, m):
    return -(-n // m) * m


def seq_places():
    me = lax.axis_index("seq")
    near = me + 1 - 2 * lax.rem(me, 2)
    across = lax.rem(me + 2, 4)
    far = lax.rem(near + 2, 4)
    return me, near, across, far


def cuts_of(rows, parts):
    tiles = rows // ROW_TILE
    edges = [(tiles * i // parts) * ROW_TILE for i in range(parts + 1)]
    return [(a, b - a) for a, b in zip(edges[:-1], edges[1:])]


class Bank:
    def __init__(self, sems):
        self.sems, self.used = sems, 0

    def pair(self):
        self.used += 1
        return self.sems.at[0, self.used - 1], self.sems.at[1, self.used - 1]

    def remote(self, src, dst, axis, place, recv=None):
        send, own = self.pair()
        return pltpu.make_async_remote_copy(
            src_ref=src,
            dst_ref=dst,
            send_sem=send,
            recv_sem=own if recv is None else recv,
            device_id={axis: place},
            device_id_type=pl.DeviceIdType.MESH,
        )

    def local(self, src, dst):
        return pltpu.make_async_copy(src, dst, self.pair()[0])


def greet(seq_peers, wide_peers=()):
    barrier = pltpu.get_barrier_semaphore()
    for place in seq_peers:
        pl.semaphore_signal(
            barrier, inc=1, device_id={"seq": place}, device_id_type=pl.DeviceIdType.MESH
        )
    for place in wide_peers:
        pl.semaphore_signal(
            barrier, inc=1, device_id={"wide": place}, device_id_type=pl.DeviceIdType.MESH
        )
    pl.semaphore_wait(barrier, len(seq_peers) + len(wide_peers))


class RowScatter:
    def __init__(self, bank, partial, got, sent, crossed, cuts):
        self.partial, self.got, self.sent, self.crossed = partial, got, sent, crossed
        me, near, across, far = seq_places()
        self.me, self.across = me, across
        self.cuts = cuts
        self.far_part, self.near_part, self.cross = [], [], []
        for at, size in cuts:
            rows = pl.ds(at, size)
            self.far_part.append(bank.remote(partial.at[far, rows], got.at[1, rows], "seq", near))
            self.near_part.append(bank.remote(partial.at[near, rows], got.at[0, rows], "seq", near))
            self.cross.append(bank.remote(sent.at[rows], crossed.at[rows], "seq", across))

    def start(self):
        for copy in self.far_part:
            copy.start()
        for copy in self.near_part:
            copy.start()
        for i, (at, size) in enumerate(self.cuts):
            rows = pl.ds(at, size)
            self.far_part[i].wait_recv()
            self.sent[rows, :] = (
                self.partial[self.across, rows].astype(F32) + self.got[1, rows].astype(F32)
            ).astype(BF16)
            self.cross[i].start()

    def total(self, i):
        at, size = self.cuts[i]
        rows = pl.ds(at, size)
        self.near_part[i].wait_recv()
        chip = self.partial[self.me, rows].astype(F32) + self.got[0, rows].astype(F32)
        self.cross[i].wait_recv()
        return chip + self.crossed[rows, :].astype(F32)

    def finish(self):
        for copy in self.far_part + self.near_part + self.cross:
            copy.wait_send()


class RowGather:
    def __init__(self, bank, whole, cuts):
        self.whole = whole
        me, near, across, far = seq_places()
        self.me = me
        self.cuts = cuts
        self.near_copy, self.cross, self.onward = [], [], []
        for at, size in cuts:
            mine = whole.at[me, pl.ds(at, size)]
            theirs = whole.at[across, pl.ds(at, size)]
            self.near_copy.append(bank.remote(mine, mine, "seq", near))
            self.cross.append(bank.remote(mine, mine, "seq", across))
            self.onward.append(bank.remote(theirs, theirs, "seq", near))

    def send(self, i, rows):
        at, size = self.cuts[i]
        self.whole[self.me, pl.ds(at, size)] = rows
        self.cross[i].start()
        self.near_copy[i].start()

    def finish(self):
        for i in range(len(self.cuts)):
            self.cross[i].wait_recv()
            self.onward[i].start()
        for copy in self.near_copy + self.onward:
            copy.wait_recv()
        for copy in self.near_copy + self.cross + self.onward:
            copy.wait_send()


def wide_places():
    me = lax.axis_index("wide")
    half = lax.rem(me, 2)
    return me, half, me // 2, me + 1 - 2 * half


def wide_peers():
    _, half, pair, partner = wide_places()
    pairs = lax.axis_size("wide") // 2
    return [2 * lax.rem(pair + d, pairs) + half for d in range(1, pairs)] + [partner]


class Spread:
    def __init__(self, bank, src, dst):
        me, half, pair, partner = wide_places()
        pairs = lax.axis_size("wide") // 2
        self.own = bank.local(src, dst.at[me])
        self.first = [bank.remote(src, dst.at[me], "wide", p) for p in wide_peers()[:-1]]
        self.second = [bank.remote(src, dst.at[me], "wide", partner)]
        for d in range(1, pairs):
            source = 2 * lax.rem(pair + pairs - d, pairs) + half
            self.second.append(bank.remote(dst.at[source], dst.at[source], "wide", partner))

    def start(self):
        for copy in self.first:
            copy.start()
        self.second[0].start()
        self.own.start()

    def advance(self):
        for arrived, onward in zip(self.first, self.second[1:]):
            arrived.wait_recv()
            onward.start()

    def finish(self):
        for copy in self.second:
            copy.wait_recv()
        for copy in self.first + self.second:
            copy.wait_send()
        self.own.wait()


class RootSpread:
    def __init__(self, bank, src, dst):
        me, half, pair, partner = wide_places()
        self.root = pair == lax.axis_index("seq")
        landed = bank.pair()[1]
        self.own = bank.local(src, dst.at[half])
        self.out = [
            bank.remote(src, dst.at[half], "wide", p, recv=landed) for p in wide_peers()[:-1]
        ]
        self.onward = bank.remote(dst.at[half], dst.at[half], "wide", partner)

    def start(self):
        @pl.when(self.root)
        def _():
            for copy in self.out:
                copy.start()
            self.own.start()

    def advance(self):
        @pl.when(self.root)
        def _():
            self.own.wait()

        @pl.when(jnp.logical_not(self.root))
        def _():
            self.out[0].wait_recv()

        self.onward.start()

    def finish(self):
        self.onward.wait_recv()
        self.onward.wait_send()

        @pl.when(self.root)
        def _():
            for copy in self.out:
                copy.wait_send()


class Reduce:
    def __init__(self, bank, terms, came, sent, back):
        self.terms, self.came, self.sent, self.back = terms, came, sent, back
        _, self.half, self.pair, partner = wide_places()
        pairs = lax.axis_size("wide") // 2
        self.homes = [lax.rem(self.pair + d, pairs) for d in range(1, pairs)] + [self.pair]
        self.halves = [
            bank.remote(terms.at[2 * h + 1 - self.half], came.at[d], "wide", partner)
            for d, h in enumerate(self.homes)
        ]
        self.home = [
            bank.remote(sent.at[d], back.at[self.pair], "wide", 2 * h + self.half)
            for d, h in enumerate(self.homes[:-1])
        ]

    def start(self):
        for copy in self.halves:
            copy.start()

    def advance(self):
        for d, h in enumerate(self.homes):
            self.halves[d].wait_recv()
            both = self.terms[2 * h + self.half].astype(F32) + self.came[d].astype(F32)
            if d < len(self.home):
                self.sent[d] = both.astype(self.sent.dtype)
                self.home[d].start()
            else:
                self.back[self.pair] = both.astype(self.back.dtype)

    def total(self):
        for copy in self.home:
            copy.wait_recv()
        total = self.back[0].astype(F32)
        for p in range(1, self.back.shape[0]):
            total = total + self.back[p].astype(F32)
        return total

    def finish(self):
        for copy in self.halves + self.home:
            copy.wait_send()


class RootReduce:
    def __init__(self, bank, terms, came, sent, back, low, out):
        self.terms, self.came, self.sent, self.back = terms, came, sent, back
        self.low = low
        _, self.half, self.pair, partner = wide_places()
        me, near, across, far = seq_places()
        pairs = lax.axis_size("wide") // 2
        self.root = self.pair == me
        self.halves = bank.remote(terms.at[1 - self.half], came, "wide", partner)
        self.to_root = []
        for d in range(1, pairs):
            place = lax.rem(self.pair + d, pairs)
            copy = bank.remote(sent, back.at[self.pair], "wide", 2 * place + self.half)
            self.to_root.append((place == me, copy))
        landed = bank.pair()[1]
        self.own = bank.local(low, out)
        self.cast = [bank.remote(low, out, "seq", p, recv=landed) for p in (across, far, near)]

    def start(self):
        self.halves.start()

    def advance(self):
        self.halves.wait_recv()
        both = (self.terms[self.half].astype(F32) + self.came[...].astype(F32)).astype(BF16)
        self.sent[...] = both

        @pl.when(self.root)
        def _():
            self.back[self.pair] = both

        for mine, copy in self.to_root:

            @pl.when(mine)
            def _():
                copy.start()

    def settle(self):
        @pl.when(self.root)
        def _():
            for _, copy in self.to_root:
                copy.wait_recv()
            total = self.back[0].astype(F32)
            for p in range(1, self.back.shape[0]):
                total = total + self.back[p].astype(F32)
            self.low[...] = total.astype(BF16)
            for copy in self.cast:
                copy.start()
            self.own.start()

    def finish(self):
        self.halves.wait_send()
        for mine, copy in self.to_root:

            @pl.when(mine)
            def _():
                copy.wait_send()

        @pl.when(self.root)
        def _():
            for copy in self.cast:
                copy.wait_send()
            self.own.wait()

        @pl.when(jnp.logical_not(self.root))
        def _():
            self.cast[0].wait_recv()


class BlockGather:
    def __init__(self, bank, src, whole):
        me, near, across, far = seq_places()
        self.own = bank.local(src, whole.at[me])
        self.near_copy = bank.remote(src, whole.at[me], "seq", near)
        self.cross = bank.remote(src, whole.at[me], "seq", across)
        self.onward = bank.remote(whole.at[across], whole.at[across], "seq", near)

    def start(self):
        self.cross.start()
        self.near_copy.start()
        self.own.start()

    def advance(self):
        self.cross.wait_recv()
        self.onward.start()

    def finish(self):
        self.near_copy.wait_recv()
        self.onward.wait_recv()
        self.own.wait()
        for copy in (self.near_copy, self.cross, self.onward):
            copy.wait_send()


class Task:
    def __init__(self, ins, outs, scratch, make):
        self.ins, self.outs, self.scratch, self.make = ins, outs, scratch, make


def like(x):
    return jax.ShapeDtypeStruct(x.shape, x.dtype)


def spread_task(block, view=lambda ref: ref, shape=None):
    shape = block.shape if shape is None else shape
    wide = lax.axis_size("wide")
    return Task(
        [(block, VMEM)],
        [(jax.ShapeDtypeStruct((wide, *shape), block.dtype), ANY)],
        [],
        lambda bank, ins, outs, scratch: Spread(bank, view(ins[0]), outs[0]),
    )


def root_spread_task(block):
    return Task(
        [(block, VMEM)],
        [(jax.ShapeDtypeStruct((2, *block.shape), block.dtype), ANY)],
        [],
        lambda bank, ins, outs, scratch: RootSpread(bank, ins[0], outs[0]),
    )


def reduce_scratch(block, dtype=BF16):
    pairs = lax.axis_size("wide") // 2
    return [
        pltpu.VMEM((pairs, *block), dtype),
        pltpu.VMEM((max(pairs - 1, 1), *block), dtype),
        pltpu.VMEM((pairs, *block), dtype),
    ]


class ReduceOut(Reduce):
    def __init__(self, bank, terms, out, scratch):
        super().__init__(bank, terms, *scratch)
        self.out = out

    def finish(self):
        self.out[...] = self.total().astype(BF16)
        super().finish()


def reduce_task(terms):
    return Task(
        [(terms, VMEM)],
        [(jax.ShapeDtypeStruct(terms.shape[1:], BF16), VMEM)],
        reduce_scratch(terms.shape[1:]),
        lambda bank, ins, outs, scratch: ReduceOut(bank, ins[0], outs[0], scratch),
    )


class RootReduceOut(RootReduce):
    def finish(self):
        self.settle()
        super().finish()


def root_reduce_task(terms):
    block = terms.shape[1:]
    pairs = lax.axis_size("wide") // 2
    one = pltpu.VMEM(block, BF16)
    return Task(
        [(terms, VMEM)],
        [(jax.ShapeDtypeStruct(block, BF16), ANY)],
        [one, one, pltpu.VMEM((pairs, *block), BF16), one],
        lambda bank, ins, outs, scratch: RootReduceOut(bank, ins[0], *scratch, outs[0]),
    )


def block_gather_task(block):
    return Task(
        [(block, VMEM)],
        [(jax.ShapeDtypeStruct((4, *block.shape), block.dtype), ANY)],
        [],
        lambda bank, ins, outs, scratch: BlockGather(bank, ins[0], outs[0]),
    )


MAX_COPIES = 96


def call(body, ins, outs, scratch, tasks=(), cid=None, grid=None):
    all_ins, all_outs, all_scratch = list(ins), list(outs), list(scratch)
    for task in tasks:
        all_ins += task.ins
        all_outs += task.outs
        all_scratch += task.scratch
    remote = cid is not None
    if remote:
        all_scratch.append(pltpu.SemaphoreType.DMA((2, MAX_COPIES)))

    def kernel(*refs):
        refs = list(refs)
        groups = []
        for count, key in ((len(ins), "ins"), (len(outs), "outs"), (len(scratch), "scratch")):
            own, refs = refs[:count], refs[count:]
            of_tasks = []
            for task in tasks:
                n = len(getattr(task, key))
                of_tasks.append(refs[:n])
                refs = refs[n:]
            groups.append((own, of_tasks))
        bank = Bank(refs[0]) if remote else None
        live = [
            task.make(bank, groups[0][1][i], groups[1][1][i], groups[2][1][i])
            for i, task in enumerate(tasks)
        ]
        body(groups[0][0], groups[1][0], groups[2][0], bank, live)

    params = {}
    if remote:
        params = dict(collective_id=cid, has_side_effects=True)
    extra = {}
    if grid is not None:
        params["dimension_semantics"] = ("arbitrary",)
        extra["grid"] = grid
    return pl.pallas_call(
        kernel,
        out_shape=tuple(shape for shape, _ in all_outs),
        in_specs=[spec for _, spec in all_ins],
        out_specs=tuple(spec for _, spec in all_outs),
        scratch_shapes=all_scratch,
        compiler_params=pltpu.CompilerParams(**params),
        **extra,
    )(*[x for x, _ in all_ins])


def meet(tasks, far=False):
    _, near, across, beyond = seq_places()
    greet((near, across) + ((beyond,) if far else ()), wide_peers() if tasks else ())


def real_rows(at, size, tokens):
    return at + lax.broadcasted_iota(jnp.int32, (size, 1), 0) < tokens


def centre(values):
    centred = values - jnp.mean(values, axis=-1, keepdims=True)
    variance = jnp.mean(centred * centred, axis=-1, keepdims=True)
    scale = lax.rsqrt(variance + 1e-06)
    return centred * scale, scale


def norm_forward(values, gain):
    return centre(values)[0] * gain


def norm_backward(values, gain, grad):
    unit, scale = centre(values)
    grad_unit = grad * gain
    grad_in = scale * (
        grad_unit
        - jnp.mean(grad_unit, axis=-1, keepdims=True)
        - unit * jnp.mean(grad_unit * unit, axis=-1, keepdims=True)
    )
    return grad_in, jnp.sum(grad * unit, axis=0, keepdims=True)


def scatter_scratch(rows, width):
    return [
        pltpu.VMEM((2, rows, width), BF16),
        pltpu.VMEM((rows, width), BF16),
        pltpu.VMEM((rows, width), BF16),
    ]


PARTS = 2


def spread_norm(residual, gains, tokens, cid):
    rows, width = residual.shape
    cuts = cuts_of(rows, PARTS)

    def body(ins, outs, scratch, bank, tasks):
        residual_ref, gains_ref = ins
        gather = RowGather(bank, outs[0], cuts)
        meet(tasks)
        for i, (at, size) in enumerate(cuts):
            normed = norm_forward(residual_ref[pl.ds(at, size), :], gains_ref[0:1, :])
            normed = jnp.where(real_rows(at, size, tokens), normed, 0.0)
            gather.send(i, normed.astype(BF16))
        gather.finish()

    return call(
        body,
        [(residual, VMEM), (gains, VMEM)],
        [(jax.ShapeDtypeStruct((4, rows, width), BF16), VMEM)],
        [],
        cid=cid,
    )[0]


def own_columns(ref, parts, span, group, place):
    rows = ref.shape[0]
    width = ref.shape[1] // parts
    blocks = []
    for part in range(parts):
        own = jnp.zeros((rows, span), F32)
        for s in range(width // span):
            at = part * width + s * span
            own = jnp.where(place == s, ref[:, at : at + span].astype(F32), own)
        blocks.append((part * group, own))
    return blocks


def own_units(ref, place, seq):
    rows = ref.shape[0]
    cut = LANES // seq
    lane = lax.broadcasted_iota(jnp.int32, (rows, LANES), 1)
    tiles = []
    for tile in range(ref.shape[1] // (seq * LANES)):
        own = jnp.zeros((rows, LANES), F32)
        for q in range(seq):
            at = (tile * seq + q) * LANES
            shift = lax.rem(cut * q + LANES - cut * place, LANES)
            turned = pltpu.roll(ref[:, at : at + LANES].astype(F32), shift, 1)
            own = jnp.where(lane // cut == q, turned, own)
        tiles.append(own)
    return tiles


def begin(residual, small, qkv_one, proj_one, qkv_two, fc_in, tokens, span, group, cid):
    rows, width = residual.shape
    shard = qkv_one.shape[0]
    wide = lax.axis_size("wide")
    seq = lax.axis_size("seq")
    cuts = cuts_of(rows, PARTS)
    units = fc_in.shape[1] // seq

    def body(ins, outs, scratch, bank, tasks):
        residual_ref, small_ref, qkv1_ref, proj1_ref, qkv2_ref, fc_ref = ins
        whole_ref, gains_ref, router_ref, qkv2_own, fc_own, wqkv_ref, wproj_ref = outs
        small_all, own_ref = scratch
        place = lax.axis_index("seq")
        gather = RowGather(bank, whole_ref, cuts)
        smalls = Spread(bank, small_ref, small_all)
        weights = Spread(bank, own_ref, wqkv_ref)
        proj = RootSpread(bank, proj1_ref, wproj_ref)
        _, near, across, _ = seq_places()
        greet((near, across), wide_peers())
        smalls.start()
        own_ref[...] = jnp.zeros_like(own_ref)
        for at, own in own_columns(qkv1_ref, 3, span, group, place):
            own_ref[:, at : at + span] = own.astype(BF16)
        weights.start()
        proj.start()
        smalls.advance()
        smalls.finish()
        column = lax.broadcasted_iota(jnp.int32, (LANES, width), 1)
        lane = lax.broadcasted_iota(jnp.int32, (LANES, width), 0)
        joined = jnp.zeros((small_ref.shape[0], width), F32)
        for w in range(wide):
            spot = ((column == lane + w * shard) & (lane < shard)).astype(F32).astype(BF16)
            joined += jnp.dot(small_all[w], spot, preferred_element_type=F32)
        gains_ref[...] = joined
        experts = wide // 2
        router_ref[...] = jnp.zeros_like(router_ref)
        router_ref[0 : joined.shape[0], :] = jnp.concatenate(
            [joined[4:], jnp.zeros((4, width), F32)], axis=0
        ).astype(BF16)
        for i, (at, size) in enumerate(cuts):
            normed = norm_forward(residual_ref[pl.ds(at, size), :], gains_ref[0:1, :])
            normed = jnp.where(real_rows(at, size, tokens), normed, 0.0)
            gather.send(i, normed.astype(BF16))
        proj.advance()
        weights.advance()
        qkv2_own[...] = jnp.zeros_like(qkv2_own)
        for at, own in own_columns(qkv2_ref, 3, span, group, place):
            qkv2_own[:, at : at + span] = own.astype(BF16)
        for tile, own in enumerate(own_units(fc_ref, place, seq)):
            fc_own[:, tile * LANES : (tile + 1) * LANES] = own.astype(BF16)
        gather.finish()
        proj.finish()
        weights.finish()

    shape = jax.ShapeDtypeStruct
    return call(
        body,
        [(x, VMEM) for x in (residual, small, qkv_one, proj_one, qkv_two, fc_in)],
        [
            (shape((4, rows, width), BF16), VMEM),
            (shape((small.shape[0], width), F32), VMEM),
            (shape((LANES, width), BF16), VMEM),
            (shape((shard, 3 * group), BF16), VMEM),
            (shape((shard, units), BF16), VMEM),
            (shape((wide, shard, 3 * group), BF16), ANY),
            (shape((2, shard, width), BF16), ANY),
        ],
        [
            pltpu.VMEM((wide, *small.shape), BF16),
            pltpu.VMEM((shard, 3 * group), BF16),
        ],
        cid=cid,
    )


def join_forward(partial, residual, gains, which, tokens, cid, tasks=()):
    rows, width = residual.shape
    cuts = cuts_of(rows, PARTS)

    def body(ins, outs, scratch, bank, tasks):
        partial_ref, residual_ref, gains_ref = ins
        out_ref, whole_ref = outs
        scatter = RowScatter(bank, partial_ref, *scratch, cuts)
        gather = RowGather(bank, whole_ref, cuts)
        meet(tasks)
        for task in tasks:
            task.start()
        scatter.start()
        for i, (at, size) in enumerate(cuts):
            total = residual_ref[pl.ds(at, size), :] + scatter.total(i)
            out_ref[pl.ds(at, size), :] = total
            normed = norm_forward(total, gains_ref[which : which + 1, :])
            normed = jnp.where(real_rows(at, size, tokens), normed, 0.0)
            gather.send(i, normed.astype(BF16))
        for task in tasks:
            task.advance()
        gather.finish()
        scatter.finish()
        for task in tasks:
            task.finish()

    return call(
        body,
        [(partial, VMEM), (residual, VMEM), (gains, VMEM)],
        [
            (jax.ShapeDtypeStruct((rows, width), F32), VMEM),
            (jax.ShapeDtypeStruct((4, rows, width), BF16), VMEM),
        ],
        scatter_scratch(rows, width),
        tasks,
        cid,
    )


def join_backward(partial, residual, gains, which, grad, tokens, cid, tasks=()):
    rows, width = residual.shape
    cuts = cuts_of(rows, PARTS)

    def body(ins, outs, scratch, bank, tasks):
        partial_ref, residual_ref, gains_ref, grad_ref = ins
        out_ref, gain_grad_ref, whole_ref = outs
        gather = RowGather(bank, whole_ref, cuts)
        scatter = RowScatter(bank, partial_ref, *scratch, cuts)
        meet(tasks, far=bool(tasks))
        for task in tasks:
            task.start()
        scatter.start()
        gain_grad = jnp.zeros((1, width), F32)
        for i, (at, size) in enumerate(cuts):
            rows_here = pl.ds(at, size)
            grad_in, term = norm_backward(
                residual_ref[rows_here, :], gains_ref[which : which + 1, :], scatter.total(i)
            )
            gain_grad = gain_grad + term
            grad_out = grad_ref[rows_here, :] + grad_in
            out_ref[rows_here, :] = grad_out
            gather.send(i, grad_out.astype(BF16))
        gain_grad_ref[...] = gain_grad
        for task in tasks:
            task.advance()
        gather.finish()
        scatter.finish()
        for task in tasks:
            task.finish()

    return call(
        body,
        [(partial, VMEM), (residual, VMEM), (gains, VMEM), (grad, VMEM)],
        [
            (jax.ShapeDtypeStruct((rows, width), F32), VMEM),
            (jax.ShapeDtypeStruct((1, width), F32), VMEM),
            (jax.ShapeDtypeStruct((4, rows, width), BF16), VMEM),
        ],
        scatter_scratch(rows, width),
        tasks,
        cid,
    )


def close_plain(partial, residual, gains, grad, tokens, cid):
    rows, width = residual.shape
    cuts = cuts_of(rows, PARTS)

    def body(ins, outs, scratch, bank, tasks):
        partial_ref, residual_ref, gains_ref, grad_ref = ins
        out_ref, gain_grad_ref = outs
        scatter = RowScatter(bank, partial_ref, *scratch, cuts)
        meet(tasks)
        scatter.start()
        gain_grad = jnp.zeros((1, width), F32)
        for i, (at, size) in enumerate(cuts):
            rows_here = pl.ds(at, size)
            grad_in, term = norm_backward(
                residual_ref[rows_here, :], gains_ref[0:1, :], scatter.total(i)
            )
            gain_grad = gain_grad + term
            keep = min(size, tokens - at)
            out_ref[pl.ds(at, keep), :] = (grad_ref[rows_here, :] + grad_in)[:keep]
        gain_grad_ref[...] = gain_grad
        scatter.finish()

    return call(
        body,
        [(partial, VMEM), (residual, VMEM), (gains, VMEM), (grad, VMEM)],
        [
            (jax.ShapeDtypeStruct((tokens, width), F32), VMEM),
            (jax.ShapeDtypeStruct((1, width), F32), VMEM),
        ],
        scatter_scratch(rows, width),
        cid=cid,
    )


def close(partial, residual, gains, grad, smalls, qkv_terms, proj_terms, fc_block, tokens, cid):
    rows, width = residual.shape
    cuts = cuts_of(rows, PARTS)
    wide = lax.axis_size("wide")
    shard = qkv_terms.shape[1]
    block = qkv_terms.shape[1:]
    small_rows = ROW_TILE

    def body(ins, outs, scratch, bank, tasks):
        partial_ref, residual_ref, gains_ref, grad_ref, smalls_ref, terms_ref, fc_ref = ins
        out_ref, small_ref, qkv_ref, fc_all = outs
        scatter = RowScatter(bank, partial_ref, *scratch[:3], cuts)
        reduce = Reduce(bank, terms_ref, *scratch[3:6])
        low_ref = scratch[6]
        small_terms = scratch[7]
        small = Reduce(bank, small_terms, *scratch[8:11])
        mine, met, both, crossed = scratch[11:15]
        _, near, across, far = seq_places()
        spread = BlockGather(bank, low_ref, qkv_ref)
        fc = BlockGather(bank, fc_ref, fc_all)
        to_near = bank.remote(mine, met, "seq", near)
        to_across = bank.remote(both, crossed, "seq", across)
        greet((near, across, far), wide_peers())
        for task in tasks:
            task.start()
        reduce.start()
        scatter.start()
        gain_grad = jnp.zeros((1, width), F32)
        for i, (at, size) in enumerate(cuts):
            rows_here = pl.ds(at, size)
            grad_in, term = norm_backward(
                residual_ref[rows_here, :], gains_ref[0:1, :], scatter.total(i)
            )
            gain_grad = gain_grad + term
            keep = min(size, tokens - at)
            out_ref[pl.ds(at, keep), :] = (grad_ref[rows_here, :] + grad_in)[:keep]
        fc.start()
        terms = jnp.concatenate(
            [gain_grad, smalls_ref[...], jnp.zeros((small_rows - 1 - smalls_ref.shape[0], width), F32)],
            axis=0,
        )
        high = terms.astype(BF16)
        rest = (terms - high.astype(F32)).astype(BF16)
        column = lax.broadcasted_iota(jnp.int32, (LANES, width), 1)
        lane = lax.broadcasted_iota(jnp.int32, (LANES, width), 0)
        for w in range(wide):
            spot = ((column == lane + w * shard) & (lane < shard)).astype(F32).astype(BF16)
            small_terms[w] = lax.dot_general(
                high, spot, NT, preferred_element_type=F32
            ) + lax.dot_general(rest, spot, NT, preferred_element_type=F32)
        small.start()
        for task in tasks:
            task.advance()
        reduce.advance()
        small.advance()
        fc.advance()
        low_ref[...] = reduce.total().astype(BF16)
        spread.start()
        mine[...] = small.total()
        to_near.start()
        for task in tasks:
            task.settle()
        to_near.wait_recv()
        both[...] = mine[...] + met[...]
        to_across.start()
        spread.advance()
        to_across.wait_recv()
        small_ref[...] = both[...] + crossed[...]
        scatter.finish()
        reduce.finish()
        small.finish()
        fc.finish()
        spread.finish()
        for task in tasks:
            task.finish()
        to_near.wait_send()
        to_across.wait_send()

    shape = jax.ShapeDtypeStruct
    small_block = pltpu.VMEM((small_rows, LANES), F32)
    root = root_reduce_task(proj_terms)
    root.make = lambda bank, ins, outs, scratch: RootReduce(bank, ins[0], *scratch, outs[0])
    return call(
        body,
        [
            (x, VMEM)
            for x in (partial, residual, gains, grad, smalls, qkv_terms, fc_block)
        ],
        [
            (shape((tokens, width), F32), VMEM),
            (shape((small_rows, LANES), F32), VMEM),
            (shape((4, *block), BF16), ANY),
            (shape((4, *fc_block.shape), BF16), ANY),
        ],
        scatter_scratch(rows, width)
        + reduce_scratch(block)
        + [pltpu.VMEM(block, BF16), pltpu.VMEM((wide, small_rows, LANES), F32)]
        + reduce_scratch((small_rows, LANES), F32)
        + [small_block] * 4,
        [root],
        cid,
    )


def assemble(qkv_one, qkv_two, fc_in, fc_out, proj_one, proj_two, span, group):
    seq, shard, _ = qkv_one.shape
    width = proj_one.shape[1]
    cut = LANES // seq
    tiles = fc_in.shape[2] // LANES

    def body(ins, outs, scratch, bank, tasks):
        for src, out in zip(ins[:2], outs[:2]):
            for part in range(3):
                for s in range(seq):
                    at = part * width + s * span
                    out[:, at : at + span] = src[s, :, part * group : part * group + span].astype(
                        F32
                    )
        lane = lax.broadcasted_iota(jnp.int32, (shard, LANES), 1)
        for tile in range(tiles):
            pieces = [
                ins[2][s, :, tile * LANES : (tile + 1) * LANES].astype(F32) for s in range(seq)
            ]
            for q in range(seq):
                own = jnp.zeros((shard, LANES), F32)
                for s in range(seq):
                    turned = pieces[s]
                    if s != q:
                        turned = pltpu.roll(turned, (cut * (s - q)) % LANES, 1)
                    own = jnp.where(lane // cut == s, turned, own)
                at = (tile * seq + q) * LANES
                outs[2][:, at : at + LANES] = own
        for s in range(seq):
            for g in range(fc_out.shape[1] // cut):
                outs[3][pl.ds(g * LANES + s * cut, cut), :] = ins[3][s, pl.ds(g * cut, cut), :].astype(
                    F32
                )
        outs[4][...] = ins[4][...].astype(F32)
        outs[5][...] = ins[5][...].astype(F32)

    shape = jax.ShapeDtypeStruct
    return call(
        body,
        [(x, VMEM) for x in (qkv_one, qkv_two, fc_in, fc_out, proj_one, proj_two)],
        [
            (shape((shard, 3 * width), F32), VMEM),
            (shape((shard, 3 * width), F32), VMEM),
            (shape((shard, seq * fc_in.shape[2]), F32), VMEM),
            (shape((seq * fc_out.shape[1], width), F32), VMEM),
            (shape((shard, width), F32), VMEM),
            (shape((shard, width), F32), VMEM),
        ],
        [],
    )


def head_lanes(rows, head):
    lane = lax.broadcasted_iota(jnp.int32, (rows, LANES), 1)
    low = (head % 2) * HEAD_DIM
    return (lane >= low) & (lane < low + HEAD_DIM)


def kept(*shape):
    return pl.BlockSpec(shape, lambda i: (0,) * len(shape))


def padded_rows(ref, src, span):
    ref[0:span, :] = src[...].reshape(span, src.shape[-1])
    ref[span:, :] = jnp.zeros((ref.shape[0] - span, ref.shape[1]), ref.dtype)


def attend_forward(normed_all, wqkv, wproj, bias_row, heads, cid=None, tasks=()):
    blocks, rows, width = normed_all.shape
    group = wqkv.shape[1] // 3
    span = heads * HEAD_DIM
    total = blocks * rows

    def body(ins, outs, scratch, bank, tasks):
        normed_ref, wqkv_ref, wproj_in, bias_ref = ins
        qkv_ref, lse_ref, mixed_ref, part_ref = outs
        (wproj_ref,) = scratch
        step = pl.program_id(0)

        @pl.when(step == 0)
        def _():
            if tasks:
                meet(tasks)
            for task in tasks:
                task.start()
            padded_rows(wproj_ref, wproj_in, span)

            @pl.loop(0, blocks)
            def _(b):
                qkv_ref[b] = jnp.dot(
                    normed_ref[b], wqkv_ref[...], preferred_element_type=F32
                ).astype(BF16)

        lane = lax.broadcasted_iota(jnp.int32, (rows, LANES), 1)
        lse = jnp.zeros((rows, LANES), F32)
        for pair in range(group // LANES):
            lo = pair * LANES
            query = qkv_ref[step, :, lo : lo + LANES].astype(F32) * HEAD_DIM ** (-0.5)
            keys = qkv_ref[:, :, group + lo : group + lo + LANES].reshape(total, LANES)
            values = qkv_ref[:, :, 2 * group + lo : 2 * group + lo + LANES].reshape(total, LANES)
            mixed = jnp.zeros((rows, LANES), F32)
            for head in range(2 * pair, min(2 * pair + 2, heads)):
                mine = head_lanes(rows, head)
                scores = lax.dot_general(
                    jnp.where(mine, query, 0.0).astype(BF16), keys, NT, preferred_element_type=F32
                )
                scores = scores + bias_ref[...]
                peak = jnp.max(scores, axis=-1, keepdims=True)
                exps = jnp.exp(scores - peak)
                row_total = jnp.sum(exps, axis=-1, keepdims=True)
                out = jnp.dot(exps.astype(BF16), values, preferred_element_type=F32)
                mixed = jnp.where(mine, out / row_total, mixed)
                lse = jnp.where(lane == head, peak + jnp.log(row_total), lse)
            mixed_ref[step, :, lo : lo + LANES] = mixed.astype(BF16)
        lse_ref[step] = lse
        part_ref[step] = jnp.dot(
            mixed_ref[step], wproj_ref[...], preferred_element_type=F32
        ).astype(BF16)

        if tasks:

            @pl.when(step == blocks - 2)
            def _():
                for task in tasks:
                    task.advance()

            @pl.when(step == blocks - 1)
            def _():
                for task in tasks:
                    task.finish()

    shape = jax.ShapeDtypeStruct
    return call(
        body,
        [
            (normed_all, kept(blocks, rows, width)),
            (wqkv, kept(width, 3 * group)),
            (wproj, kept(*wproj.shape)),
            (bias_row, kept(1, total)),
        ],
        [
            (shape((blocks, rows, 3 * group), BF16), kept(blocks, rows, 3 * group)),
            (shape((blocks, rows, LANES), F32), kept(blocks, rows, LANES)),
            (shape((blocks, rows, group), BF16), kept(blocks, rows, group)),
            (shape((blocks, rows, width), BF16), kept(blocks, rows, width)),
        ],
        [pltpu.VMEM((group, width), BF16)],
        tasks,
        cid,
        (blocks,),
    )


def attend_backward(branch_all, qkv, lse, mixed, wqkv, wproj, bias_col, heads, cid=None, tasks=()):
    blocks, rows, width = branch_all.shape
    group = wqkv.shape[1] // 3
    span = heads * HEAD_DIM
    pairs = group // LANES
    total = blocks * rows

    def body(ins, outs, scratch, bank, tasks):
        branch_ref, qkv_ref, lse_ref, mixed_ref, wqkv_ref, wproj_in, bias_ref = ins
        grad_ref, part_ref = outs
        gm_ref, query_ref, grads_ref, stats_ref, dq_ref, wproj_ref = scratch
        step = pl.program_id(0)

        @pl.when(step == 0)
        def _():
            if tasks:
                meet(tasks)
            for task in tasks:
                task.start()
            padded_rows(wproj_ref, wproj_in, span)

            @pl.loop(0, blocks)
            def _(b):
                gm_ref[b] = lax.dot_general(
                    branch_ref[b], wproj_ref[...], NT, preferred_element_type=F32
                ).astype(BF16)

            lse_rows = lse_ref[...].reshape(total, LANES).T
            for head in range(heads):
                lo = (head // 2) * LANES
                mine = head_lanes(total, head)
                query = qkv_ref[:, :, lo : lo + LANES].reshape(total, LANES).astype(F32)
                query_ref[head] = jnp.where(mine, query * HEAD_DIM ** (-0.5), 0.0).astype(BF16)
                grads = gm_ref[:, :, lo : lo + LANES].reshape(total, LANES).astype(F32)
                grads = jnp.where(mine, grads, 0.0)
                grads_ref[head] = grads.astype(BF16)
                out = mixed_ref[:, :, lo : lo + LANES].reshape(total, LANES).astype(F32)
                stats_ref[head] = jnp.concatenate(
                    [
                        lse_rows[head : head + 1],
                        jnp.sum((grads * out).T, axis=0, keepdims=True),
                        jnp.zeros((6, total), F32),
                    ],
                    axis=0,
                )
            dq_ref[...] = jnp.zeros_like(dq_ref)

        for pair in range(pairs):
            lo = pair * LANES
            keys = qkv_ref[step, :, group + lo : group + lo + LANES]
            values = qkv_ref[step, :, 2 * group + lo : 2 * group + lo + LANES]
            grad_keys = jnp.zeros((rows, LANES), F32)
            grad_values = jnp.zeros((rows, LANES), F32)
            for head in range(2 * pair, min(2 * pair + 2, heads)):
                scores = lax.dot_general(keys, query_ref[head], NT, preferred_element_type=F32)
                probs = jnp.exp(scores + bias_ref[step] - stats_ref[head, 0:1])
                grad_probs = lax.dot_general(
                    values, grads_ref[head], NT, preferred_element_type=F32
                )
                grad_scores = (probs * (grad_probs - stats_ref[head, 1:2])).astype(BF16)
                grad_values += jnp.dot(
                    probs.astype(BF16), grads_ref[head], preferred_element_type=F32
                )
                grad_keys += jnp.dot(grad_scores, query_ref[head], preferred_element_type=F32)
                mine = head_lanes(rows, head)
                own_keys = jnp.where(mine, keys.astype(F32), 0.0).T.astype(BF16)
                dq_ref[pl.ds(lo, LANES), :] += jnp.dot(
                    own_keys, grad_scores, preferred_element_type=F32
                )
            grad_ref[step, :, group + lo : group + lo + LANES] = grad_keys.astype(BF16)
            grad_ref[step, :, 2 * group + lo : 2 * group + lo + LANES] = grad_values.astype(BF16)

        if tasks:

            @pl.when(step == blocks - 2)
            def _():
                for task in tasks:
                    task.advance()

        @pl.when(step == blocks - 1)
        def _():
            for pair in range(pairs):
                lo = pair * LANES
                grad_query = dq_ref[pl.ds(lo, LANES), :].T * HEAD_DIM ** (-0.5)
                grad_ref[:, :, lo : lo + LANES] = grad_query.astype(BF16).reshape(
                    blocks, rows, LANES
                )

            @pl.loop(0, blocks)
            def _(b):
                part_ref[b] = lax.dot_general(
                    grad_ref[b], wqkv_ref[...], NT, preferred_element_type=F32
                ).astype(BF16)

            for task in tasks:
                task.finish()

    shape = jax.ShapeDtypeStruct
    return call(
        body,
        [
            (branch_all, kept(blocks, rows, width)),
            (qkv, kept(blocks, rows, 3 * group)),
            (lse, kept(blocks, rows, LANES)),
            (mixed, kept(blocks, rows, group)),
            (wqkv, kept(width, 3 * group)),
            (wproj, kept(*wproj.shape)),
            (bias_col, kept(blocks, rows, 1)),
        ],
        [
            (shape((blocks, rows, 3 * group), BF16), kept(blocks, rows, 3 * group)),
            (shape((blocks, rows, width), BF16), kept(blocks, rows, width)),
        ],
        [
            pltpu.VMEM((blocks, rows, group), BF16),
            pltpu.VMEM((heads, total, LANES), BF16),
            pltpu.VMEM((heads, total, LANES), BF16),
            pltpu.VMEM((heads, 8, total), F32),
            pltpu.VMEM((group, total), F32),
            pltpu.VMEM((group, width), BF16),
        ],
        tasks,
        cid,
        (blocks,),
    )


def dispatch(partial, residual, gains, router, routes, cotangent, target, tokens, slots, cid):
    rows, width = residual.shape
    wide = lax.axis_size("wide")
    experts = wide // 2
    cuts = cuts_of(rows, PARTS)

    def kernel(
        partial_ref,
        residual_ref,
        gain_ref,
        router_ref,
        routes_ref,
        cot_ref,
        target_ref,
        third_ref,
        routed_ref,
        probs_ref,
        gates_ref,
        rows_ref,
        grads_ref,
        got,
        sent,
        crossed,
        send_rows,
        send_grads,
        gated_ref,
        all_sems,
    ):
        bank = Bank(all_sems)
        _, near, across, _ = seq_places()
        me, half, expert, partner = wide_places()
        scatter = RowScatter(bank, partial_ref, got, sent, crossed, cuts)
        others = [lax.rem(expert + d, experts) for d in range(1, experts)]
        greet((near, across), [2 * e + half for e in others] + [partner])
        scatter.start()
        for i, (at, size) in enumerate(cuts):
            here = pl.ds(at, size)
            total = residual_ref[here, :] + scatter.total(i)
            third_ref[here, :] = total
            normed = norm_forward(total, gain_ref[3:4, :])
            normed = jnp.where(real_rows(at, size, tokens), normed, 0.0)
            routed_ref[here, :] = normed.astype(BF16)
        scatter.finish()

        slot = lax.broadcasted_iota(jnp.int32, (slots, rows), 0)

        def chosen(e, k):
            return (slot + e * slots == target_ref[k : k + 1, :]).astype(F32)

        def exchange(block_of, send, out):
            first = []
            for d, e in enumerate(others):
                send[d] = block_of(e)
                first.append(bank.remote(send.at[d], out.at[me], "wide", 2 * e + half))
                first[-1].start()
            out[me] = block_of(expert)
            return first

        def pass_on(first, out):
            second = [bank.remote(out.at[me], out.at[me], "wide", partner)]
            second[0].start()
            for d in range(1, experts):
                first[d - 1].wait_recv()
                source = 2 * lax.rem(expert + experts - d, experts) + half
                second.append(bank.remote(out.at[source], out.at[source], "wide", partner))
                second[-1].start()
            return second

        def row_block(e):
            pick = (chosen(e, 0) + chosen(e, 1)).astype(BF16)
            return jnp.dot(pick, routed_ref[...], preferred_element_type=F32).astype(BF16)

        first_rows = exchange(row_block, send_rows, rows_ref)

        lane = lax.broadcasted_iota(jnp.int32, (rows, LANES), 1)
        logits = lax.dot_general(
            routed_ref[...], router_ref[...], NT, preferred_element_type=F32
        )
        logits = jnp.where(lane < experts, logits, -1e30)
        exps = jnp.exp(logits - jnp.max(logits, axis=-1, keepdims=True))
        probs = exps / jnp.sum(exps, axis=-1, keepdims=True)
        probs_ref[...] = probs
        gates = jnp.zeros((rows, LANES), F32)
        for k in range(2):
            gate = jnp.sum(
                jnp.where(lane == routes_ref[:, k : k + 1], probs, 0.0), axis=-1, keepdims=True
            )
            gates = jnp.where(lane == k, gate, gates)
            gated_ref[k] = (gate * cot_ref[...].astype(F32)).astype(BF16)
        gates_ref[...] = gates

        def grad_block(e):
            both = jnp.dot(chosen(e, 0).astype(BF16), gated_ref[0], preferred_element_type=F32)
            both += jnp.dot(chosen(e, 1).astype(BF16), gated_ref[1], preferred_element_type=F32)
            return both.astype(BF16)

        first_grads = exchange(grad_block, send_grads, grads_ref)
        second = pass_on(first_rows, rows_ref)
        second += pass_on(first_grads, grads_ref)
        for copy in second:
            copy.wait_recv()
        for copy in first_rows + first_grads + second:
            copy.wait_send()

    return pl.pallas_call(
        kernel,
        out_shape=(
            jax.ShapeDtypeStruct((rows, width), F32),
            jax.ShapeDtypeStruct((rows, width), BF16),
            jax.ShapeDtypeStruct((rows, LANES), F32),
            jax.ShapeDtypeStruct((rows, LANES), F32),
            jax.ShapeDtypeStruct((wide, slots, width), BF16),
            jax.ShapeDtypeStruct((wide, slots, width), BF16),
        ),
        in_specs=[VMEM] * 7,
        out_specs=(VMEM,) * 6,
        scratch_shapes=scatter_scratch(rows, width)
        + [
            pltpu.VMEM((experts - 1, slots, width), BF16),
            pltpu.VMEM((experts - 1, slots, width), BF16),
            pltpu.VMEM((2, rows, width), BF16),
            pltpu.SemaphoreType.DMA((2, 4 * experts + 3 * PARTS)),
        ],
        compiler_params=pltpu.CompilerParams(collective_id=cid, has_side_effects=True),
    )(partial, residual, gains, router, routes, cotangent, target)


def combine(
    part, row_grads, third, routed, probs, gates, gains, router, routes, cotangent, target, tokens, cid
):
    wide, slots, width = part.shape
    experts = wide // 2
    rows = third.shape[0]
    cuts = cuts_of(rows, PARTS)

    def kernel(
        part_ref,
        row_grads_ref,
        third_ref,
        routed_ref,
        probs_ref,
        gates_ref,
        gain_ref,
        router_ref,
        routes_ref,
        cot_ref,
        target_ref,
        output_ref,
        grad_ref,
        gain_grad_ref,
        router_grad_ref,
        whole_ref,
        from_part,
        from_grads,
        send_part,
        send_grads,
        back_part,
        back_grads,
        all_sems,
    ):
        bank = Bank(all_sems)
        _, near, across, _ = seq_places()
        me, half, expert, partner = wide_places()
        gather = RowGather(bank, whole_ref, cuts)
        homes = [lax.rem(expert + d, experts) for d in range(1, experts)] + [expert]
        greet((near, across), [2 * h + half for h in homes[:-1]] + [partner])

        def halves(src, into):
            copies = []
            for d, home in enumerate(homes):
                copies.append(
                    bank.remote(src.at[2 * home + 1 - half], into.at[d], "wide", partner)
                )
                copies[-1].start()
            return copies

        def homeward(copies, src, arrived, send, back):
            sent = []
            for d, home in enumerate(homes):
                copies[d].wait_recv()
                both = (src[2 * home + half].astype(F32) + arrived[d].astype(F32)).astype(BF16)
                if d == experts - 1:
                    back[expert] = both
                else:
                    send[d] = both
                    sent.append(
                        bank.remote(send.at[d], back.at[expert], "wide", 2 * home + half)
                    )
                    sent[-1].start()
            return sent

        part_halves = halves(part_ref, from_part)
        grad_halves = halves(row_grads_ref, from_grads)
        part_sent = homeward(part_halves, part_ref, from_part, send_part, back_part)
        grad_sent = homeward(
            grad_halves, row_grads_ref, from_grads, send_grads, back_grads
        )

        spot = lax.broadcasted_iota(jnp.int32, (rows, experts * slots), 1)
        picks = [(spot == target_ref[:, k : k + 1]).astype(F32) for k in range(2)]
        cot = cot_ref[...].astype(F32)
        lane = lax.broadcasted_iota(jnp.int32, (rows, LANES), 1)
        for copy in part_sent:
            copy.wait_recv()
        returned = back_part[...].reshape(experts * slots, width)
        output = third_ref[...]
        grad_probs = jnp.zeros((rows, LANES), F32)
        for k in range(2):
            picked = jnp.dot(picks[k].astype(BF16), returned, preferred_element_type=F32)
            output += gates_ref[:, k : k + 1] * picked
            grad_gate = jnp.sum(cot * picked, axis=-1, keepdims=True)
            grad_probs += jnp.where(lane == routes_ref[:, k : k + 1], grad_gate, 0.0)
        output_ref[...] = output[:tokens]
        probs = probs_ref[...]
        delta = jnp.sum(probs * grad_probs, axis=-1, keepdims=True)
        logit_grad = probs * (grad_probs - delta)
        logit_low = logit_grad.astype(BF16)
        router_grad_ref[...] = jnp.dot(
            logit_low.astype(F32).T.astype(BF16), routed_ref[...], preferred_element_type=F32
        )
        routed_grad = jnp.dot(logit_low, router_ref[...], preferred_element_type=F32)
        for copy in grad_sent:
            copy.wait_recv()
        routed_grad += jnp.dot(
            (picks[0] + picks[1]).astype(BF16),
            back_grads[...].reshape(experts * slots, width),
            preferred_element_type=F32,
        )
        grad_in, gain_grad = norm_backward(third_ref[...], gain_ref[3:4, :], routed_grad)
        gain_grad_ref[...] = gain_grad
        grad_ref[...] = cot + grad_in
        for i, (at, size) in enumerate(cuts):
            gather.send(i, grad_ref[pl.ds(at, size), :].astype(BF16))
        gather.finish()
        for copy in part_halves + grad_halves + part_sent + grad_sent:
            copy.wait_send()

    blocks = pltpu.VMEM((experts, slots, width), BF16)
    sends = pltpu.VMEM((experts - 1, slots, width), BF16)
    return pl.pallas_call(
        kernel,
        out_shape=(
            jax.ShapeDtypeStruct((tokens, width), F32),
            jax.ShapeDtypeStruct((rows, width), F32),
            jax.ShapeDtypeStruct((1, width), F32),
            jax.ShapeDtypeStruct((LANES, width), F32),
            jax.ShapeDtypeStruct((4, rows, width), BF16),
        ),
        in_specs=[VMEM] * 11,
        out_specs=(VMEM,) * 5,
        scratch_shapes=[
            blocks,
            blocks,
            sends,
            sends,
            blocks,
            blocks,
            pltpu.SemaphoreType.DMA((2, 4 * experts + 3 * PARTS)),
        ],
        compiler_params=pltpu.CompilerParams(collective_id=cid, has_side_effects=True),
    )(part, row_grads, third, routed, probs, gates, gains, router, routes, cotangent, target)


def gelu_parts(values):
    cdf = 0.5 * (1.0 + lax.erf(values * 0.5**0.5))
    density = jnp.exp(-0.5 * values * values) * 0.3989422804014327
    return values * cdf, cdf + values * density


def slot_targets(routes, fill_order, experts, capacity, slots):
    tokens = routes.shape[0]
    pair_expert = routes.reshape(-1)
    pair_key = (jnp.arange(2, dtype=jnp.int32)[None, :] * tokens + fill_order[:, None]).reshape(-1)
    same_expert = pair_expert[:, None] == pair_expert[None, :]
    earlier = pair_key[None, :] < pair_key[:, None]
    slot_rank = jnp.sum((same_expert & earlier).astype(jnp.int32), axis=1)
    target = jnp.where(slot_rank < capacity, pair_expert * slots + slot_rank, -1)
    return target.reshape(tokens, 2)


def dense(a, b, dims, dtype=BF16):
    return lax.dot_general(a, b, (dims, ((), ())), preferred_element_type=F32).astype(dtype)


def on_device(
    images,
    cotangent,
    key_mask,
    routes,
    fill_order,
    norm_gain1,
    qkv_weight1,
    proj_weight1,
    norm_gain2,
    fc_in,
    fc_out,
    norm_gain3,
    qkv_weight2,
    proj_weight2,
    norm_gain4,
    router,
    expert_in,
    expert_out,
):
    seq = lax.axis_size("seq")
    wide = lax.axis_size("wide")
    place = lax.axis_index("seq")
    tokens, width = images.shape[1:]
    rows = round_up(tokens, ROW_TILE)
    pad = rows - tokens
    total = seq * rows
    experts = wide // 2
    capacity = (5 * tokens + 2 * experts - 1) // (2 * experts)
    slots = round_up(capacity, ROW_TILE)
    span = width // seq
    heads = span // HEAD_DIM
    group = round_up(span, LANES)
    shard = width // wide
    units = fc_in.shape[1]
    unit_cut = units // (seq * wide)

    valid = jnp.pad(key_mask[0].reshape(seq, tokens) > 0, ((0, 0), (0, pad)))
    bias = jnp.where(valid, 0.0, -1e30).astype(F32)
    bias_row = bias.reshape(1, total)
    bias_col = bias.reshape(seq, rows, 1)
    target = jnp.pad(
        slot_targets(routes[0], fill_order[0], experts, capacity, slots),
        ((0, pad), (0, 0)),
        constant_values=-1,
    )
    routes_rows = jnp.pad(routes[0], ((0, pad), (0, 0)))
    cot = jnp.pad(cotangent[0], ((0, pad), (0, 0)))
    start = jnp.pad(images[0].astype(F32), ((0, pad), (0, 0)))

    tidy = shard % ROW_TILE == 0 and fc_out.shape[0] % LANES == 0 and experts == seq
    small = jnp.concatenate(
        [jnp.stack([norm_gain1, norm_gain2, norm_gain3, norm_gain4]), router.T], axis=0
    )
    if tidy:
        small = jnp.pad(small, ((0, ROW_TILE - small.shape[0]), (0, LANES - shard)))
        normed_one, gains, router_all, own_two, own_fc, wqkv_one, wproj_one = begin(
            start, small, qkv_weight1, proj_weight1, qkv_weight2, fc_in, tokens, span, group, 1
        )
        wqkv_one = wqkv_one.reshape(width, 3 * group)
    else:

        def gathered(x):
            return lax.all_gather(x, "wide", axis=0, tiled=True)

        def own_qkv(w):
            own = lax.dynamic_index_in_dim(w.reshape(shard, 3, seq, span), place, 2, keepdims=False)
            own = jnp.pad(own, ((0, 0), (0, 0), (0, group - span)))
            return gathered(own.reshape(shard, 3 * group))

        def own_proj(w):
            own = lax.dynamic_slice_in_dim(gathered(w), place * span, span, 0)
            return own.reshape(2, span // 2, width)

        small = lax.all_gather(small, "wide", axis=0)
        small = small.transpose(1, 0, 2).reshape(4 + experts, width)
        gains = small[:4].astype(F32)
        router_all = jnp.pad(small[4:], ((0, LANES - experts), (0, 0)))
        wqkv_one = own_qkv(qkv_weight1)
        wproj_one = own_proj(proj_weight1)
        w_in = gathered(
            lax.dynamic_index_in_dim(
                fc_in.reshape(shard, wide, seq, unit_cut), place, 2, keepdims=False
            ).reshape(shard, wide * unit_cut)
        )
        w_out = gathered(lax.dynamic_slice_in_dim(fc_out, place * unit_cut, unit_cut, 0))
        wqkv_two = own_qkv(qkv_weight2)
        wproj_two = own_proj(proj_weight2)
        normed_one = spread_norm(start, gains, tokens, 1)

    tasks = [spread_task(own_fc)] if tidy else []
    qkv_one, lse_one, mixed_one, part, *came = attend_forward(
        normed_one, wqkv_one, wproj_one, bias_row, heads, 2 if tidy else None, tasks
    )
    if tidy:
        w_in = came[0].reshape(width, wide * unit_cut)
        cut = LANES // seq
        tasks = [
            spread_task(
                fc_out.reshape(-1, LANES, width),
                lambda ref: ref.at[:, pl.ds(lax.axis_index("seq") * cut, cut)],
                (fc_out.shape[0] // LANES, cut, width),
            )
        ]
    first, normed_two, *came = join_forward(part, start, gains, 1, tokens, 3, tasks)
    if tidy:
        w_out = came[0].reshape(-1, width)
    flat_two = normed_two.reshape(total, width)
    pre = dense(flat_two, w_in, ((1,), (0,)), F32)
    hidden, slope = gelu_parts(pre)
    hidden, slope = hidden.astype(BF16), slope.astype(BF16)
    part = dense(hidden, w_out, ((1,), (0,))).reshape(seq, rows, width)
    tasks = [spread_task(own_two), root_spread_task(proj_weight2)] if tidy else []
    second, normed_three, *came = join_forward(part, first, gains, 2, tokens, 4, tasks)
    if tidy:
        wqkv_two = came[0].reshape(width, 3 * group)
        wproj_two = came[1]
    qkv_two, lse_two, mixed_two, part = attend_forward(
        normed_three, wqkv_two, wproj_two, bias_row, heads
    )
    third, routed, probs, gates, got_rows, got_grads = dispatch(
        part, second, gains, router_all, routes_rows, cot, target.T, tokens, slots, 5
    )
    got_rows = got_rows.reshape(wide * slots, width)
    got_grads = got_grads.reshape(wide * slots, width)
    pre = dense(got_rows, expert_in[0], ((1,), (0,)), F32)
    e_hidden, e_slope = gelu_parts(pre)
    e_hidden = e_hidden.astype(BF16)
    e_part = dense(e_hidden, expert_out[0], ((1,), (0,)))
    e_pre = (dense(got_grads, expert_out[0], ((1,), (1,)), F32) * e_slope).astype(BF16)
    e_rows = dense(e_pre, expert_in[0], ((1,), (1,)))
    output, grad, gain4_grad, router_grad, branch = combine(
        e_part.reshape(wide, slots, width),
        e_rows.reshape(wide, slots, width),
        third,
        routed,
        probs,
        gates,
        gains,
        router_all,
        routes_rows,
        cot,
        target,
        tokens,
        6,
    )
    e_out_grad = dense(e_hidden, got_grads, ((0,), (0,)))
    e_in_grad = dense(got_rows, e_pre, ((0,), (0,)))

    def qkv_terms(normed, grad_qkv):
        return dense(normed.reshape(total, width), grad_qkv.reshape(total, 3 * group), ((0,), (0,)))

    def proj_terms(mixed, branch):
        return dense(mixed.reshape(total, group), branch.reshape(total, width), ((0,), (0,)))[:span]

    def reduced(terms):
        own = lax.psum_scatter(terms, "wide", scatter_dimension=0, tiled=True)
        return lax.all_gather(own, "seq", axis=0).astype(F32)

    def attention_grads(gq, gp):
        gq = gq.reshape(width, 3, group)[:, :, :span].reshape(width, 3 * span)
        gp = lax.all_to_all(gp, "seq", split_axis=1, concat_axis=0, tiled=True)
        whole = reduced(jnp.concatenate([gq, gp], axis=1))
        gq = whole[:, :, : 3 * span].reshape(seq, shard, 3, span).transpose(1, 2, 0, 3)
        gp = whole[:, :, 3 * span :].transpose(1, 0, 2)
        return gq.reshape(shard, 3 * width), gp.reshape(shard, width)

    grad_qkv, part = attend_backward(
        branch, qkv_two, lse_two, mixed_two, wqkv_two, wproj_two, bias_col, heads
    )
    qkv_two_terms = qkv_terms(normed_three, grad_qkv)
    proj_two_terms = proj_terms(mixed_two, branch)
    tasks = []
    if tidy:
        tasks = [
            reduce_task(qkv_two_terms.reshape(wide, shard, 3 * group)),
            root_reduce_task(proj_two_terms.reshape(2, shard, width)),
        ]
    grad, gain3_grad, branch, *came = join_backward(
        part, second, gains, 2, grad, tokens, 7, tasks
    )
    if tidy:
        qkv_two_own, proj_two_own = came
    branch_flat = branch.reshape(total, width)
    pre_grad = (dense(branch_flat, w_out, ((1,), (1,)), F32) * slope).astype(BF16)
    part = dense(pre_grad, w_in, ((1,), (1,))).reshape(seq, rows, width)
    fc_in_terms = dense(flat_two, pre_grad, ((0,), (0,)))
    fc_out_terms = dense(hidden, branch_flat, ((0,), (0,)))
    tasks = [reduce_task(fc_in_terms.reshape(wide, shard, -1))] if tidy else []
    grad, gain2_grad, branch, *came = join_backward(
        part, first, gains, 1, grad, tokens, 8, tasks
    )
    tasks = []
    if tidy:
        tasks = [
            reduce_task(fc_out_terms.reshape(wide, -1, width)),
            block_gather_task(came[0]),
            block_gather_task(qkv_two_own),
        ]
    grad_qkv, part, *came = attend_backward(
        branch,
        qkv_one,
        lse_one,
        mixed_one,
        wqkv_one,
        wproj_one,
        bias_col,
        heads,
        9 if tidy else None,
        tasks,
    )
    qkv_one_terms = qkv_terms(normed_one, grad_qkv)
    proj_one_terms = proj_terms(mixed_one, branch)
    others = [gain2_grad, gain3_grad, gain4_grad, router_grad[:experts]]
    if tidy:
        image_grad, small_own, qkv_one_all, fc_out_all, proj_one_own = close(
            part,
            start,
            gains,
            grad,
            jnp.concatenate(others, axis=0),
            qkv_one_terms.reshape(wide, shard, 3 * group),
            proj_one_terms.reshape(2, shard, width),
            came[0],
            tokens,
            10,
        )
        small_own = small_own[:, :shard]
        qkv1_grad, qkv2_grad, fc_in_grad, fc_out_grad, proj1_grad, proj2_grad = assemble(
            qkv_one_all, came[2], came[1], fc_out_all, proj_one_own, proj_two_own, span, group
        )
    else:
        image_grad, gain1_grad = close_plain(part, start, gains, grad, tokens, 10)
        qkv1_grad, proj1_grad = attention_grads(qkv_one_terms, proj_one_terms)
        qkv2_grad, proj2_grad = attention_grads(qkv_two_terms, proj_two_terms)
        fc_whole = reduced(jnp.concatenate([fc_in_terms, fc_out_terms], axis=1))
        fc_in_grad = fc_whole[:, :, : wide * unit_cut].reshape(seq, shard, wide, unit_cut)
        fc_in_grad = fc_in_grad.transpose(1, 2, 0, 3).reshape(shard, units)
        fc_out_grad = fc_whole[:, :, wide * unit_cut :].reshape(seq * unit_cut, width)
        small_own = lax.psum(jnp.concatenate([gain1_grad] + others, axis=0), ("seq", "wide"))
        small_own = lax.dynamic_slice_in_dim(
            small_own, lax.axis_index("wide") * shard, shard, 1
        )
    e_in_all = lax.psum(e_in_grad, "seq").astype(F32)
    e_out_all = lax.psum(e_out_grad, "seq").astype(F32)
    return (
        output[None],
        image_grad[None],
        small_own[0],
        qkv1_grad,
        proj1_grad,
        small_own[1],
        fc_in_grad,
        fc_out_grad,
        small_own[2],
        qkv2_grad,
        proj2_grad,
        small_own[3],
        small_own[4 : 4 + experts].T,
        e_in_all[None],
        e_out_all[None],
    )


def solution(mesh):
    placed = (
        P("wide", "seq", None),
        P("wide", "seq", None),
        P("wide", None),
        P("wide", "seq", None),
        P("wide", "seq"),
        P("wide"),
        P("wide", None),
        P("wide", None),
        P("wide"),
        P("wide", None),
        P("wide", None),
        P("wide"),
        P("wide", None),
        P("wide", None),
        P("wide"),
        P("wide", None),
        P("wide", None, None),
        P("wide", None, None),
    )
    return jax.shard_map(
        on_device,
        mesh=mesh,
        in_specs=placed,
        out_specs=(
            P("wide", "seq", None),
            P("wide", "seq", None),
            P("wide"),
            P("wide", None),
            P("wide", None),
            P("wide"),
            P("wide", None),
            P("wide", None),
            P("wide"),
            P("wide", None),
            P("wide", None),
            P("wide"),
            P("wide", None),
            P("wide", None, None),
            P("wide", None, None),
        ),
        check_vma=False,
    )
```

time: 875 us -> 624 us (0.71)
  waiting for transfers between devices: 238 us -> 0.02 us
  Pallas kernels: 379 us -> 503 us
  blocking collectives: 85.9 us -> 0 us
  local copies, waits for them, and re-layouts: 65.6 us -> 14.5 us
    reduce_scatter x3 -> x0, waiting for transfers between devices: 121 us -> none  [reduced(): own = lax.psum_scatter(terms, 'wide', scatter_dimension=0, tiled=True)]
    pallas_call x10 -> x11, Pallas kernels: 221 us -> 332 us  [call(): pl.pallas_call(kernel, out_shape=tuple((shape for shape, _ in all_outs)),...]
    all_gather x7 -> x0, waiting for transfers between devices: 107 us -> none  [the longest x6 107 us: gathered(): return lax.all_gather(x, 'wide', axis=0, tiled=True)]
    all_gather x3 -> x0, blocking collectives: 43.7 us -> none  [the longest x1 28.3 us: on_device(): small = lax.all_gather(small, 'wide', axis=0)]
    psum x1 -> x0, blocking collectives: 42.1 us -> none  [on_device(): small_grads = lax.psum(small_grads, ('seq', 'wide'))]
    reshape x10 -> x0, local copies, waits for them, and re-layouts: 18 us -> none  [the longest x4 5.27 us: attention_grads(): return (gq.reshape(shard, 3 * width), gp.reshape(shard, width))]
    pallas_call x1, Pallas kernels: 82.2 us -> 93.6 us  [combine(): pl.pallas_call(kernel, out_shape=(jax.ShapeDtypeStruct((tokens, width), F...]
  transfers between devices with their start and end apart: 13 -> 1, of which waited for: 9 -> 0; matrix products, arithmetic and copies ran while one was open for 11% -> 8% of each run, Pallas kernels for 18% -> 46%
where the time goes in v2:
time: 624 us; the launch traced here: 614 us
  Pallas kernels  503 us (81%)
  matrix products  69.1 us (11%)
  between operations  15 us (2%)
  local copies, waits for them, and re-layouts  14.5 us (2%)
  other arithmetic  11.9 us (2%)
    pallas_call x11, Pallas kernels, call(): pl.pallas_call(kernel, out_shape=tuple((shape for shape, _ in all_outs)),...  332 us
    pallas_call x1, Pallas kernels, combine(): pl.pallas_call(kernel, out_shape=(jax.ShapeDtypeStruct((tokens, width), F...  93.6 us
    pallas_call x1, Pallas kernels, dispatch(): pl.pallas_call(kernel, out_shape=(jax.ShapeDtypeStruct((rows, width), F32...  77.8 us
    dot_general x16, matrix products, dense(): lax.dot_general(a, b, (dims, ((), ())), preferred_element_type=F32)  69.1 us
  transfers between devices with their start and end apart: 1, of which 0 were waited for; matrix products, arithmetic and copies ran while one was open for 8% of the time, Pallas kernels for 46%

profile of v2, /device:TPU:0, one launch (start us, length us, event | category | flops | bytes accessed | tf_op | source)
XLA Modules:
  0.0 613.6 jit_solution(16670052129155298404)
XLA Ops:
  7.2 0.0 copy-start
  7.3 0.0 all-reduce.9.cloned.1.call-start
  7.3 2.1 pad_convert_fusion.refs_0_.refs_1_
  9.4 0.7 compare_reduce_fusion
  10.1 0.1 gt.11
  10.2 0.7 reshape.144.refs_3_
  10.9 0.8 copy.44
  11.7 0.1 eq.15
  11.9 0.7 reduce.1
  12.6 0.1 broadcast_add_fusion
  12.7 0.1 add.68
  12.8 0.4 convert_reduce_fusion
  13.2 0.1 reduce_sum.12
  13.4 0.7 fusion.19
  14.1 0.7 copy.46.target_ref
  14.8 0.7 pad.29.routes_ref
  15.5 0.6 pad.27.refs_1_
  16.1 0.8 pad.30.cot_ref
  16.9 31.4 %shard_map.289 = (bf16[4,272,768]{2,1,0:T(8,128)(2,1)}, f32[16,768]{1,0:T(8,128)}, bf16[128,768]{1,0:T(8,128)(2,1)}, bf16[96,768]{1,0:T(8,128)(2,1)}, bf16[96,76...) custom-call(f32[272,768]{1,0:T(8,128)} %pad_convert_fusion.refs_0_.refs_1_, ...), custom_call_target="tpu_custom_call" | custom-call | tf_op jit(solution)/shard_map/pallas_call | solution.py:481
  48.3 35.0 %shard_map.290 = (bf16[4,272,768]{2,1,0:T(8,128)(2,1)}, f32[4,272,128]{2,1,0:T(8,128)}, bf16[4,272,256]{2,1,0:T(8,128)(2,1)}, bf16[4,272,768]{2,1,0:T(8,128)(2,1)}, bf16[8,96,768]{2,1,0:T(8,128)(2,1)}) custom-call(bf16[4,272,768]{2,1,0:T(8,128)(2,1)} %get-tuple-element.76.refs_0_, bf16[768,768]{1,0:T(8,128)(2,1)} %bitcast.98, ...), custom_call_target="tpu_custom_call" | custom-call | tf_op jit(solution)/shard_map/pallas_call | solution.py:481
  83.4 32.8 %shard_map.291 = (f32[272,768]{1,0:T(8,128)}, bf16[4,272,768]{2,1,0:T(8,128)(2,1)}, bf16[8,3,32,768]{3,2,1,0:T(8,128)(2,1)}) custom-call(bf16[4,272,768]{2,1,0:T(8,128)(2,1)} %get-tuple-element.80.refs_0_, f32[272,768]{1,0:T(8,128)} %pad_convert_fusion.refs_0_.refs_1_, f32[16,768]{1,0:T(8,128)} %get-tuple-element.81.refs_2_.gain_ref, ...), custom_call_target="tpu_custom_call" | custom-call | tf_op jit(solution)/shard_map/pallas_call | solution.py:481
  116.2 4.9 multiply_convert_fusion.1
  121.1 2.7 convolution_convert_fusion.5
  123.8 32.7 %shard_map.292 = (f32[272,768]{1,0:T(8,128)}, bf16[4,272,768]{2,1,0:T(8,128)(2,1)}, bf16[8,96,768]{2,1,0:T(8,128)(2,1)}, bf16[2,96,768]{2,1,0:T(8,128)(2,1)}) custom-call(bf16[4,272,768]{2,1,0:T(8,128)(2,1)} %bitcast.104, f32[272,768]{1,0:T(8,128)} %get-tuple-element.85.refs_1_, f32[16,768]{1,0:T(8,128)} %get-tuple-element.81.refs_2_.gain_ref, ...), custom_call_target="tpu_custom_call" | custom-call | tf_op jit(solution)/shard_map/pallas_call | solution.py:481
  156.5 13.8 %shard_map.293 = (bf16[4,272,768]{2,1,0:T(8,128)(2,1)}, f32[4,272,128]{2,1,0:T(8,128)}, bf16[4,272,256]{2,1,0:T(8,128)(2,1)}, bf16[4,272,768]{2,1,0:T(8,128)(2,1)}) custom-call(bf16[4,272,768]{2,1,0:T(8,128)(2,1)} %get-tuple-element.87.refs_0_, bf16[768,768]{1,0:T(8,128)(2,1)} %bitcast.96, bf16[2,96,768]{2,1,0:T(8,128)(2,1)} %get-tuple-element.89.refs_2_.refs_5_, ...), custom_call_target="tpu_custom_call" | custom-call | tf_op jit(solution)/shard_map/pallas_call | solution.py:481
  170.3 77.8 %shard_map.294 = (f32[272,768]{1,0:T(8,128)}, bf16[272,768]{1,0:T(8,128)(2,1)}, f32[272,128]{1,0:T(8,128)}, f32[272,128]{1,0:T(8,128)}, bf16[8,176,768]{2,1,0:T(8,128)(2,1)}, /*index=5*/bf16[8,176,768]{2,1,0:T(8,128)(2,1)}) custom-call(bf16[4,272,768]{2,1,0:T(8,128)(2,1)} %get-tuple-element.90.partial_ref, ...), custom_call_target="tpu_custom_call" | custom-call | tf_op jit(solution)/shard_map/pallas_call | solution.py:1267
  248.1 0.0 copy-start.18
  248.1 5.6 multiply_convert_fusion
  253.7 0.0 copy-start.29
  253.8 5.9 fusion.4
  259.7 0.0 copy-start.28
  259.7 5.2 fusion.11
  265.0 5.2 fusion.12
  270.2 0.0 all-reduce.9.cloned.1.call-update
  270.2 0.0 copy-start.19
  270.2 0.0 copy-start.30
  270.2 7.3 %convolution_convert_fusion.2 = bf16[1408,768]{1,0:T(8,128)(2,1)} fusion(bf16[1408,1536]{1,0:T(8,128)(2,1)} %copy-done.28, bf16[1,768,1536]{2,1,0:T(8,128)(2,1)S(1)} %copy-done), kind=kOutput, calls=%fused_computation.14 | convolution fusion | flops 3322970112 | bytes 8847360 | tf_op jit(solution)/shard_map/dot_general | solution.py:1444
  277.5 5.1 convolution_convert_fusion.3
  282.6 93.6 %shard_map.295 = (f32[257,768]{1,0:T(8,128)}, f32[272,768]{1,0:T(8,128)}, f32[1,768]{1,0:T(1,128)}, f32[128,768]{1,0:T(8,128)}, bf16[4,272,768]{2,1,0:T(8,128)(2,1)}) custom-call(bf16[8,176,768]{2,1,0:T(8,128)(2,1)} %bitcast.101, bf16[8,176,768]{2,1,0:T(8,128)(2,1)} %bitcast.100, f32[272,768]{1,0:T(8,128)} %get-tuple-element.95.third_ref, ...), custom_call_target="tpu_custom_call" | custom-call | tf_op jit(solution)/shard_map/pallas_call | solution.py:1402
  376.2 2.2 convolution_bitcast_fusion.1
  378.4 0.7 slice.48
  379.1 1.1 copy.47.refs_6_
  380.2 21.6 %shard_map.296 = (bf16[4,272,768]{2,1,0:T(8,128)(2,1)}, bf16[4,272,768]{2,1,0:T(8,128)(2,1)}) custom-call(bf16[4,272,768]{2,1,0:T(8,128)(2,1)} %get-tuple-element.100.refs_0_, bf16[4,272,768]{2,1,0:T(8,128)(2,1)} %get-tuple-element.101.refs_1_, f32[4,272,128]{2,1,0:T(8,128)} %get-tuple-element.102.refs_2_, bf16[4,272,256]{2,1,0:T(8,128)(2,1)} %get-tuple-element.103.refs_3_, ...), custom_call_target="tpu_custom_call" | custom-call | tf_op jit(solution)/shard_map/pallas_call | solution.py:481
  401.8 4.2 bitcast_convert_fusion.1
  406.0 45.8 %shard_map.297 = (f32[272,768]{1,0:T(8,128)}, f32[1,768]{1,0:T(1,128)}, bf16[4,272,768]{2,1,0:T(8,128)(2,1)}, bf16[96,768]{1,0:T(8,128)(2,1)}, bf16[96,768]{1,0:T(8,128)(2,1)}) custom-call(bf16[4,272,768]{2,1,0:T(8,128)(2,1)} %get-tuple-element.104.refs_0_, f32[272,768]{1,0:T(8,128)} %get-tuple-element.91.residual_ref.refs_1_, ...), custom_call_target="tpu_custom_call" | custom-call | tf_op jit(solution)/shard_map/pallas_call | solution.py:481
  451.9 4.7 fusion.5
  456.6 2.7 convolution_convert_fusion.4
  459.3 2.8 convolution_convert_fusion.7
  462.1 31.6 %shard_map.298 = (f32[272,768]{1,0:T(8,128)}, f32[1,768]{1,0:T(1,128)}, bf16[4,272,768]{2,1,0:T(8,128)(2,1)}, bf16[96,768]{1,0:T(8,128)(2,1)}) custom-call(bf16[4,272,768]{2,1,0:T(8,128)(2,1)} %bitcast.103, f32[272,768]{1,0:T(8,128)} %get-tuple-element.85.refs_1_, f32[16,768]{1,0:T(8,128)} %get-tuple-element.81.refs_2_.gain_ref, ...), custom_call_target="tpu_custom_call" | custom-call | tf_op jit(solution)/shard_map/pallas_call | solution.py:481
  493.7 2.3 convolution_bitcast_fusion
  495.9 0.7 slice.47
  496.7 0.7 slice.31
  497.4 4.2 convolution_convert_fusion.6
  501.7 34.7 %shard_map.299 = (bf16[4,272,768]{2,1,0:T(8,128)(2,1)}, bf16[4,272,768]{2,1,0:T(8,128)(2,1)}, bf16[96,768]{1,0:T(8,128)(2,1)}, bf16[4,96,768]{2,1,0:T(8,128)(2,1)}, bf16[4,96,768]{2,1,0:T(8,128)(2,1)}) custom-call(bf16[4,272,768]{2,1,0:T(8,128)(2,1)} %get-tuple-element.109.refs_0_, bf16[4,272,768]{2,1,0:T(8,128)(2,1)} %get-tuple-element.110.refs_1_, ...), custom_call_target="tpu_custom_call" | custom-call | tf_op jit(solution)/shard_map/pallas_call | solution.py:481
  536.4 0.6 pad_maximum_fusion.refs_4_
  537.0 4.2 bitcast_convert_fusion
  541.2 48.2 %shard_map.300 = (f32[257,768]{1,0:T(8,128)}, f32[16,128]{1,0:T(8,128)}, bf16[4,96,768]{2,1,0:T(8,128)(2,1)}, bf16[4,96,768]{2,1,0:T(8,128)(2,1)}, bf16[96,768]{1,0:T(8,128)(2,1)}) custom-call(bf16[4,272,768]{2,1,0:T(8,128)(2,1)} %get-tuple-element.115.refs_0_, f32[272,768]{1,0:T(8,128)} %pad_convert_fusion.refs_0_.refs_1_, ...), custom_call_target="tpu_custom_call" | custom-call | tf_op jit(solution)/shard_map/pallas_call | solution.py:481
  589.4 2.8 copy.50
  592.2 1.7 copy.49
  593.9 4.1 shard_map.301
  598.0 0.5 slice_bitcast_fusion.1
  598.5 0.6 slice_bitcast_fusion
  599.1 4.6 broadcast_in_dim.37
  603.7 2.5 broadcast_in_dim.39
  (61 shorter events, 0.2 us)
Async XLA Ops:
  7.2 240.9 %copy-start = (bf16[1,768,1536]{2,1,0:T(8,128)(2,1)S(1)}, bf16[1,768,1536]{2,1,0:T(8,128)(2,1)}, u32[]{:S(2)}) copy-start(bf16[1,768,1536]{2,1,0:T(8,128)(2,1)} %param.34) | copy-start | bytes 7077892
  7.2 8.3 %copy-start.14 = (bf16[96]{0:T(256)(128)(2,1)S(1)}, bf16[96]{0:T(256)(128)(2,1)}, u32[]{:S(2)}) copy-start(bf16[96]{0:T(256)(128)(2,1)} %param.23) | copy-start | bytes 580
  7.2 8.2 %copy-start.15 = (bf16[96]{0:T(256)(128)(2,1)S(1)}, bf16[96]{0:T(256)(128)(2,1)}, u32[]{:S(2)}) copy-start(bf16[96]{0:T(256)(128)(2,1)} %param.26) | copy-start | bytes 580
  7.2 8.2 %copy-start.16 = (bf16[96]{0:T(256)(128)(2,1)S(1)}, bf16[96]{0:T(256)(128)(2,1)}, u32[]{:S(2)}) copy-start(bf16[96]{0:T(256)(128)(2,1)} %param.29) | copy-start | bytes 580
  7.2 8.2 %copy-start.17 = (bf16[96]{0:T(256)(128)(2,1)S(1)}, bf16[96]{0:T(256)(128)(2,1)}, u32[]{:S(2)}) copy-start(bf16[96]{0:T(256)(128)(2,1)} %param.32) | copy-start | bytes 580
  7.2 8.2 %copy-start.13 = (bf16[96,4]{0,1:T(4,128)(2,1)S(1)}, bf16[96,4]{0,1:T(4,128)(2,1)}, u32[]{:S(2)}) copy-start(bf16[96,4]{0,1:T(4,128)(2,1)} %param.33) | copy-start | bytes 2308
  7.2 8.9 %copy-start.8 = (bf16[1,257,768]{2,1,0:T(8,128)(2,1)S(1)}, bf16[1,257,768]{2,1,0:T(8,128)(2,1)}, u32[]{:S(2)}) copy-start(bf16[1,257,768]{2,1,0:T(8,128)(2,1)} %param.19) | copy-start | bytes 1184260
  7.3 591.8 %all-reduce.9.cloned.1.call-start = ((), (), s32[]{:S(2)}) async-start(), calls=%async_computation | async-start | bytes 9437184 | tf_op jit(solution)/shard_map/psum | solution.py:1690
  83.3 32.8 %copy-start.24 = (bf16[8,96,768]{2,1,0:T(8,128)(2,1)S(1)}, bf16[8,96,768]{2,1,0:T(8,128)(2,1)}, u32[]{:S(2)}) copy-start(bf16[8,96,768]{2,1,0:T(8,128)(2,1)} %get-tuple-element.83) | copy-start | bytes 3538948
  116.2 5.0 copy-start.25
  121.1 2.7 copy-start.27
  248.1 5.6 copy-start.18
  248.1 5.6 copy-start.20
  253.7 11.2 %copy-start.29 = (bf16[1408,1536]{1,0:T(8,128)(2,1)}, bf16[1408,1536]{1,0:T(8,128)(2,1)S(1)}, u32[]{:S(2)}) copy-start(bf16[1408,1536]{1,0:T(8,128)(2,1)S(1)} %get-tuple-element.194) | copy-start | bytes 12976132
  253.8 6.0 copy-start.21
  259.7 5.2 copy-start.28
  270.2 7.3 %copy-start.19 = (bf16[1,1536,768]{2,1,0:T(8,128)(2,1)S(1)}, bf16[1,1536,768]{2,1,0:T(8,128)(2,1)}, u32[]{:S(2)}) copy-start(bf16[1,1536,768]{2,1,0:T(8,128)(2,1)} %param.35) | copy-start | bytes 7077892
  270.2 7.3 %copy-start.30 = (bf16[1408,1536]{1,0:T(8,128)(2,1)S(1)}, bf16[1408,1536]{1,0:T(8,128)(2,1)}, u32[]{:S(2)}) copy-start(bf16[1408,1536]{1,0:T(8,128)(2,1)} %copy-done.29) | copy-start | bytes 12976132
  282.6 93.6 %copy-start.3 = (bf16[4,272,256]{2,1,0:T(8,128)(2,1)S(1)}, bf16[4,272,256]{2,1,0:T(8,128)(2,1)}, u32[]{:S(2)}) copy-start(bf16[4,272,256]{2,1,0:T(8,128)(2,1)} %get-tuple-element.103.refs_3_) | copy-start | bytes 1671172
  380.2 21.7 %copy-start.6 = (bf16[4,272,768]{2,1,0:T(8,128)(2,1)S(1)}, bf16[4,272,768]{2,1,0:T(8,128)(2,1)}, u32[]{:S(2)}) copy-start(bf16[4,272,768]{2,1,0:T(8,128)(2,1)} %get-tuple-element.87.refs_0_) | copy-start | bytes 5013508
  406.0 45.8 %copy-start.26 = (bf16[8,3,32,768]{3,2,1,0:T(8,128)(2,1)S(1)}, bf16[8,3,32,768]{3,2,1,0:T(8,128)(2,1)}, u32[]{:S(2)}) copy-start(bf16[8,3,32,768]{3,2,1,0:T(8,128)(2,1)} %get-tuple-element.84) | copy-start | bytes 3538948
  456.6 2.7 copy-start.22
  462.1 31.6 %copy-start.4 = (bf16[4,272,256]{2,1,0:T(8,128)(2,1)S(1)}, bf16[4,272,256]{2,1,0:T(8,128)(2,1)}, u32[]{:S(2)}) copy-start(bf16[4,272,256]{2,1,0:T(8,128)(2,1)} %get-tuple-element.112.refs_3_) | copy-start | bytes 1671172
  493.6 3.8 copy-start.23
  501.6 34.7 %copy-start.9 = (f32[1,768]{1,0:T(1,128)S(1)}, f32[1,768]{1,0:T(1,128)}, u32[]{:S(2)}) copy-start(f32[1,768]{1,0:T(1,128)} %get-tuple-element.119) | copy-start | bytes 9220
  501.6 34.7 %copy-start.10 = (f32[1,768]{1,0:T(1,128)S(1)}, f32[1,768]{1,0:T(1,128)}, u32[]{:S(2)}) copy-start(f32[1,768]{1,0:T(1,128)} %get-tuple-element.118) | copy-start | bytes 9220
  501.6 34.7 %copy-start.11 = (f32[1,768]{1,0:T(1,128)S(1)}, f32[1,768]{1,0:T(1,128)}, u32[]{:S(2)}) copy-start(f32[1,768]{1,0:T(1,128)} %get-tuple-element.117) | copy-start | bytes 9220
  501.6 35.3 %copy-start.5 = (bf16[4,272,768]{2,1,0:T(8,128)(2,1)S(1)}, bf16[4,272,768]{2,1,0:T(8,128)(2,1)}, u32[]{:S(2)}) copy-start(bf16[4,272,768]{2,1,0:T(8,128)(2,1)} %get-tuple-element.76.refs_0_) | copy-start | bytes 5013508
  541.2 51.0 %copy-start.7 = (f32[257,768]{1,0:T(8,128)S(1)}, f32[257,768]{1,0:T(8,128)}, u32[]{:S(2)}) copy-start(f32[257,768]{1,0:T(8,128)} %get-tuple-element.99) | copy-start | bytes 2368516
  592.2 5.8 copy-start.12
  599.1 4.7 copy-start.2
  603.7 2.6 copy-start.1
Sparse Core Ops, SparseCore 0:
  270.3 111.3 all-reduce.8
